TPU v7x, 8 devices: a whole 2x2x1 slice. The times are simulated.
8 devices in a mesh: data: 1 (over z), sp: 8 (over y, x, core).
Axes of the slice: x: 2, y: 2, z: 1, core: 2. Of those that a mesh axis runs over, the one named last changes fastest.
Arguments:
- latents: bfloat16 [16, 64, 32, 384], P('data', 'sp')
- cotangent: bfloat16 [16, 64, 32, 384], P('data', 'sp')
- ln_params: bfloat16 [2, 4, 384], replicated
- w_qkv: bfloat16 [2, 384, 1152], replicated
- w_out: bfloat16 [2, 6, 64, 384], replicated
- w_up: bfloat16 [2, 384, 1536], replicated
- w_down: bfloat16 [2, 1536, 384], replicated
Outputs:
- output 1: bfloat16 [16, 64, 32, 384], P('data', 'sp')
- output 2: bfloat16 [16, 64, 32, 384], P('data', 'sp')
- output 3: float32 [2, 4, 384], P('data')
- output 4: float32 [2, 384, 1152], P('data')
- output 5: float32 [2, 6, 64, 384], P('data')
- output 6: float32 [2, 384, 1536], P('data')
- output 7: float32 [2, 1536, 384], P('data')
All inputs are finite; a program needn't handle non-finite values.
Results may differ from a plain program's by a relative error of at most 0.02.
Values are sent between devices in bfloat16 or wider.
A program may use at most 1 GiB of HBM per device.

v0:
```python
import jax
import jax.numpy as jnp
from jax import lax
from jax.sharding import PartitionSpec as P

SPATIAL = ('bamhe,banhe->bahmn', 'bahmn,banhe->bamhe', 'bahmn,bamhe->banhe')
TEMPORAL = ('bmche,bnche->bchmn', 'bchmn,bnche->bmche', 'bchmn,bmche->bnche')


def layer_norm(resid32, ln_gain, ln_shift):
    row_mean = jnp.mean(resid32, axis=-1, keepdims=True)
    centered = resid32 - row_mean
    inv_std = lax.rsqrt(jnp.mean(centered * centered, axis=-1, keepdims=True) + 1e-6)
    normed = centered * inv_std
    return (normed * ln_gain + ln_shift).astype(jnp.bfloat16), normed, inv_std


def layer_norm_back(d_ln_out, normed, inv_std, ln_gain):
    d_out32 = d_ln_out.astype(jnp.float32)
    d_gain = jnp.sum(d_out32 * normed, axis=(0, 1, 2))
    d_shift = jnp.sum(d_out32, axis=(0, 1, 2))
    d_norm = d_out32 * ln_gain
    d_center = d_norm - jnp.mean(d_norm, axis=-1, keepdims=True)
    d_resid = inv_std * (d_center - normed * jnp.mean(d_norm * normed, axis=-1, keepdims=True))
    return d_resid, d_gain, d_shift


def gelu_tanh(pre_act):
    return jax.nn.gelu(pre_act, approximate=True)


def qkv_forward(block_in32, ln_f32, w_qkv, num_heads):
    model_width = w_qkv.shape[0]
    a_in, normed, inv_std = layer_norm(block_in32, ln_f32[0], ln_f32[1])
    w_heads = w_qkv.reshape(model_width, 3, num_heads, model_width // num_heads)
    qkv_heads = jnp.einsum('bacd,dkhe->kbache', a_in, w_heads, preferred_element_type=jnp.float32)
    return qkv_heads.astype(jnp.bfloat16), (a_in, normed, inv_std)


def attend_forward(qkv_heads, attn_forms):
    score_scale = qkv_heads.shape[-1] ** -0.5
    scores = jnp.einsum(attn_forms[0], qkv_heads[0], qkv_heads[1], preferred_element_type=jnp.float32) * score_scale
    attn_probs = jax.nn.softmax(scores, axis=-1).astype(jnp.bfloat16)
    attn_out = jnp.einsum(attn_forms[1], attn_probs, qkv_heads[2], preferred_element_type=jnp.float32)
    return attn_out.astype(jnp.bfloat16), attn_probs


def tail_forward(block_in32, attn_out, ln_f32, w_out, w_up, w_down):
    attn_proj = jnp.einsum('bache,hef->bacf', attn_out, w_out, preferred_element_type=jnp.float32)
    hid32 = (block_in32 + attn_proj).astype(jnp.bfloat16).astype(jnp.float32)
    m_in, normed, inv_std = layer_norm(hid32, ln_f32[2], ln_f32[3])
    up_proj = jnp.dot(m_in, w_up, preferred_element_type=jnp.float32)
    act_out = gelu_tanh(up_proj).astype(jnp.bfloat16)
    block_out = (hid32 + jnp.dot(act_out, w_down, preferred_element_type=jnp.float32)).astype(jnp.bfloat16)
    return block_out, (m_in, normed, inv_std, up_proj, act_out)


def tail_backward(d_block_out, attn_out, tail_saved, ln_f32, w_out, w_up, w_down):
    m_in, normed, inv_std, up_proj, act_out = tail_saved
    g_down = jnp.einsum('bacf,bacd->fd', act_out, d_block_out, preferred_element_type=jnp.float32)
    d_act = jnp.einsum('bacd,fd->bacf', d_block_out, w_down, preferred_element_type=jnp.float32).astype(jnp.bfloat16)
    gelu_pull = jax.vjp(gelu_tanh, up_proj)[1]
    d_up = gelu_pull(d_act.astype(jnp.float32))[0].astype(jnp.bfloat16)
    g_up = jnp.einsum('bacd,bacf->df', m_in, d_up, preferred_element_type=jnp.float32)
    d_m_in = jnp.einsum('bacf,df->bacd', d_up, w_up, preferred_element_type=jnp.float32).astype(jnp.bfloat16)
    d_hid32, g_gain, g_shift = layer_norm_back(d_m_in, normed, inv_std, ln_f32[2])
    d_hid = (d_hid32 + d_block_out.astype(jnp.float32)).astype(jnp.bfloat16)
    g_out = jnp.einsum('bache,bacf->hef', attn_out, d_hid, preferred_element_type=jnp.float32)
    d_attn = jnp.einsum('bacf,hef->bache', d_hid, w_out, preferred_element_type=jnp.float32).astype(jnp.bfloat16)
    return d_attn, d_hid, (g_gain, g_shift, g_out, g_up, g_down)


def attend_backward(d_attn, qkv_heads, attn_probs, attn_forms):
    score_scale = qkv_heads.shape[-1] ** -0.5
    d_probs = jnp.einsum(attn_forms[0], d_attn, qkv_heads[2], preferred_element_type=jnp.float32)
    d_probs = d_probs.astype(jnp.bfloat16).astype(jnp.float32)
    probs32 = attn_probs.astype(jnp.float32)
    row_dot = jnp.sum(d_probs * probs32, axis=-1, keepdims=True)
    d_scores = (probs32 * (d_probs - row_dot) * score_scale).astype(jnp.bfloat16)
    d_query = jnp.einsum(attn_forms[1], d_scores, qkv_heads[1], preferred_element_type=jnp.float32).astype(jnp.bfloat16)
    d_key = jnp.einsum(attn_forms[2], d_scores, qkv_heads[0], preferred_element_type=jnp.float32).astype(jnp.bfloat16)
    d_value = jnp.einsum(attn_forms[2], attn_probs, d_attn, preferred_element_type=jnp.float32).astype(jnp.bfloat16)
    return jnp.stack([d_query, d_key, d_value])


def qkv_backward(d_qkv, d_hid, head_saved, ln_f32, w_qkv):
    a_in, normed, inv_std = head_saved
    model_width = w_qkv.shape[0]
    w_heads = w_qkv.reshape(model_width, 3, d_qkv.shape[-2], d_qkv.shape[-1])
    g_qkv = jnp.einsum('bacd,kbache->dkhe', a_in, d_qkv, preferred_element_type=jnp.float32)
    d_a_in = jnp.einsum('kbache,dkhe->bacd', d_qkv, w_heads, preferred_element_type=jnp.float32).astype(jnp.bfloat16)
    d_in32, g_gain, g_shift = layer_norm_back(d_a_in, normed, inv_std, ln_f32[0])
    d_block_in = (d_in32 + d_hid.astype(jnp.float32)).astype(jnp.bfloat16)
    return d_block_in, (g_gain, g_shift, g_qkv.reshape(model_width, 3 * model_width))


def block_forward(block_in, ln_params, w_qkv, w_out, w_up, w_down, attn_forms):
    ln_f32 = ln_params.astype(jnp.float32)
    block_in32 = block_in.astype(jnp.float32)
    qkv_heads, head_saved = qkv_forward(block_in32, ln_f32, w_qkv, w_out.shape[0])
    attn_out, attn_probs = attend_forward(qkv_heads, attn_forms)
    block_out, tail_saved = tail_forward(block_in32, attn_out, ln_f32, w_out, w_up, w_down)
    return block_out, (head_saved, qkv_heads, attn_probs, attn_out, tail_saved)


def block_backward(d_block_out, saved, ln_params, w_qkv, w_out, w_up, w_down, attn_forms):
    head_saved, qkv_heads, attn_probs, attn_out, tail_saved = saved
    ln_f32 = ln_params.astype(jnp.float32)
    d_attn, d_hid, tail_grads = tail_backward(d_block_out, attn_out, tail_saved, ln_f32, w_out, w_up, w_down)
    d_qkv = attend_backward(d_attn, qkv_heads, attn_probs, attn_forms)
    d_block_in, head_grads = qkv_backward(d_qkv, d_hid, head_saved, ln_f32, w_qkv)
    ln_grads = jnp.stack([head_grads[0], head_grads[1], tail_grads[0], tail_grads[1]])
    return d_block_in, (ln_grads, head_grads[2], tail_grads[2], tail_grads[3], tail_grads[4])


def device_step(latents, cotangent, ln_params, w_qkv, w_out, w_up, w_down):
    spatial_w = (ln_params[0], w_qkv[0], w_out[0], w_up[0], w_down[0])
    temporal_w = (ln_params[1], w_qkv[1], w_out[1], w_up[1], w_down[1])
    mid_act, spatial_saved = block_forward(latents, *spatial_w, SPATIAL)
    mid_swap = lax.all_to_all(mid_act, 'sp', 2, 1, tiled=True)
    out_swap, temporal_saved = block_forward(mid_swap, *temporal_w, TEMPORAL)
    result = lax.all_to_all(out_swap, 'sp', 1, 2, tiled=True)
    cot_swap = lax.all_to_all(cotangent, 'sp', 2, 1, tiled=True)
    d_mid_swap, temporal_grads = block_backward(cot_swap, temporal_saved, *temporal_w, TEMPORAL)
    d_mid = lax.all_to_all(d_mid_swap, 'sp', 1, 2, tiled=True)
    latents_grad, spatial_grads = block_backward(d_mid, spatial_saved, *spatial_w, SPATIAL)
    weight_grads = lax.psum([jnp.stack([grad_s, grad_t]) for grad_s, grad_t in zip(spatial_grads, temporal_grads)], 'sp')
    return (result, latents_grad) + tuple(weight_grads)


def solution(mesh):
    act_spec = P('data', 'sp', None, None)
    replicated = P()
    part_spec = P('data')
    return jax.shard_map(device_step, mesh=mesh,
                         in_specs=(act_spec, act_spec, replicated, replicated, replicated, replicated, replicated),
                         out_specs=(act_spec, act_spec, part_spec, part_spec, part_spec, part_spec, part_spec),
                         check_vma=False)
```

profile of v0, /device:TPU:0, one launch (start us, length us, event | category | flops | bytes accessed | tf_op | source)
XLA Modules:
  0.0 913.1 jit_solution(6329701393026333584)
XLA Ops:
  17.3 14.7 %convert_bitcast_fusion.1 = bf16[3,16,8,32,6,64]{5,3,4,0,2,1:T(8,128)(2,1)} fusion(bf16[384,3,6,64,1,1]{0,3,2,1,5,4:T(8,128)(2,1)} %bitcast.359, bf16[16,8,32,384]{3,2,1,0:T(8,128)(2,1)S(1)} %copy-done.2, f32[384]{0:T(512)S(1)} %get-tuple-element.29, f32[384]{0:T(512)S(1)} %get-tuple-element.30, f32[16,8,32]{2,1,0:T(8,128)S(1)} %add_rsqrt_fusion.2, ...), kind=kOutput, calls=%fused_computation.43 | convolution fusion | flops 3638034432 | bytes 13503488 | tf_op jit(solution)/shard_map/bacd,dkhe->kbache/dot_general | solution.py:36
  32.0 12.5 %fusion.121 = f32[16,8,6,32,32]{3,4,2,1,0:T(8,128)} fusion(bf16[3,16,8,32,6,64]{5,3,4,0,2,1:T(8,128)(2,1)} %convert_bitcast_fusion.1), kind=kOutput, calls=%fused_computation.187 | convolution fusion | flops 100663296 | bytes 15728640 | tf_op jit(solution)/shard_map/bamhe,banhe->bahmn/dot_general | solution.py:42
  44.5 17.3 %fusion.221 = (f32[16,8,6,32]{3,2,1,0:T(8,128)}, f32[16,8,6,32,32]{3,4,2,1,0:T(8,128)}) fusion(f32[16,8,6,32,32]{3,4,2,1,0:T(8,128)} %fusion.121), kind=kOutput, calls=%fused_computation.301 | output fusion | flops 3145759 | bytes 6389760 | tf_op jit(solution)/shard_map/sub | solution.py:43
  80.8 16.9 %convert_reduce_fusion.5 = (f32[16,8,32]{2,1,0:T(8,128)S(1)}, bf16[16,8,32,384]{3,2,1,0:T(8,128)(2,1)S(1)}) fusion(bf16[16,8,32,6,64]{4,2,3,1,0:T(8,128)(2,1)} %convert_bitcast_fusion.9, bf16[2,6,64,384]{3,2,1,0:T(8,128)(2,1)} %param.11, bf16[16,8,32,384]{3,2,1,0:T(8,128)(2,1)S(1)} %copy-done.2), kind=kOutput, calls=%fused_computation.87 | convolution fusion | flops 1215819776 | bytes 12894208 | tf_op jit(solution)/shard_map/bache,hef->bacf/dot_general | solution.py:49
  99.3 15.5 %multiply_convert_fusion.1 = (bf16[16,8,32,1536]{3,2,1,0:T(8,128)(2,1)}, f32[16,8,32,1536]{3,2,1,0:T(8,128)}) fusion(bf16[2,384,1536]{2,1,0:T(8,128)(2,1)S(1)} %copy-done.54, bf16[16,8,32,384]{3,2,1,0:T(8,128)(2,1)S(1)} %get-tuple-element.47, f32[384]{0:T(512)S(1)} %get-tuple-element.28, f32[384]{0:T(512)S(1)} %get-tuple-element.27, ...), kind=kOutput, calls=%fused_computation.33 | convolution fusion | flops 4897898496 | bytes 42209280 | tf_op jit(solution)/shard_map/dot_general | solution.py:52
  138.8 30.9 %all-to-all-done = bf16[16,8,32,384]{3,1,0,2:T(8,128)(2,1)S(1)} async-done(((bf16[16,8,32,384]{3,1,0,2:T(8,128)(2,1)}), bf16[16,8,32,384]{3,1,0,2:T(8,128)(2,1)S(1)}, u32[]{:S(2)}, u32[]{:S(2)}) %all-to-all-start) | async-done | bytes 3145760 | tf_op jit(solution)/shard_map/all_to_all | solution.py:120
  184.9 14.9 %convert_bitcast_fusion = bf16[3,16,64,4,6,64]{5,2,4,0,3,1:T(8,128)(2,1)} fusion(bf16[384,3,6,64,1,1]{0,3,2,1,5,4:T(8,128)(2,1)} %bitcast.361, bf16[16,8,8,4,384]{4,1,3,2,0:T(8,128)(2,1)S(1)} %bitcast.344, f32[384]{0:T(512)S(1)} %get-tuple-element.25, f32[384]{0:T(512)S(1)} %get-tuple-element.26, f32[16,8,8,4]{2,3,1,0:T(4,128)} %copy.223, ...), kind=kOutput, calls=%fused_computation.42 | convolution fusion | flops 3638034432 | bytes 13503488 | tf_op jit(solution)/shard_map/bacd,dkhe->kbache/dot_general | solution.py:36
  199.8 12.6 %fusion.125 = f32[16,4,6,64,64]{3,4,2,1,0:T(8,128)} fusion(bf16[3,16,64,4,6,64]{5,2,4,0,3,1:T(8,128)(2,1)} %convert_bitcast_fusion), kind=kOutput, calls=%fused_computation.191 | convolution fusion | flops 201326592 | bytes 18874368 | tf_op jit(solution)/shard_map/bmche,bnche->bchmn/dot_general | solution.py:42
  212.4 17.0 %fusion.222 = (f32[16,4,6,64]{3,2,1,0:T(8,128)}, f32[16,4,6,64,64]{3,4,2,1,0:T(8,128)}) fusion(f32[16,4,6,64,64]{3,4,2,1,0:T(8,128)} %fusion.125), kind=kOutput, calls=%fused_computation.302 | output fusion | flops 6291519 | bytes 12681216 | tf_op jit(solution)/shard_map/sub | solution.py:43
  257.0 17.0 %multiply_convert_fusion = (bf16[16,64,4,1536]{3,1,2,0:T(8,128)(2,1)}, f32[16,64,4,1536]{3,1,2,0:T(8,128)}) fusion(bf16[2,384,1536]{2,1,0:T(8,128)(2,1)} %param.12, bf16[16,64,4,384]{3,1,2,0:T(8,128)(2,1)S(1)} %get-tuple-element.53, f32[384]{0:T(512)S(1)} %get-tuple-element.24, f32[384]{0:T(512)S(1)} %get-tuple-element.23, ...), kind=kOutput, calls=%fused_computation.32 | convolution fusion | flops 4897898496 | bytes 42109952 | tf_op jit(solution)/shard_map/dot_general | solution.py:52
  273.9 24.2 %fusion.6 = bf16[16,64,4,1536]{3,1,2,0:T(8,128)(2,1)} fusion(f32[16,64,4,1536]{3,1,2,0:T(8,128)} %get-tuple-element.55, bf16[16,8,8,4,384]{4,1,0,3,2:T(8,128)(2,1)} %bitcast.50, bf16[2,1536,384]{2,1,0:T(8,128)(2,1)S(1)} %copy-done.58), kind=kOutput, calls=%fused_computation.14 | convolution fusion | flops 4970250240 | bytes 42074112 | tf_op jit(solution)/shard_map/bacd,fd->bacf/dot_general | solution.py:61
  354.6 17.4 %convert_bitcast_fusion.8 = bf16[1,16,64,4,6,64]{2,5,4,3,1,0:T(8,128)(2,1)} fusion(bf16[16,4,6,64,64]{3,4,2,1,0:T(8,128)(2,1)} %divide_convert_fusion, bf16[16,4,6,64,64]{3,4,2,1,0:T(8,128)(2,1)} %fusion.128, bf16[3,16,64,4,6,64]{5,2,4,0,3,1:T(8,128)(2,1)} %convert_bitcast_fusion), kind=kOutput, calls=%fused_computation.176 | convolution fusion | flops 217079872 | bytes 18874368 | tf_op jit(solution)/shard_map/bchmn,bnche->bmche/dot_general | solution.py:80
  372.1 17.5 %convert_bitcast_fusion.7 = bf16[1,16,64,4,6,64]{2,5,4,3,1,0:T(8,128)(2,1)} fusion(bf16[16,4,6,64,64]{3,4,2,1,0:T(8,128)(2,1)} %divide_convert_fusion, bf16[16,4,6,64,64]{3,4,2,1,0:T(8,128)(2,1)} %fusion.128, bf16[3,16,64,4,6,64]{5,2,4,0,3,1:T(8,128)(2,1)} %convert_bitcast_fusion), kind=kOutput, calls=%fused_computation.175 | convolution fusion | flops 217079872 | bytes 18874368 | tf_op jit(solution)/shard_map/bchmn,bmche->bnche/dot_general | solution.py:81
  389.8 20.7 %fusion.219 = (bf16[3,6,64,64,16,4]{3,2,1,5,4,0:T(8,128)(2,1)}, bf16[3,16,64,4,6,64]{2,5,4,3,1,0:T(8,128)(2,1)}) fusion(bf16[1,16,64,4,6,64]{2,5,4,3,1,0:T(8,128)(2,1)} %convert_bitcast_fusion.6, bf16[1,16,64,4,6,64]{2,5,4,3,1,0:T(8,128)(2,1)} %convert_bitcast_fusion.7, bf16[1,16,64,4,6,64]{2,5,4,3,1,0:T(8,128)(2,1)} %convert_bitcast_fusion.8), kind=kLoop, calls=%fused_computation.299 | loop fusion | flops 9437184 | bytes 28311552 | tf_op jit(solution)/shard_map/bacd,kbache->dkhe/dot_general | solution.py:90
  435.7 29.6 %copy.302 = bf16[3,6,64,64,16,4]{2,1,0,3,5,4:T(8,128)(2,1)} copy(bf16[3,6,64,64,16,4]{3,2,1,5,4,0:T(8,128)(2,1)} %get-tuple-element.37) | data formatting | bytes 18874368 | tf_op jit(solution)/shard_map/bacd,kbache->dkhe/dot_general | solution.py:90
  465.4 29.9 %reshape.188 = bf16[1152,64,16,4]{0,1,3,2:T(8,128)(2,1)} reshape(bf16[3,6,64,64,16,4]{2,1,0,3,5,4:T(8,128)(2,1)} %copy.302) | data formatting | bytes 18874368 | tf_op jit(solution)/shard_map/bacd,kbache->dkhe/dot_general | solution.py:90
  526.8 11.7 %fusion.154 = f32[1,1536,384]{2,1,0:T(8,128)} fusion(bf16[16,8,32,384]{3,2,1,0:T(8,128)(2,1)} %all_to_all.58, bf16[16,8,32,1536]{3,2,1,0:T(8,128)(2,1)} %get-tuple-element.48), kind=kOutput, calls=%fused_computation.221 | convolution fusion | flops 4831838208 | bytes 18087936 | tf_op jit(solution)/shard_map/bacf,bacd->fd/dot_general | solution.py:60
  538.6 22.7 %fusion.11 = bf16[16,8,32,1536]{3,2,1,0:T(8,128)(2,1)} fusion(f32[16,8,32,1536]{3,2,1,0:T(8,128)} %get-tuple-element.49, bf16[16,8,32,384]{3,2,1,0:T(8,128)(2,1)S(1)} %copy-done.10, bf16[2,1536,384]{2,1,0:T(8,128)(2,1)S(1)} %copy-done.59), kind=kOutput, calls=%fused_computation.19 | convolution fusion | flops 4970250240 | bytes 42074112 | tf_op jit(solution)/shard_map/bacd,fd->bacf/dot_general | solution.py:61
  561.3 11.5 %fusion.159 = f32[1,384,1536]{2,1,0:T(8,128)} fusion(bf16[16,8,32,1536]{3,2,1,0:T(8,128)(2,1)} %fusion.11, bf16[16,8,32,384]{3,2,1,0:T(8,128)(2,1)S(1)} %copy-done.9, f32[384]{0:T(512)S(1)} %copy-done.49, f32[384]{0:T(512)S(1)} %copy-done.47, f32[16,8,32]{2,1,0:T(8,128)S(1)} %copy-done.34, f32[16,8,32]{2,1,0:T(8,128)S(1)} %copy-done.28), kind=kOutput, calls=%fused_computation.223 | convolution fusion | flops 4841275392 | bytes 18123776 | tf_op jit(solution)/shard_map/bacd,bacf->df/dot_general | solution.py:64
  610.5 17.2 %convert_bitcast_fusion.5 = bf16[1,16,8,32,6,64]{5,3,4,2,1,0:T(8,128)(2,1)} fusion(bf16[16,8,6,32,32]{3,4,2,1,0:T(8,128)(2,1)} %divide_convert_fusion.1, bf16[16,8,6,32,32]{3,4,2,1,0:T(8,128)(2,1)} %fusion.129, bf16[3,16,8,32,6,64]{5,3,4,0,2,1:T(8,128)(2,1)} %convert_bitcast_fusion.1), kind=kOutput, calls=%fused_computation.173 | convolution fusion | flops 109338656 | bytes 15728640 | tf_op jit(solution)/shard_map/bahmn,banhe->bamhe/dot_general | solution.py:80
  627.7 14.9 %convert_bitcast_fusion.4 = bf16[1,16,8,32,6,64]{5,3,4,2,1,0:T(8,128)(2,1)} fusion(bf16[3,16,8,32,6,64]{5,3,4,0,2,1:T(8,128)(2,1)} %convert_bitcast_fusion.1, bf16[16,8,6,32,32]{3,4,2,1,0:T(8,128)(2,1)} %divide_convert_fusion.1, bf16[16,8,6,32,32]{3,4,2,1,0:T(8,128)(2,1)} %fusion.129), kind=kOutput, calls=%fused_computation.172 | convolution fusion | flops 109338656 | bytes 15728640 | tf_op jit(solution)/shard_map/bahmn,bamhe->banhe/dot_general | solution.py:81
  699.0 68.2 %all-to-all-done.1 = bf16[16,64,4,384]{3,2,0,1:T(4,128)(2,1)} async-done(((bf16[16,64,4,384]{3,2,0,1:T(4,128)(2,1)}), bf16[16,64,4,384]{3,2,0,1:T(4,128)(2,1)}, u32[]{:S(2)}, u32[]{:S(2)}) %all-to-all-start.1) | async-done | bytes 3145760 | tf_op jit(solution)/shard_map/all_to_all | solution.py:122
  778.2 25.5 %psum.35 = f32[2,4,384]{2,1,0:T(4,128)} all-reduce(f32[2,4,384]{2,1,0:T(4,128)S(1)} %pad_maximum_fusion.6), channel_id=1, replica_groups=mesh['data'=1,'sp'=8] {'sp'}, use_global_device_ids=true, to_apply=%region_30.0 | all-reduce | flops 3072 | bytes 24576 | tf_op jit(solution)/shard_map/psum | solution.py:127
  809.9 85.1 %all-reduce.3.cloned.1.call-done = (f32[2,384,1152]{2,1,0:T(8,128)}, f32[2,6,64,384]{3,2,1,0:T(8,128)}, f32[2,384,1536]{2,1,0:T(8,128)}, f32[2,1536,384]{2,1,0:T(8,128)}) async-done(((f32[2,384,1152]{2,1,0:T(8,128)}, f32[2,6,64,384]{3,2,1,0:T(8,128)}, f32[2,384,1536]{2,1,0:T(8,128)}, f32[2,1536,384]{2,1,0:T(8,128)}), (f32[2,384,1152]{2,1,0:T(8,128)}, f32[2,6,64,384]{3,2,1,0:T(8,128)}, ...) | async-done | bytes 14155792 | tf_op jit(solution)/shard_map/psum | solution.py:127
  (252 shorter events, 332.1 us)
Async XLA Ops:
  8.1 23.9 %copy-start.40 = (f32[384]{0:T(512)}, f32[384]{0:T(512)S(1)}, u32[]{:S(2)}) copy-start(f32[384]{0:T(512)S(1)} %get-tuple-element.30) | copy-start | bytes 4612
  8.1 23.9 %copy-start.44 = (f32[384]{0:T(512)}, f32[384]{0:T(512)S(1)}, u32[]{:S(2)}) copy-start(f32[384]{0:T(512)S(1)} %get-tuple-element.29) | copy-start | bytes 4612
  8.1 91.2 %copy-start.46 = (f32[384]{0:T(512)}, f32[384]{0:T(512)S(1)}, u32[]{:S(2)}) copy-start(f32[384]{0:T(512)S(1)} %get-tuple-element.27) | copy-start | bytes 4612
  8.1 91.2 %copy-start.48 = (f32[384]{0:T(512)}, f32[384]{0:T(512)S(1)}, u32[]{:S(2)}) copy-start(f32[384]{0:T(512)S(1)} %get-tuple-element.28) | copy-start | bytes 4612
  10.8 21.2 %copy-start.21 = (f32[16,8,32]{2,1,0:T(8,128)}, f32[16,8,32]{2,1,0:T(8,128)S(1)}, u32[]{:S(2)}) copy-start(f32[16,8,32]{2,1,0:T(8,128)S(1)} %broadcast_multiply_fusion.6) | copy-start | bytes 49156
  13.7 18.3 %copy-start.25 = (f32[16,8,32]{2,1,0:T(8,128)}, f32[16,8,32]{2,1,0:T(8,128)S(1)}, u32[]{:S(2)}) copy-start(f32[16,8,32]{2,1,0:T(8,128)S(1)} %add_rsqrt_fusion.2) | copy-start | bytes 49156
  80.8 18.5 %copy-start.54 = (bf16[2,384,1536]{2,1,0:T(8,128)(2,1)S(1)}, bf16[2,384,1536]{2,1,0:T(8,128)(2,1)}, u32[]{:S(2)}) copy-start(bf16[2,384,1536]{2,1,0:T(8,128)(2,1)} %param.12) | copy-start | bytes 7077892
  127.6 42.1 %all-to-all-start = ((bf16[16,8,32,384]{3,1,0,2:T(8,128)(2,1)}), bf16[16,8,32,384]{3,1,0,2:T(8,128)(2,1)S(1)}, u32[]{:S(2)}, u32[]{:S(2)}) async-start(bf16[16,8,32,384]{3,1,0,2:T(8,128)(2,1)} %copy.215), calls=%async_computation | async-start | bytes 6291456 | tf_op jit(solution)/shard_map/all_to_all | solution.py:120
  138.8 46.1 %copy-start.38 = (f32[384]{0:T(512)}, f32[384]{0:T(512)S(1)}, u32[]{:S(2)}) copy-start(f32[384]{0:T(512)S(1)} %get-tuple-element.26) | copy-start | bytes 4612
  138.8 46.1 %copy-start.50 = (f32[384]{0:T(512)}, f32[384]{0:T(512)S(1)}, u32[]{:S(2)}) copy-start(f32[384]{0:T(512)S(1)} %get-tuple-element.25) | copy-start | bytes 4612
  171.4 102.6 %all-to-all-start.2 = ((bf16[16,8,32,384]{3,1,0,2:T(8,128)(2,1)}), bf16[16,8,32,384]{3,1,0,2:T(8,128)(2,1)}, u32[]{:S(2)}, u32[]{:S(2)}) async-start(bf16[16,8,32,384]{3,1,0,2:T(8,128)(2,1)} %copy.233), calls=%async_computation.2 | async-start | bytes 6291456 | tf_op jit(solution)/shard_map/all_to_all | solution.py:123
  176.9 71.3 %copy-start = (bf16[16,8,32,384]{3,1,2,0:T(8,128)(2,1)}, bf16[16,8,32,384]{3,1,2,0:T(8,128)(2,1)S(1)}, u32[]{:S(2)}) copy-start(bf16[16,8,32,384]{3,1,2,0:T(8,128)(2,1)S(1)} %copy.216) | copy-start | bytes 9437188
  273.9 24.2 %copy-start.6 = (bf16[16,64,4,384]{3,1,2,0:T(8,128)(2,1)S(1)}, bf16[16,64,4,384]{3,1,2,0:T(8,128)(2,1)}, u32[]{:S(2)}) copy-start(bf16[16,64,4,384]{3,1,2,0:T(8,128)(2,1)} %copy-done.5) | copy-start | bytes 9437188
  389.8 20.7 %copy-start.24 = (bf16[1,384,1152]{1,2,0:T(8,128)(2,1)S(1)}, bf16[1,384,1152]{1,2,0:T(8,128)(2,1)}, u32[]{:S(2)}) copy-start(bf16[1,384,1152]{1,2,0:T(8,128)(2,1)} %copy.225) | copy-start | bytes 2654212
  432.5 88.2 %all-to-all-start.3 = ((bf16[16,64,4,384]{3,2,0,1:T(4,128)(2,1)}), bf16[16,64,4,384]{3,2,0,1:T(4,128)(2,1)}, u32[]{:S(2)}, u32[]{:S(2)}) async-start(bf16[16,64,4,384]{3,2,0,1:T(4,128)(2,1)} %copy.244), calls=%async_computation.3 | async-start | bytes 6291456 | tf_op jit(solution)/shard_map/all_to_all | solution.py:125
  435.7 459.3 %all-reduce.3.cloned.1.call-start = ((), (), s32[]{:S(2)}) async-start(), calls=%async_computation.4 | async-start | bytes 28311552 | tf_op jit(solution)/shard_map/psum | solution.py:127
  465.4 29.9 %copy-start.51 = (f32[384]{0:T(512)S(1)}, f32[384]{0:T(512)}, u32[]{:S(2)}) copy-start(f32[384]{0:T(512)} %copy-done.50) | copy-start | bytes 4612
  538.5 22.7 %copy-start.9 = (bf16[16,8,32,384]{3,2,1,0:T(8,128)(2,1)S(1)}, bf16[16,8,32,384]{3,2,1,0:T(8,128)(2,1)}, u32[]{:S(2)}) copy-start(bf16[16,8,32,384]{3,2,1,0:T(8,128)(2,1)} %copy-done.8) | copy-start | bytes 9437188
  538.6 22.7 %copy-start.28 = (f32[16,8,32]{2,1,0:T(8,128)S(1)}, f32[16,8,32]{2,1,0:T(8,128)}, u32[]{:S(2)}) copy-start(f32[16,8,32]{2,1,0:T(8,128)} %copy-done.27) | copy-start | bytes 49156
  538.6 22.7 %copy-start.34 = (f32[16,8,32]{2,1,0:T(8,128)S(1)}, f32[16,8,32]{2,1,0:T(8,128)}, u32[]{:S(2)}) copy-start(f32[16,8,32]{2,1,0:T(8,128)} %copy-done.33) | copy-start | bytes 49156
  538.6 22.7 %copy-start.47 = (f32[384]{0:T(512)S(1)}, f32[384]{0:T(512)}, u32[]{:S(2)}) copy-start(f32[384]{0:T(512)} %copy-done.46) | copy-start | bytes 4612
  538.6 22.7 %copy-start.49 = (f32[384]{0:T(512)S(1)}, f32[384]{0:T(512)}, u32[]{:S(2)}) copy-start(f32[384]{0:T(512)} %copy-done.48) | copy-start | bytes 4612
  561.3 25.9 %slice-start.2 = ((s8[6291456]{0:T(1024)(128)(4,1)}), s8[4194304]{0:T(1024)(128)(4,1)S(1)}, s32[]{:S(2)}) async-start(s8[6291456]{0:T(1024)(128)(4,1)} %bitcast.352), calls=%async_computation.7 | async-start | bytes 8388608
  695.7 71.5 %all-to-all-start.1 = ((bf16[16,64,4,384]{3,2,0,1:T(4,128)(2,1)}), bf16[16,64,4,384]{3,2,0,1:T(4,128)(2,1)}, u32[]{:S(2)}, u32[]{:S(2)}) async-start(bf16[16,64,4,384]{3,2,0,1:T(4,128)(2,1)} %copy.229), calls=%async_computation.1 | async-start | bytes 6291456 | tf_op jit(solution)/shard_map/all_to_all | solution.py:122
  (54 other events, 448.2 us)
Sparse Core Ops, SparseCore 0:
  680.9 214.0 all-reduce.2
where the time goes:
time: 914 us; the launch traced here: 913 us
  matrix products  422 us (46%)
  waiting for transfers between devices  184 us (20%)
  other arithmetic  127 us (14%)
  local copies, waits for them, and re-layouts  126 us (14%)
  blocking collectives  25.5 us (3%)
  between operations  15.5 us (2%)
  starting transfers between devices  13.9 us (2%)
    psum x1, waiting for transfers between devices, device_step(): lax.psum([jnp.stack([grad_s, grad_t]) for grad_s, grad_t in zip(spatial_g...  85.1 us
    all_to_all x1, waiting for transfers between devices, device_step(): result = lax.all_to_all(out_swap, 'sp', 1, 2, tiled=True)  68.2 us
    dot_general x2, local copies, waits for them, and re-layouts, qkv_backward(): jnp.einsum('bacd,kbache->dkhe', a_in, d_qkv, preferred_element_type=jnp.f...  59.6 us
    dot_general x2, matrix products, tail_backward(): jnp.einsum('bacd,fd->bacf', d_block_out, w_down, preferred_element_type=j...  46.8 us
    dot_general x2, matrix products, attend_backward(): jnp.einsum(attn_forms[1], d_scores, qkv_heads[1], preferred_element_type=...  34.6 us
    sub x2, other arithmetic, attend_forward(): attn_probs = jax.nn.softmax(scores, axis=-1).astype(jnp.bfloat16)  34.3 us
    dot_general x2, matrix products, tail_forward(): up_proj = jnp.dot(m_in, w_up, preferred_element_type=jnp.float32)  32.5 us
    dot_general x2, matrix products, attend_backward(): jnp.einsum(attn_forms[2], d_scores, qkv_heads[0], preferred_element_type=...  32.4 us
  transfers between devices with their start and end apart: 5, of which 3 were waited for; matrix products, arithmetic and copies ran while one was open for 24% of the time, Pallas kernels for 0%

commit v1 on v0

v1 whole, which is shorter than its diff:
```python
import functools

import jax
import jax.numpy as jnp
import numpy as np
from jax import lax
from jax.experimental import pallas as pl
from jax.experimental.pallas import tpu as pltpu
from jax.sharding import PartitionSpec as P

BF16 = jnp.bfloat16
F32 = jnp.float32
N_DEV = 8
WIDTH = 384
HIDDEN = 4 * WIDTH
QKV = 3 * WIDTH
VIDEOS = 16
HALF = 8
ROWS = 256
NV = 2
STEP_ROWS = ROWS * NV
GROUP = 128
PAIRS = 3
SCALE = 0.125
LOG2E = 1.4426950408889634
GELU_C = 0.7978845608028654
GELU_C3 = GELU_C * 0.044715
VMEM_LIMIT = 62 * 1024 * 1024


def dot_nn(a, b):
    return lax.dot_general(a, b, (((1,), (0,)), ((), ())), preferred_element_type=F32)


def dot_nt(a, b):
    return lax.dot_general(a, b, (((1,), (1,)), ((), ())), preferred_element_type=F32)


def dot_tn(a, b):
    return lax.dot_general(a, b, (((0,), (0,)), ((), ())), preferred_element_type=F32)


def norm_stats(x32):
    centered = x32 - jnp.mean(x32, axis=-1, keepdims=True)
    inv_std = lax.rsqrt(jnp.mean(centered * centered, axis=-1, keepdims=True) + 1e-6)
    return centered * inv_std, inv_std


def norm_back(d_out32, normed, inv_std, gain):
    d_gain = jnp.sum(d_out32 * normed, axis=0, keepdims=True)
    d_shift = jnp.sum(d_out32, axis=0, keepdims=True)
    d_norm = d_out32 * gain
    d_center = d_norm - jnp.mean(d_norm, axis=-1, keepdims=True)
    d_in = inv_std * (d_center - normed * jnp.mean(d_norm * normed, axis=-1, keepdims=True))
    return d_in, d_gain, d_shift


def gelu_parts(x):
    x2 = x * x
    t = jnp.tanh(x * (GELU_C + GELU_C3 * x2))
    half = 0.5 + 0.5 * t
    slope = half + (x * (0.5 - 0.5 * (t * t))) * (GELU_C + (3.0 * GELU_C3) * x2)
    return x * half, slope


def gelu_value(x):
    t = jnp.tanh(x * (GELU_C + GELU_C3 * (x * x)))
    return x * (0.5 + 0.5 * t)


def lane_masks():
    lane = lax.broadcasted_iota(jnp.int32, (1, GROUP), 1)
    low = (lane < GROUP // 2)
    m_low = jnp.where(low, 1.0, 0.0).astype(BF16)
    m_high = jnp.where(low, 0.0, 1.0).astype(BF16)
    return low, m_low, m_high


def split_heads(k, m_low, m_high):
    return jnp.concatenate([k * m_low, k * m_high], axis=0)


GROUPS = STEP_ROWS // GROUP
BLOCKS = [(g, pair) for g in range(GROUPS) for pair in range(PAIRS)]


def rows_of(g):
    return pl.ds(g * GROUP, GROUP)


def part(kind, pair):
    return pl.ds(kind * WIDTH + pair * GROUP, GROUP)


def both(pair):
    return pl.ds(pair * 2 * GROUP, 2 * GROUP)


def attend(qkv_ref, bias_ref, p_ref, o_ref, s_ref):
    low, m_low, m_high = lane_masks()
    for g, pair in BLOCKS:
        k2 = split_heads(qkv_ref[rows_of(g), part(1, pair)], m_low, m_high)
        s_ref[rows_of(g), both(pair)] = dot_nt(qkv_ref[rows_of(g), part(0, pair)], k2) * (SCALE * LOG2E) + bias_ref[...]
    for g, pair in BLOCKS:
        s = s_ref[rows_of(g), both(pair)]
        probs = []
        for h in range(2):
            s_h = s[:, h * GROUP:(h + 1) * GROUP]
            e_h = jnp.exp2(s_h - jnp.max(s_h, axis=-1, keepdims=True))
            probs.append(e_h * (1.0 / jnp.sum(e_h, axis=-1, keepdims=True)))
        p_ref[rows_of(g), both(pair)] = jnp.concatenate(probs, axis=1).astype(BF16)
    for g, pair in BLOCKS:
        v2 = split_heads(qkv_ref[rows_of(g), part(2, pair)], m_low, m_high)
        o_ref[rows_of(g), part(0, pair)] = dot_nn(p_ref[rows_of(g), both(pair)], v2).astype(BF16)


def attend_back(qkv_ref, p_ref, do_ref, dqkv_ref, dp_ref):
    low, m_low, m_high = lane_masks()
    for g, pair in BLOCKS:
        do = do_ref[rows_of(g), part(0, pair)]
        v2 = split_heads(qkv_ref[rows_of(g), part(2, pair)], m_low, m_high)
        dp_ref[rows_of(g), both(pair)] = dot_nt(do, v2).astype(BF16)
        dv = dot_tn(p_ref[rows_of(g), both(pair)], do)
        dqkv_ref[rows_of(g), part(2, pair)] = jnp.where(low, dv[:GROUP], dv[GROUP:]).astype(BF16)
    for g, pair in BLOCKS:
        p32 = p_ref[rows_of(g), both(pair)].astype(F32)
        t = dp_ref[rows_of(g), both(pair)].astype(F32) * p32
        ds = []
        for h in range(2):
            half = slice(h * GROUP, (h + 1) * GROUP)
            ds.append(t[:, half] - p32[:, half] * jnp.sum(t[:, half], axis=-1, keepdims=True))
        dp_ref[rows_of(g), both(pair)] = jnp.concatenate(ds, axis=1).astype(BF16)
    for g, pair in BLOCKS:
        ds = dp_ref[rows_of(g), both(pair)]
        k2 = split_heads(qkv_ref[rows_of(g), part(1, pair)], m_low, m_high)
        dqkv_ref[rows_of(g), part(0, pair)] = (dot_nn(ds, k2) * SCALE).astype(BF16)
        dk = dot_tn(ds, qkv_ref[rows_of(g), part(0, pair)])
        dqkv_ref[rows_of(g), part(1, pair)] = (jnp.where(low, dk[:GROUP], dk[GROUP:]) * SCALE).astype(BF16)


CHUNK = 512
CHUNKS = HIDDEN // CHUNK


def cut(c):
    return pl.ds(c * CHUNK, CHUNK)


def gains(ln_ref):
    ln = ln_ref[...].astype(F32)
    return [ln[r:r + 1, :] for r in range(4)]


def spatial_forward_kernel(n_alias, *refs):
    x_ref, dy_ref, ln_ref, wqkv_ref, wout_ref, wup_ref, wdown_ref, bias_ref, perm_ref = refs[:9]
    out_ref, h_ref, o_ref, qkv_ref, p_ref, act_ref, s_ref = refs[9 + n_alias:]
    gain1, shift1, gain2, shift2 = gains(ln_ref)
    normed, _ = norm_stats(x_ref[...].astype(F32))
    a_in = (normed * gain1 + shift1).astype(BF16)
    for c in range(3):
        cols = pl.ds(c * WIDTH, WIDTH)
        qkv_ref[:, cols] = dot_nn(a_in, wqkv_ref[:, cols]).astype(BF16)
    attend(qkv_ref, bias_ref, p_ref, o_ref, s_ref)
    h_ref[...] = (x_ref[...].astype(F32) + dot_nn(o_ref[...], wout_ref[...])).astype(BF16)
    normed, _ = norm_stats(h_ref[...].astype(F32))
    m_in = (normed * gain2 + shift2).astype(BF16)
    for c in range(CHUNKS):
        act_ref[:, cut(c)] = gelu_value(dot_nn(m_in, wup_ref[:, cut(c)])).astype(BF16)
    out = (h_ref[...].astype(F32) + dot_nn(act_ref[...], wdown_ref[...])).astype(BF16)
    for v in range(NV):
        moved = dot_nn(perm_ref[...], out[v * ROWS:(v + 1) * ROWS]).astype(BF16)
        for d in range(N_DEV):
            out_ref[d, 0, v] = moved[d * 32:(d + 1) * 32]
        moved = dot_nn(perm_ref[...], dy_ref[pl.ds(v * ROWS, ROWS), :]).astype(BF16)
        for d in range(N_DEV):
            out_ref[d, 1, v] = moved[d * 32:(d + 1) * 32]


def add_blocks(sum_ref, first, product):
    for c in range(product.shape[1] // WIDTH):
        rows = pl.ds(first + c * WIDTH, WIDTH)
        sum_ref[rows, :] += product[:, c * WIDTH:(c + 1) * WIDTH]


def tail_backward(dv_ref, o_ref, m_ref, normed, inv_std, gain2, gp_ref, act_ref, dup_ref, do_ref,
                  wout_ref, wup_ref, wdown_ref, sum_ref):
    add_blocks(sum_ref, ROW_DOWN, dot_tn(dv_ref[...], act_ref[...]))
    for c in range(CHUNKS):
        d_act = dot_nt(dv_ref[...], wdown_ref[cut(c), :]).astype(BF16).astype(F32)
        dup_ref[:, cut(c)] = (d_act * gp_ref[:, cut(c)]).astype(BF16)
    add_blocks(sum_ref, ROW_UP, dot_tn(m_ref[...], dup_ref[...]))
    d_m = dot_nt(dup_ref[...], wup_ref[...]).astype(BF16).astype(F32)
    d_h, g_gain, g_shift = norm_back(d_m, normed, inv_std, gain2)
    dv_ref[...] = (d_h + dv_ref[...].astype(F32)).astype(BF16)
    add_blocks(sum_ref, ROW_OUT, dot_tn(o_ref[...], dv_ref[...]))
    do_ref[...] = dot_nt(dv_ref[...], wout_ref[...]).astype(BF16)
    return g_gain, g_shift


def qkv_backward(u32, a_ref, dh_ref, dqkv_ref, gain1, wqkv_ref, sum_ref):
    normed, inv_std = norm_stats(u32)
    add_blocks(sum_ref, ROW_QKV, dot_tn(a_ref[...], dqkv_ref[...]))
    d_a = dot_nt(dqkv_ref[...], wqkv_ref[...]).astype(BF16).astype(F32)
    d_in, g_gain, g_shift = norm_back(d_a, normed, inv_std, gain1)
    return (d_in + dh_ref[...].astype(F32)).astype(BF16), g_gain, g_shift


def up_forward(h32, gain2, shift2, m_ref, wup_ref, act_ref, gp_ref):
    normed, inv_std = norm_stats(h32)
    m_ref[...] = (normed * gain2 + shift2).astype(BF16)
    for c in range(CHUNKS):
        act, slope = gelu_parts(dot_nn(m_ref[...], wup_ref[:, cut(c)]))
        act_ref[:, cut(c)] = act.astype(BF16)
        gp_ref[:, cut(c)] = slope
    return normed, inv_std


def add_ln_sums(ref, first, sums):
    for r, g in enumerate(sums):
        ref[first + r:first + r + 1, :] += g


def temporal_kernel(n_sums, *refs):
    act_in_ref, ln_ref, wqkv_ref, wout_ref, wup_ref, wdown_ref, bias_ref = refs[:7]
    sums_in = refs[7:7 + n_sums]
    (out_ref, sum_ref, u_ref, dv_ref, a_ref, qkv_ref, p_ref, o_ref, m_ref, act_ref,
     dup_ref, do_ref, dqkv_ref, dp_ref, gp_ref, s_ref) = refs[7 + n_sums:]

    @pl.when(pl.program_id(0) == 0)
    def _():
        sum_ref[...] = sums_in[0][...] if n_sums else jnp.zeros_like(sum_ref)

    gain1, shift1, gain2, shift2 = gains(ln_ref)
    places = [(v, g, s) for v in range(NV) for g in range(2) for s in range(N_DEV)]
    for v, g, s in places:
        dst = pl.ds(v * ROWS + g * GROUP + s * 16, 16)
        u_ref[dst, :] = act_in_ref[s, 0, v, pl.ds(g * 16, 16), :]
        dv_ref[dst, :] = act_in_ref[s, 1, v, pl.ds(g * 16, 16), :]
    normed1, _ = norm_stats(u_ref[...].astype(F32))
    a_ref[...] = (normed1 * gain1 + shift1).astype(BF16)
    for c in range(3):
        cols = pl.ds(c * WIDTH, WIDTH)
        qkv_ref[:, cols] = dot_nn(a_ref[...], wqkv_ref[:, cols]).astype(BF16)
    attend(qkv_ref, bias_ref, p_ref, o_ref, s_ref)
    h = (u_ref[...].astype(F32) + dot_nn(o_ref[...], wout_ref[...])).astype(BF16)
    h32 = h.astype(F32)
    normed, inv_std = up_forward(h32, gain2, shift2, m_ref, wup_ref, act_ref, gp_ref)
    out = (h32 + dot_nn(act_ref[...], wdown_ref[...])).astype(BF16)
    for v, g, s in places:
        src = v * ROWS + g * GROUP + s * 16
        out_ref[s, 0, v, pl.ds(g * 16, 16), :] = out[src:src + 16]
    g_gain2, g_shift2 = tail_backward(dv_ref, o_ref, m_ref, normed, inv_std, gain2, gp_ref, act_ref, dup_ref, do_ref,
                                      wout_ref, wup_ref, wdown_ref, sum_ref)
    attend_back(qkv_ref, p_ref, do_ref, dqkv_ref, dp_ref)
    d_in, g_gain1, g_shift1 = qkv_backward(u_ref[...].astype(F32), a_ref, dv_ref, dqkv_ref, gain1, wqkv_ref, sum_ref)
    add_ln_sums(sum_ref, SUM_ROWS, (g_gain1, g_shift1, g_gain2, g_shift2))
    for v, g, s in places:
        src = v * ROWS + g * GROUP + s * 16
        out_ref[s, 1, v, pl.ds(g * 16, 16), :] = d_in[src:src + 16]


def position():
    me = lax.axis_index('sp')
    y, x, c = me // 4, (me // 2) % 2, me % 2
    return me, y, x, c, 4 * y + 2 * x + 1 - c, 4 * y + 2 * (1 - x) + c, 4 * (1 - y) + 2 * x + c


def span(k, idx, n):
    return pl.ds(pl.multiple_of(k * LAP_ROWS + idx * BLOCK, 16), n * BLOCK)


def slot(k, idx, n):
    return pl.ds((k * SLOTS + idx) * BLOCK, n * BLOCK)


def reduce_copies(phase, k, w_ref, r_ref, sems):
    _, y, x, c, partner, xn, yn = position()
    own0, own1 = c * 8 + x * 2, c * 8 + 4 + y * 2
    moves = (
        [((1 - c) * 8, 8, 0, partner)],
        [(c * 8 + (1 - x) * 2, 2, 8, xn), (c * 8 + 4 + (1 - y) * 2, 2, 10, yn)],
        [(own0 + 1 - y, 1, 12, yn), (own1 + 1 - x, 1, 13, xn)],
        [(own0 + y, 1, None, yn), (own1 + x, 1, None, xn)],
        [(own0, 2, None, xn), (own1, 2, None, yn)],
        [(c * 8, 8, None, partner)],
    )[phase]
    copies = []
    for j, (idx, n, place, device) in enumerate(moves):
        src = w_ref.at[span(k, idx, n), :]
        dst = src if place is None else r_ref.at[slot(k, place, n), :]
        copies.append(pltpu.make_async_remote_copy(
            src_ref=src, dst_ref=dst, send_sem=sems.at[0, phase, k, j], recv_sem=sems.at[1, phase, k, j],
            device_id={'sp': device}, device_id_type=pl.DeviceIdType.MESH))
    return copies


def reduce_peers(phase):
    _, _, _, _, partner, xn, yn = position()
    return ([partner], [xn, yn], [yn, xn])[phase]


def reduce_start(phase, k, w_ref, r_ref, sems, credits):
    copies = reduce_copies(phase, k, w_ref, r_ref, sems)
    for j, copy in enumerate(copies):
        if phase >= 3:
            pl.semaphore_wait(credits.at[5 - phase, k, j], 1)
        copy.start()


def reduce_finish(phase, k, w_ref, r_ref, sems, credits):
    for j, copy in enumerate(reduce_copies(phase, k, w_ref, r_ref, sems)):
        copy.wait()
        if phase < 3:
            pl.semaphore_signal(credits.at[phase, k, j], inc=1, device_id={'sp': reduce_peers(phase)[j]},
                                device_id_type=pl.DeviceIdType.MESH)
    _, y, x, c, _, _, _ = position()
    own0, own1 = c * 8 + x * 2, c * 8 + 4 + y * 2
    adds = ([(c * 8, 8, 0)], [(own0, 2, 8), (own1, 2, 10)], [(own0 + y, 1, 12), (own1 + x, 1, 13)], (), (), ())[phase]
    for idx, n, place in adds:
        def body(i, carry):
            w_rows = pl.ds(pl.multiple_of(k * LAP_ROWS + (idx + i) * BLOCK, 16), BLOCK)
            r_rows = pl.ds(pl.multiple_of((k * SLOTS + place + i) * BLOCK, 16), BLOCK)
            w_ref[w_rows, :] += r_ref[r_rows, :]
            return carry
        lax.fori_loop(0, n, body, 0)


def enter():
    me = lax.axis_index('sp')
    barrier = pltpu.get_barrier_semaphore()
    for d in range(1, N_DEV):
        pl.semaphore_signal(barrier, inc=1, device_id={'sp': lax.rem(me + d, N_DEV)},
                            device_id_type=pl.DeviceIdType.MESH)
    pl.semaphore_wait(barrier, N_DEV - 1)


def ln_copies(ln_ref, sems):
    me = lax.axis_index('sp')
    return [pltpu.make_async_remote_copy(
        src_ref=ln_ref.at[me], dst_ref=ln_ref.at[me], send_sem=sems.at[0, d], recv_sem=sems.at[1, d],
        device_id={'sp': lax.rem(me + d, N_DEV)}, device_id_type=pl.DeviceIdType.MESH) for d in range(1, N_DEV)]


def spatial_backward_kernel(*refs):
    (back_ref, x_ref, h_ref, o_ref, qkv_ref, p_ref,
     ln_ref, wqkv_ref, wout_ref, wup_ref, wdown_ref, perm_ref, gt_ref) = refs[:13]
    (y_ref, dx_ref, rt_ref, rs_ref, lnsum_ref, dv_ref, a_ref, m_ref, act_ref, dup_ref, do_ref, dqkv_ref, dp_ref, gp_ref,
     sum_ref, t_ref, rb_s_ref, rb_t_ref, ln_s_ref, ln_all_ref, sems_s, sems_t, credits_s, credits_t,
     sems_ln, sems_io) = refs[13:]
    step, last = pl.program_id(0), pl.num_programs(0) - 1
    me = lax.axis_index('sp')
    load_t = pltpu.make_async_copy(gt_ref.at[pl.ds(0, SUM_ROWS), :], t_ref, sems_io.at[0])
    load_ln = pltpu.make_async_copy(gt_ref.at[pl.ds(SUM_ROWS, 8), :], ln_all_ref.at[me, pl.ds(0, 8), :], sems_io.at[1])
    args_t, args_s = (t_ref, rb_t_ref, sems_t, credits_t), (sum_ref, rb_s_ref, sems_s, credits_s)

    @pl.when(step == 0)
    def _():
        enter()
        load_t.start()
        load_ln.start()
        sum_ref[...] = jnp.zeros_like(sum_ref)
        ln_s_ref[...] = jnp.zeros_like(ln_s_ref)

    @pl.when(step == 1)
    def _():
        load_t.wait()
        load_ln.wait()
        for k in range(LAPS):
            reduce_start(0, k, *args_t)

    for phase, at in enumerate(T_FINISH):
        @pl.when(step == at)
        def _(phase=phase):
            for k in range(LAPS):
                reduce_finish(phase, k, *args_t)
                reduce_start(phase + 1, k, *args_t)

    gain1, shift1, gain2, shift2 = gains(ln_ref)
    for v in range(NV):
        rows = pl.ds(v * ROWS, ROWS)
        dv_ref[rows, :] = dot_tn(perm_ref[...], back_ref[:, 1, v].reshape(ROWS, WIDTH)).astype(BF16)
        y_ref[rows, :] = dot_tn(perm_ref[...], back_ref[:, 0, v].reshape(ROWS, WIDTH)).astype(BF16)
    normed1, _ = norm_stats(x_ref[...].astype(F32))
    a_ref[...] = (normed1 * gain1 + shift1).astype(BF16)
    normed, inv_std = up_forward(h_ref[...].astype(F32), gain2, shift2, m_ref, wup_ref, act_ref, gp_ref)
    g_gain2, g_shift2 = tail_backward(dv_ref, o_ref, m_ref, normed, inv_std, gain2, gp_ref, act_ref, dup_ref, do_ref,
                                      wout_ref, wup_ref, wdown_ref, sum_ref)
    attend_back(qkv_ref, p_ref, do_ref, dqkv_ref, dp_ref)
    d_in, g_gain1, g_shift1 = qkv_backward(x_ref[...].astype(F32), a_ref, dv_ref, dqkv_ref, gain1, wqkv_ref, sum_ref)
    add_ln_sums(ln_s_ref, 0, (g_gain1, g_shift1, g_gain2, g_shift2))
    dx_ref[...] = d_in

    @pl.when(step == last)
    def _():
        ln_all_ref[me, pl.ds(8, 8), :] = ln_s_ref[...]
        for copy in ln_copies(ln_all_ref, sems_ln):
            copy.start()
        for k in range(LAPS):
            reduce_start(0, k, *args_s)
        for k in range(LAPS):
            reduce_finish(4, k, *args_t)
            reduce_start(5, k, *args_t)
        for phase in range(5):
            for k in range(LAPS):
                reduce_finish(phase, k, *args_s)
                reduce_start(phase + 1, k, *args_s)
            if phase == 0:
                for k in range(LAPS):
                    reduce_finish(5, k, *args_t)
                pltpu.make_async_copy(t_ref, rt_ref, sems_io.at[0]).start()
            if phase == 1:
                for copy in ln_copies(ln_all_ref, sems_ln):
                    copy.wait()
                total = ln_all_ref[0]
                for d in range(1, N_DEV):
                    total += ln_all_ref[d]
                lnsum_ref[...] = total
        outs = []
        for k in range(LAPS):
            reduce_finish(5, k, *args_s)
            lap = pl.ds(k * LAP_ROWS, LAP_ROWS)
            outs.append(pltpu.make_async_copy(sum_ref.at[lap, :], rs_ref.at[lap, :], sems_io.at[1 + k]))
            outs[-1].start()
        pltpu.make_async_copy(t_ref, rt_ref, sems_io.at[0]).wait()
        for copy in outs:
            copy.wait()


def assemble_kernel(s_ref, t_ref, ln_ref, qkv_ref, out_ref, up_ref, down_ref, gln_ref):
    block, part_id = pl.program_id(0), pl.program_id(1)
    moved = jnp.where(block == 0, s_ref[...], t_ref[...])

    @pl.when(part_id < 3)
    def _():
        qkv_ref[...] = moved

    @pl.when(part_id == 3)
    def _():
        out_ref[...] = moved
        gln_ref[...] = jnp.where(block == 0, ln_ref[8:12, :], ln_ref[0:4, :])

    @pl.when((part_id >= 4) & (part_id < 8))
    def _():
        up_ref[...] = moved

    @pl.when(part_id >= 8)
    def _():
        down_ref[...] = moved.T


def full(shape):
    return pl.BlockSpec(shape, lambda i: (0,) * len(shape), pipeline_mode=pl.Buffered(1))


def weight_specs(block):
    shapes = [(4, WIDTH), (WIDTH, QKV), (WIDTH, WIDTH), (WIDTH, HIDDEN), (HIDDEN, WIDTH)]
    return [pl.BlockSpec((None,) + s, lambda i: (block, 0, 0), pipeline_mode=pl.Buffered(1)) for s in shapes]


def rows_spec(width, first=0):
    return pl.BlockSpec((STEP_ROWS, width), lambda i: (i + first, 0))


def pair_spec():
    return pl.BlockSpec((N_DEV, 2, NV, 32, WIDTH), lambda i: (0, 0, i, 0, 0))


ANY = pl.BlockSpec(memory_space=pl.ANY)


def params():
    return pltpu.CompilerParams(dimension_semantics=("arbitrary",), vmem_limit_bytes=VMEM_LIMIT)


def cost(us, mib):
    return pl.CostEstimate(flops=int(us * 9e8), bytes_accessed=int(mib * 2 ** 20), transcendentals=0)


def sds(shape, dtype):
    return jax.ShapeDtypeStruct(shape, dtype)


def vm(width, dtype=BF16):
    return pltpu.VMEM((STEP_ROWS, width), dtype)


TOKENS = VIDEOS * ROWS
PROBS = 6 * GROUP
EXCHANGE = (N_DEV, 2, HALF, 32, WIDTH)
ROW_QKV, ROW_OUT, ROW_UP, ROW_DOWN = 0, 3 * WIDTH, 4 * WIDTH, 8 * WIDTH
SUM_ROWS = 12 * WIDTH
LAPS = 2
LAP_ROWS = SUM_ROWS // LAPS
BLOCK = LAP_ROWS // 16
SLOTS = 14
T_FINISH = (2, 4, 5, 6)


def spatial_forward_call(half, x, dy, weights, bias, perm, saved):
    first = half * (HALF // NV)
    widths = (WIDTH, WIDTH, QKV, PROBS)
    n_in = 9
    return pl.pallas_call(
        functools.partial(spatial_forward_kernel, len(saved)), grid=(HALF // NV,), name="spatial_fwd",
        in_specs=[rows_spec(WIDTH, first)] * 2 + weight_specs(0) + [full((GROUP, 2 * GROUP)), full((ROWS, ROWS))]
        + [ANY] * len(saved),
        out_specs=[pair_spec()] + [rows_spec(w, first) for w in widths],
        out_shape=[sds(EXCHANGE, BF16)] + [sds((TOKENS, w), BF16) for w in widths],
        scratch_shapes=[vm(HIDDEN), vm(PROBS, F32)],
        input_output_aliases={n_in + i: 1 + i for i in range(len(saved))},
        compiler_params=params(), cost_estimate=cost(25, 16),
    )(x, dy, *weights, bias, perm, *saved)


def temporal_call(acts, weights, bias, sums):
    n_in = 7
    return pl.pallas_call(
        functools.partial(temporal_kernel, len(sums)), grid=(HALF // NV,), name="temporal",
        in_specs=[pair_spec()] + weight_specs(1) + [full((GROUP, 2 * GROUP))] + [full((SUM_ROWS + 8, WIDTH))] * len(sums),
        out_specs=[pair_spec(), full((SUM_ROWS + 8, WIDTH))],
        out_shape=[sds(EXCHANGE, BF16), sds((SUM_ROWS + 8, WIDTH), F32)],
        scratch_shapes=[vm(w) for w in (WIDTH, WIDTH, WIDTH, QKV, PROBS, WIDTH, WIDTH, HIDDEN, HIDDEN, WIDTH, QKV, PROBS)]
        + [vm(HIDDEN, F32), vm(PROBS, F32)],
        input_output_aliases={n_in + i: 1 + i for i in range(len(sums))},
        compiler_params=params(), cost_estimate=cost(60, 20),
    )(acts, *weights, bias, *sums)


def spatial_backward_call(back, x, saved, weights, perm, sum_t):
    return pl.pallas_call(
        spatial_backward_kernel, grid=(VIDEOS // NV,), name="spatial_bwd",
        in_specs=[pl.BlockSpec((N_DEV, 2, NV, 32, WIDTH), lambda i: (0, 0, i, 0, 0))]
        + [rows_spec(w) for w in (WIDTH, WIDTH, WIDTH, QKV, PROBS)] + weight_specs(0) + [full((ROWS, ROWS)), ANY],
        out_specs=[rows_spec(WIDTH)] * 2 + [ANY, ANY, full((16, WIDTH))],
        out_shape=[sds((TOKENS, WIDTH), BF16)] * 2 + [sds((SUM_ROWS, WIDTH), F32)] * 2 + [sds((16, WIDTH), F32)],
        scratch_shapes=[vm(w) for w in (WIDTH, WIDTH, WIDTH, HIDDEN, HIDDEN, WIDTH, QKV, PROBS)] + [vm(HIDDEN, F32)]
        + [pltpu.VMEM((SUM_ROWS, WIDTH), F32)] * 2 + [pltpu.VMEM((LAPS * SLOTS * BLOCK, WIDTH), F32)] * 2
        + [pltpu.VMEM((8, WIDTH), F32), pltpu.VMEM((N_DEV, 16, WIDTH), F32)]
        + [pltpu.SemaphoreType.DMA((2, 6, LAPS, 2))] * 2 + [pltpu.SemaphoreType.REGULAR((3, LAPS, 2))] * 2
        + [pltpu.SemaphoreType.DMA((2, N_DEV)), pltpu.SemaphoreType.DMA((4,))],
        compiler_params=pltpu.CompilerParams(dimension_semantics=("arbitrary",), vmem_limit_bytes=VMEM_LIMIT,
                                             collective_id=1, has_side_effects=True),
        cost_estimate=cost(160, 60),
    )(back, x, *saved, *weights, perm, sum_t)


def assemble_call(sum_s, sum_t, ln_sums):
    def block(clip):
        return lambda b, j: (b,) + clip(j)
    grads = [(2, WIDTH, QKV), (2, WIDTH, WIDTH), (2, WIDTH, HIDDEN), (2, HIDDEN, WIDTH), (2, 4, WIDTH)]
    maps = [lambda j: (0, jnp.minimum(j, 2)), lambda j: (0, 0), lambda j: (0, jnp.clip(j - 4, 0, 3)),
            lambda j: (jnp.clip(j - 8, 0, 3), 0)]
    return pl.pallas_call(
        assemble_kernel, grid=(2, 12), name="assemble",
        in_specs=[pl.BlockSpec((WIDTH, WIDTH), lambda b, j: (jnp.where(b == 0, j, 11), 0)),
                  pl.BlockSpec((WIDTH, WIDTH), lambda b, j: (jnp.where(b == 0, 0, j), 0)),
                  pl.BlockSpec((16, WIDTH), lambda b, j: (0, 0))],
        out_specs=[pl.BlockSpec((None, WIDTH, WIDTH), block(m)) for m in maps]
        + [pl.BlockSpec((None, 4, WIDTH), lambda b, j: (b, 0, 0))],
        out_shape=[sds(g, F32) for g in grads],
        compiler_params=pltpu.CompilerParams(dimension_semantics=("arbitrary", "arbitrary"), vmem_limit_bytes=VMEM_LIMIT),
        cost_estimate=cost(10, 28),
    )(sum_s, sum_t, ln_sums)


def constants():
    row = np.arange(ROWS)
    dev, patch, frame = row // 32, (row // 8) % 4, row % 8
    perm = np.zeros((ROWS, ROWS), np.float32)
    perm[row, frame * 32 + dev * 4 + patch] = 1.0
    r = np.arange(GROUP)
    frame_of = r // 32
    patch_of = (r // 8) % 2
    bias_s = np.where(frame_of[:, None] == frame_of[None], 0.0, -np.inf).astype(np.float32)
    bias_t = np.where(patch_of[:, None] == patch_of[None], 0.0, -np.inf).astype(np.float32)
    return perm, np.concatenate([bias_s] * 2, 1), np.concatenate([bias_t] * 2, 1)


def swap(arr):
    return lax.all_to_all(arr, 'sp', 0, 0, tiled=True)


def device_step(latents, cotangent, ln_params, w_qkv, w_out, w_up, w_down):
    perm, bias_s, bias_t = constants()
    perm = jnp.asarray(perm, BF16)
    bias_s, bias_t = jnp.asarray(bias_s), jnp.asarray(bias_t)
    weights = (ln_params, w_qkv, w_out.reshape(2, WIDTH, WIDTH), w_up, w_down)
    x = latents.reshape(TOKENS, WIDTH)
    dy = cotangent.reshape(TOKENS, WIDTH)

    act_a, *saved = spatial_forward_call(0, x, dy, weights, bias_s, perm, ())
    act_a = swap(act_a)
    act_b, *saved = spatial_forward_call(1, x, dy, weights, bias_s, perm, saved)
    act_b = swap(act_b)
    back_a, sum_t = temporal_call(act_a, weights, bias_t, ())
    back_a = swap(back_a)
    back_b, sum_t = temporal_call(act_b, weights, bias_t, (sum_t,))
    back_b = swap(back_b)
    back = jnp.concatenate([back_a, back_b], axis=2)
    y, dx, sum_t, sum_s, ln_sums = spatial_backward_call(back, x, saved, weights, perm, sum_t)
    g_qkv, g_out, g_up, g_down, g_ln = assemble_call(sum_s, sum_t, ln_sums)
    g_out = g_out.reshape(2, 6, 64, WIDTH)
    shape = latents.shape
    return y.reshape(shape), dx.reshape(shape), g_ln, g_qkv, g_out, g_up, g_down


def solution(mesh):
    act_spec = P('data', 'sp', None, None)
    replicated = P()
    part_spec = P('data')
    return jax.shard_map(device_step, mesh=mesh,
                         in_specs=(act_spec, act_spec, replicated, replicated, replicated, replicated, replicated),
                         out_specs=(act_spec, act_spec, part_spec, part_spec, part_spec, part_spec, part_spec),
                         check_vma=False)
```

time: 914 us -> 444 us (0.49)
  matrix products: 422 us -> 0 us
  Pallas kernels: 0 us -> 325 us
  waiting for transfers between devices: 184 us -> 14 us
  other arithmetic: 127 us -> 3.31 us
  local copies, waits for them, and re-layouts: 126 us -> 5.81 us
  blocking collectives: 25.5 us -> 79.8 us
  between operations: 15.5 us -> 1.11 us
    dot_general x36 -> x0, matrix products: 422 us -> none  [the longest x2 46.8 us: tail_backward(): jnp.einsum('bacd,fd->bacf', d_block_out, w_down, preferred_element_type=j...]
    pallas_call x0 -> x6, Pallas kernels: none -> 325 us  [the longest x1 152 us: spatial_backward_call(): pl.pallas_call(spatial_backward_kernel, grid=(VIDEOS // NV,), name='spati...]
    all_to_all x4 -> x2, waiting for transfers between devices: 99.1 us -> 14 us  [swap(): return lax.all_to_all(arr, 'sp', 0, 0, tiled=True)]
    psum x1 -> x0, waiting for transfers between devices: 85.1 us -> none  [device_step(): lax.psum([jnp.stack([grad_s, grad_t]) for grad_s, grad_t in zip(spatial_g...]
    all_to_all x0 -> x2, blocking collectives: none -> 79.8 us  [swap(): return lax.all_to_all(arr, 'sp', 0, 0, tiled=True)]
    dot_general x2 -> x0, local copies, waits for them, and re-layouts: 59.6 us -> none  [qkv_backward(): jnp.einsum('bacd,kbache->dkhe', a_in, d_qkv, preferred_element_type=jnp.f...]
    convert_element_type x7 -> x0, other arithmetic: 37.2 us -> none  [the longest x2 18.9 us: attend_forward(): attn_probs = jax.nn.softmax(scores, axis=-1).astype(jnp.bfloat16)]
    sub x2 -> x0, other arithmetic: 34.3 us -> none  [attend_forward(): attn_probs = jax.nn.softmax(scores, axis=-1).astype(jnp.bfloat16)]
  transfers between devices with their start and end apart: 5 -> 2, of which waited for: 3 -> 1; matrix products, arithmetic and copies ran while one was open for 24% -> 0% of each run, Pallas kernels for 0% -> 17%
where the time goes in v1:
time: 444 us; the launch traced here: 437 us
  Pallas kernels  325 us (73%)
  blocking collectives  79.8 us (18%)
  waiting for transfers between devices  14 us (3%)
  starting transfers between devices  7.65 us (2%)
  local copies, waits for them, and re-layouts  5.81 us (1%)
    pallas_call x1, Pallas kernels, spatial_backward_call(): pl.pallas_call(spatial_backward_kernel, grid=(VIDEOS // NV,), name='spati...  152 us
    pallas_call x2, Pallas kernels, temporal_call(): pl.pallas_call(functools.partial(temporal_kernel, len(sums)), grid=(HALF...  105 us
    all_to_all x2, blocking collectives, swap(): return lax.all_to_all(arr, 'sp', 0, 0, tiled=True)  79.8 us
    pallas_call x2, Pallas kernels, spatial_forward_call(): pl.pallas_call(functools.partial(spatial_forward_kernel, len(saved)), gri...  47.7 us
    pallas_call x1, Pallas kernels, assemble_call(): pl.pallas_call(assemble_kernel, grid=(2, 12), name='assemble', in_specs=[...  20.4 us
    all_to_all x2, waiting for transfers between devices, swap(): return lax.all_to_all(arr, 'sp', 0, 0, tiled=True)  14 us
  transfers between devices with their start and end apart: 2, of which 1 were waited for; matrix products, arithmetic and copies ran while one was open for 0% of the time, Pallas kernels for 17%

profile of v1, /device:TPU:0, one launch (start us, length us, event | category | flops | bytes accessed | tf_op | source)
XLA Modules:
  0.0 436.6 jit_solution(15944080928362765007)
XLA Ops:
  0.6 23.8 %spatial_fwd.2 = (bf16[8,2,8,32,384]{4,3,2,1,0:T(8,128)(2,1)}, bf16[4096,384]{1,0:T(8,128)(2,1)}, bf16[4096,384]{1,0:T(8,128)(2,1)}, bf16[4096,1152]{1,0:T(8,128)(2,1)}, bf16[4096,768]{1,0:T(8,128)(2,1)}) custom-call(bf16[4096,384]{1,0:T(8,128)(2,1)} %bitcast.10, bf16[4096,384]{1,0:T(8,128)(2,1)} %bitcast.8, bf16[2,4,384]{2,1,0:T(4,128)(2,1)} %refs_6_.7, ...), custom_call_target="tpu_custom_call" | custom-call | flops 22499999744 | bytes 16777216 | tf_op jit(solution)/shard_map/spatial_fwd/pallas_call | solution.py:503
  24.5 4.3 all-to-all-start
  28.8 23.9 %spatial_fwd.3 = (bf16[8,2,8,32,384]{4,3,2,1,0:T(8,128)(2,1)}, bf16[4096,384]{1,0:T(8,128)(2,1)}, bf16[4096,384]{1,0:T(8,128)(2,1)}, bf16[4096,1152]{1,0:T(8,128)(2,1)}, bf16[4096,768]{1,0:T(8,128)(2,1)}) custom-call(bf16[4096,384]{1,0:T(8,128)(2,1)} %bitcast.11, ...), custom_call_target="tpu_custom_call", output_to_operand_aliasing={{1}: (9, {}), {2}: (10, {}), {3}: (11, {}), {4}: (12, {})} | custom-call | flops 22499999744 | bytes 16777216 | tf_op jit(solution)/shard_map/spatial_fwd/pallas_call | solution.py:503
  52.6 14.0 %all-to-all-done.refs_0_ = bf16[8,2,8,32,384]{4,3,2,1,0:T(8,128)(2,1)} async-done(((bf16[8,2,8,32,384]{4,3,2,1,0:T(8,128)(2,1)}), bf16[8,2,8,32,384]{4,3,2,1,0:T(8,128)(2,1)}, u32[]{:S(2)}, u32[]{:S(2)}) %all-to-all-start) | async-done | bytes 3145760 | tf_op jit(solution)/shard_map/all_to_all | solution.py:580
  66.6 3.4 all-to-all-start.2
  70.0 51.3 %temporal.2 = (bf16[8,2,8,32,384]{4,3,2,1,0:T(8,128)(2,1)}, f32[4616,384]{1,0:T(8,128)}) custom-call(bf16[8,2,8,32,384]{4,3,2,1,0:T(8,128)(2,1)} %all-to-all-done.refs_0_, bf16[2,4,384]{2,1,0:T(4,128)(2,1)} %refs_6_.7, bf16[2,384,1152]{2,1,0:T(8,128)(2,1)} %refs_7_.3, bf16[2,384,384]{2,1,0:T(8,128)(2,1)} %bitcast.15, bf16[2,384,1536]{2,1,0:T(8,128)(2,1)} %refs_9_.1, ...), custom_call_target="tpu_custom_call" | custom-call | flops 54000001024 | bytes 20971520 | tf_op jit(solution)/shard_map/temporal/pallas_call | solution.py:517
  121.3 0.0 all-to-all-done.2.refs_0_
  121.3 53.8 %temporal.3 = (bf16[8,2,8,32,384]{4,3,2,1,0:T(8,128)(2,1)}, f32[4616,384]{1,0:T(8,128)}) custom-call(bf16[8,2,8,32,384]{4,3,2,1,0:T(8,128)(2,1)} %all-to-all-done.2.refs_0_, bf16[2,4,384]{2,1,0:T(4,128)(2,1)} %refs_6_.7, bf16[2,384,1152]{2,1,0:T(8,128)(2,1)} %refs_7_.3, bf16[2,384,384]{2,1,0:T(8,128)(2,1)} %bitcast.16, ...), custom_call_target="tpu_custom_call", output_to_operand_aliasing={{1}: (7, {})} | custom-call | flops 54000001024 | bytes 20971520 | tf_op jit(solution)/shard_map/temporal/pallas_call | solution.py:517
  175.1 0.0 copy-start.1
  175.1 40.5 %all_to_all.20 = bf16[8,2,8,32,384]{4,3,2,1,0:T(8,128)(2,1)S(1)} all-to-all(bf16[8,2,8,32,384]{4,3,2,1,0:T(8,128)(2,1)} %get-tuple-element.39), channel_id=1, replica_groups=mesh['data'=1,'sp'=8] {'sp'}, dimensions={0} | all-to-all | bytes 6291456 | tf_op jit(solution)/shard_map/all_to_all | solution.py:580
  215.6 0.0 copy-done.1
  215.6 39.3 %all_to_all.21 = bf16[8,2,8,32,384]{4,3,2,1,0:T(8,128)(2,1)S(1)} all-to-all(bf16[8,2,8,32,384]{4,3,2,1,0:T(8,128)(2,1)S(1)} %copy-done.1), channel_id=1, replica_groups=mesh['data'=1,'sp'=8] {'sp'}, dimensions={0} | all-to-all | bytes 6291456 | tf_op jit(solution)/shard_map/all_to_all | solution.py:580
  254.9 3.3 pad_maximum_fusion.refs_0_
  258.2 151.8 %spatial_bwd.1 = (bf16[4096,384]{1,0:T(8,128)(2,1)}, bf16[4096,384]{1,0:T(8,128)(2,1)}, f32[4608,384]{1,0:T(8,128)}, f32[4608,384]{1,0:T(8,128)}, f32[16,384]{1,0:T(8,128)}) custom-call(bf16[8,2,16,32,384]{4,3,2,1,0:T(8,128)(2,1)} %pad_maximum_fusion.refs_0_, bf16[4096,384]{1,0:T(8,128)(2,1)} %bitcast.12, bf16[4096,384]{1,0:T(8,128)(2,1)} %get-tuple-element.40.refs_2_, ...), custom_call_target="tpu_custom_call" | custom-call | flops 143999991808 | bytes 62914560 | tf_op jit(solution)/shard_map/spatial_bwd/pallas_call | solution.py:530
  409.9 20.4 %assemble.1 = (f32[2,384,1152]{2,1,0:T(8,128)}, f32[2,384,384]{2,1,0:T(8,128)}, f32[2,384,1536]{2,1,0:T(8,128)}, f32[2,1536,384]{2,1,0:T(8,128)}, f32[2,4,384]{2,1,0:T(4,128)}) custom-call(f32[4608,384]{1,0:T(8,128)} %get-tuple-element.47.s_ref, f32[4608,384]{1,0:T(8,128)} %get-tuple-element.48.t_ref, f32[16,384]{1,0:T(8,128)} %get-tuple-element.49.ln_ref), custom_call_target="tpu_custom_call" | custom-call | flops 8999999488 | bytes 29360128 | tf_op jit(solution)/shard_map/assemble/pallas_call | solution.py:553
  430.3 0.0 copy-start
  430.3 4.1 copy.29
  434.4 0.0 copy-done
  434.4 1.7 copy.30
Async XLA Ops:
  24.5 42.1 %all-to-all-start = ((bf16[8,2,8,32,384]{4,3,2,1,0:T(8,128)(2,1)}), bf16[8,2,8,32,384]{4,3,2,1,0:T(8,128)(2,1)}, u32[]{:S(2)}, u32[]{:S(2)}) async-start(bf16[8,2,8,32,384]{4,3,2,1,0:T(8,128)(2,1)} %get-tuple-element.31), calls=%async_computation | async-start | bytes 6291456 | tf_op jit(solution)/shard_map/all_to_all | solution.py:580
  66.6 54.7 %all-to-all-start.2 = ((bf16[8,2,8,32,384]{4,3,2,1,0:T(8,128)(2,1)}), bf16[8,2,8,32,384]{4,3,2,1,0:T(8,128)(2,1)}, u32[]{:S(2)}, u32[]{:S(2)}) async-start(bf16[8,2,8,32,384]{4,3,2,1,0:T(8,128)(2,1)} %get-tuple-element.37), calls=%async_computation.2 | async-start | bytes 6291456 | tf_op jit(solution)/shard_map/all_to_all | solution.py:580
  175.1 40.5 %copy-start.1 = (bf16[8,2,8,32,384]{4,3,2,1,0:T(8,128)(2,1)S(1)}, bf16[8,2,8,32,384]{4,3,2,1,0:T(8,128)(2,1)}, u32[]{:S(2)}) copy-start(bf16[8,2,8,32,384]{4,3,2,1,0:T(8,128)(2,1)} %get-tuple-element.32) | copy-start | bytes 9437188
  430.3 4.1 copy-start

commit v2 on v1

--- a/solution.py
+++ b/solution.py
@@ -15,7 +15,6 @@
 HIDDEN = 4 * WIDTH
 QKV = 3 * WIDTH
 VIDEOS = 16
-HALF = 8
 ROWS = 256
 NV = 2
 STEP_ROWS = ROWS * NV
@@ -23,6 +22,7 @@
 PAIRS = 3
 SCALE = 0.125
 LOG2E = 1.4426950408889634
+STEPS = VIDEOS // NV
 GELU_C = 0.7978845608028654
 GELU_C3 = GELU_C * 0.044715
 VMEM_LIMIT = 62 * 1024 * 1024
@@ -151,9 +151,93 @@
     return [ln[r:r + 1, :] for r in range(4)]
 
 
-def spatial_forward_kernel(n_alias, *refs):
-    x_ref, dy_ref, ln_ref, wqkv_ref, wout_ref, wup_ref, wdown_ref, bias_ref, perm_ref = refs[:9]
-    out_ref, h_ref, o_ref, qkv_ref, p_ref, act_ref, s_ref = refs[9 + n_alias:]
+def position():
+    me = lax.axis_index('sp')
+    y, x, c = me // 4, (me // 2) % 2, me % 2
+    return me, y, x, c, 4 * y + 2 * x + 1 - c, 4 * y + 2 * (1 - x) + c, 4 * (1 - y) + 2 * x + c
+
+
+def peer(d):
+    return lax.rem(lax.axis_index('sp') + d, N_DEV)
+
+
+def enter():
+    barrier = pltpu.get_barrier_semaphore()
+    for d in range(1, N_DEV):
+        pl.semaphore_signal(barrier, inc=1, device_id={'sp': peer(d)}, device_id_type=pl.DeviceIdType.MESH)
+    pl.semaphore_wait(barrier, N_DEV - 1)
+
+
+def remote(src, dst, send_sem, recv_sem, device):
+    return pltpu.make_async_remote_copy(src_ref=src, dst_ref=dst, send_sem=send_sem, recv_sem=recv_sem,
+                                        device_id={'sp': device}, device_id_type=pl.DeviceIdType.MESH)
+
+
+def videos_of(i):
+    return pl.ds(i * NV, NV)
+
+
+class Exchange:
+    def __init__(self, stage, landing, sems):
+        self.stage, self.landing, (self.send, self.recv, self.own) = stage, landing, sems
+
+    def copies(self, i):
+        me, slot = lax.axis_index('sp'), i % 2
+        return [remote(self.stage.at[slot, peer(d)], self.landing(me, i), self.send.at[slot, d], self.recv.at[i, d], peer(d))
+                for d in range(1, N_DEV)]
+
+    def local(self, i):
+        me, slot = lax.axis_index('sp'), i % 2
+        return pltpu.make_async_copy(self.stage.at[slot, me], self.landing(me, i), self.own.at[slot])
+
+    def start(self, i):
+        for copy in self.copies(i):
+            copy.start()
+        self.local(i).start()
+
+    def wait_sent(self, i):
+        for copy in self.copies(i):
+            copy.wait_send()
+        self.local(i).wait()
+
+    def wait_received(self, i):
+        slot = i % 2
+        for d in range(1, N_DEV):
+            remote(self.stage.at[slot, 0], self.landing(peer(N_DEV - d), i), self.send.at[slot, d], self.recv.at[i, d],
+                   peer(d)).wait_recv()
+
+    def free_slot(self, i):
+        @pl.when(i >= 2)
+        def _():
+            self.wait_sent(i - 2)
+
+    def finish(self, n):
+        self.wait_sent(n - 2)
+        self.wait_sent(n - 1)
+
+        def body(i, carry):
+            self.wait_received(i)
+            return carry
+        lax.fori_loop(0, n, body, 0)
+
+
+EXCHANGE_SEMS = [pltpu.SemaphoreType.DMA((2, N_DEV)), pltpu.SemaphoreType.DMA((STEPS, N_DEV)),
+                 pltpu.SemaphoreType.DMA((2,))]
+
+
+def spatial_forward_kernel(x_ref, dy_ref, ln_ref, wqkv_ref, wout_ref, wup_ref, wdown_ref, bias_ref, perm_ref,
+                           mid_ref, dyp_ref, h_ref, o_ref, qkv_ref, p_ref, act_ref, s_ref, stage_ref, *sems):
+    step = pl.program_id(0)
+    exchange = Exchange(stage_ref, lambda src, i: mid_ref.at[src, videos_of(i)], sems)
+
+    @pl.when(step == 0)
+    def _():
+        enter()
+
+    for v in range(NV):
+        moved = dot_nn(perm_ref[...], dy_ref[pl.ds(v * ROWS, ROWS), :]).astype(BF16)
+        for d in range(N_DEV):
+            dyp_ref[d, v] = moved[d * 32:(d + 1) * 32]
     gain1, shift1, gain2, shift2 = gains(ln_ref)
     normed, _ = norm_stats(x_ref[...].astype(F32))
     a_in = (normed * gain1 + shift1).astype(BF16)
@@ -167,13 +251,16 @@
     for c in range(CHUNKS):
         act_ref[:, cut(c)] = gelu_value(dot_nn(m_in, wup_ref[:, cut(c)])).astype(BF16)
     out = (h_ref[...].astype(F32) + dot_nn(act_ref[...], wdown_ref[...])).astype(BF16)
+    exchange.free_slot(step)
     for v in range(NV):
         moved = dot_nn(perm_ref[...], out[v * ROWS:(v + 1) * ROWS]).astype(BF16)
         for d in range(N_DEV):
-            out_ref[d, 0, v] = moved[d * 32:(d + 1) * 32]
-        moved = dot_nn(perm_ref[...], dy_ref[pl.ds(v * ROWS, ROWS), :]).astype(BF16)
-        for d in range(N_DEV):
-            out_ref[d, 1, v] = moved[d * 32:(d + 1) * 32]
+            stage_ref[step % 2, d, v] = moved[d * 32:(d + 1) * 32]
+    exchange.start(step)
+
+    @pl.when(step == STEPS - 1)
+    def _():
+        exchange.finish(STEPS)
 
 
 def add_blocks(sum_ref, first, product):
@@ -220,22 +307,34 @@
         ref[first + r:first + r + 1, :] += g
 
 
-def temporal_kernel(n_sums, *refs):
-    act_in_ref, ln_ref, wqkv_ref, wout_ref, wup_ref, wdown_ref, bias_ref = refs[:7]
-    sums_in = refs[7:7 + n_sums]
-    (out_ref, sum_ref, u_ref, dv_ref, a_ref, qkv_ref, p_ref, o_ref, m_ref, act_ref,
-     dup_ref, do_ref, dqkv_ref, dp_ref, gp_ref, s_ref) = refs[7 + n_sums:]
-
-    @pl.when(pl.program_id(0) == 0)
-    def _():
-        sum_ref[...] = sums_in[0][...] if n_sums else jnp.zeros_like(sum_ref)
+def temporal_kernel(mid_ref, dyp_ref, ln_ref, wqkv_ref, wout_ref, wup_ref, wdown_ref, bias_ref,
+                    back_ref, sum_ref, u_ref, dv_ref, a_ref, qkv_ref, p_ref, o_ref, m_ref, act_ref,
+                    dup_ref, do_ref, dqkv_ref, dp_ref, gp_ref, s_ref, dy_ref, y_stage, dm_stage, *sems):
+    step = pl.program_id(0)
+    me = lax.axis_index('sp')
+    send_y = Exchange(y_stage, lambda src, i: back_ref.at[src, 0, videos_of(i)], sems[0:3])
+    send_dm = Exchange(dm_stage, lambda src, i: back_ref.at[src, 1, videos_of(i)], sems[3:6])
+    dy_send, dy_recv, dy_own = sems[6:]
+
+    def dy_copy(i, d):
+        return remote(dyp_ref.at[peer(d), videos_of(i)], dy_ref.at[me, videos_of(i)], dy_send.at[i, d], dy_recv.at[i, d],
+                      peer(d))
+
+    dy_local = pltpu.make_async_copy(dyp_ref.at[me], dy_ref.at[me], dy_own)
+
+    @pl.when(step == 0)
+    def _():
+        enter()
+        dy_local.start()
+        for i in range(STEPS):
+            for d in range(1, N_DEV):
+                dy_copy(i, d).start()
+        sum_ref[...] = jnp.zeros_like(sum_ref)
 
     gain1, shift1, gain2, shift2 = gains(ln_ref)
     places = [(v, g, s) for v in range(NV) for g in range(2) for s in range(N_DEV)]
     for v, g, s in places:
-        dst = pl.ds(v * ROWS + g * GROUP + s * 16, 16)
-        u_ref[dst, :] = act_in_ref[s, 0, v, pl.ds(g * 16, 16), :]
-        dv_ref[dst, :] = act_in_ref[s, 1, v, pl.ds(g * 16, 16), :]
+        u_ref[pl.ds(v * ROWS + g * GROUP + s * 16, 16), :] = mid_ref[s, v, pl.ds(g * 16, 16), :]
     normed1, _ = norm_stats(u_ref[...].astype(F32))
     a_ref[...] = (normed1 * gain1 + shift1).astype(BF16)
     for c in range(3):
@@ -246,23 +345,39 @@
     h32 = h.astype(F32)
     normed, inv_std = up_forward(h32, gain2, shift2, m_ref, wup_ref, act_ref, gp_ref)
     out = (h32 + dot_nn(act_ref[...], wdown_ref[...])).astype(BF16)
+    send_y.free_slot(step)
     for v, g, s in places:
         src = v * ROWS + g * GROUP + s * 16
-        out_ref[s, 0, v, pl.ds(g * 16, 16), :] = out[src:src + 16]
+        y_stage[step % 2, s, v, pl.ds(g * 16, 16), :] = out[src:src + 16]
+
+    @pl.when(step == 0)
+    def _():
+        dy_local.wait()
+
+    for d in range(1, N_DEV):
+        remote(dyp_ref.at[0, videos_of(step)], dy_ref.at[peer(N_DEV - d), videos_of(step)], dy_send.at[step, d],
+               dy_recv.at[step, d], peer(d)).wait_recv()
+    for v, g, s in places:
+        dv_ref[pl.ds(v * ROWS + g * GROUP + s * 16, 16), :] = dy_ref[s, step * NV + v, pl.ds(g * 16, 16), :]
+    send_y.start(step)
     g_gain2, g_shift2 = tail_backward(dv_ref, o_ref, m_ref, normed, inv_std, gain2, gp_ref, act_ref, dup_ref, do_ref,
                                       wout_ref, wup_ref, wdown_ref, sum_ref)
     attend_back(qkv_ref, p_ref, do_ref, dqkv_ref, dp_ref)
     d_in, g_gain1, g_shift1 = qkv_backward(u_ref[...].astype(F32), a_ref, dv_ref, dqkv_ref, gain1, wqkv_ref, sum_ref)
     add_ln_sums(sum_ref, SUM_ROWS, (g_gain1, g_shift1, g_gain2, g_shift2))
+    send_dm.free_slot(step)
     for v, g, s in places:
         src = v * ROWS + g * GROUP + s * 16
-        out_ref[s, 1, v, pl.ds(g * 16, 16), :] = d_in[src:src + 16]
-
-
-def position():
-    me = lax.axis_index('sp')
-    y, x, c = me // 4, (me // 2) % 2, me % 2
-    return me, y, x, c, 4 * y + 2 * x + 1 - c, 4 * y + 2 * (1 - x) + c, 4 * (1 - y) + 2 * x + c
+        dm_stage[step % 2, s, v, pl.ds(g * 16, 16), :] = d_in[src:src + 16]
+    send_dm.start(step)
+
+    @pl.when(step == STEPS - 1)
+    def _():
+        for i in range(STEPS):
+            for d in range(1, N_DEV):
+                dy_copy(i, d).wait_send()
+        send_y.finish(STEPS)
+        send_dm.finish(STEPS)
 
 
 def span(k, idx, n):
@@ -323,15 +438,6 @@
             w_ref[w_rows, :] += r_ref[r_rows, :]
             return carry
         lax.fori_loop(0, n, body, 0)
-
-
-def enter():
-    me = lax.axis_index('sp')
-    barrier = pltpu.get_barrier_semaphore()
-    for d in range(1, N_DEV):
-        pl.semaphore_signal(barrier, inc=1, device_id={'sp': lax.rem(me + d, N_DEV)},
-                            device_id_type=pl.DeviceIdType.MESH)
-    pl.semaphore_wait(barrier, N_DEV - 1)
 
 
 def ln_copies(ln_ref, sems):
@@ -427,25 +533,33 @@
 
 
 def assemble_kernel(s_ref, t_ref, ln_ref, qkv_ref, out_ref, up_ref, down_ref, gln_ref):
-    block, part_id = pl.program_id(0), pl.program_id(1)
-    moved = jnp.where(block == 0, s_ref[...], t_ref[...])
-
-    @pl.when(part_id < 3)
-    def _():
-        qkv_ref[...] = moved
-
-    @pl.when(part_id == 3)
-    def _():
-        out_ref[...] = moved
-        gln_ref[...] = jnp.where(block == 0, ln_ref[8:12, :], ln_ref[0:4, :])
-
-    @pl.when((part_id >= 4) & (part_id < 8))
-    def _():
-        up_ref[...] = moved
-
-    @pl.when(part_id >= 8)
-    def _():
-        down_ref[...] = moved.T
+    third = pl.program_id(1)
+
+    def place(src_ref, ln_row):
+        @pl.when(third == 0)
+        def _():
+            for c in range(3):
+                qkv_ref[:, pl.ds(c * WIDTH, WIDTH)] = src_ref[pl.ds(c * WIDTH, WIDTH), :]
+            out_ref[...] = src_ref[pl.ds(3 * WIDTH, WIDTH), :]
+            gln_ref[...] = ln_ref[ln_row:ln_row + 4, :]
+
+        @pl.when(third == 1)
+        def _():
+            for c in range(4):
+                up_ref[:, pl.ds(c * WIDTH, WIDTH)] = src_ref[pl.ds(c * WIDTH, WIDTH), :]
+
+        @pl.when(third == 2)
+        def _():
+            for c in range(4):
+                down_ref[pl.ds(c * WIDTH, WIDTH), :] = src_ref[pl.ds(c * WIDTH, WIDTH), :].T
+
+    @pl.when(pl.program_id(0) == 0)
+    def _():
+        place(t_ref, 0)
+
+    @pl.when(pl.program_id(0) == 1)
+    def _():
+        place(s_ref, 8)
 
 
 def full(shape):
@@ -457,19 +571,20 @@
     return [pl.BlockSpec((None,) + s, lambda i: (block, 0, 0), pipeline_mode=pl.Buffered(1)) for s in shapes]
 
 
-def rows_spec(width, first=0):
-    return pl.BlockSpec((STEP_ROWS, width), lambda i: (i + first, 0))
-
-
-def pair_spec():
-    return pl.BlockSpec((N_DEV, 2, NV, 32, WIDTH), lambda i: (0, 0, i, 0, 0))
+def rows_spec(width):
+    return pl.BlockSpec((STEP_ROWS, width), lambda i: (i, 0))
+
+
+def swap_spec():
+    return pl.BlockSpec((N_DEV, NV, 32, WIDTH), lambda i: (0, i, 0, 0))
 
 
 ANY = pl.BlockSpec(memory_space=pl.ANY)
 
 
-def params():
-    return pltpu.CompilerParams(dimension_semantics=("arbitrary",), vmem_limit_bytes=VMEM_LIMIT)
+def params(collective_id):
+    return pltpu.CompilerParams(dimension_semantics=("arbitrary",), vmem_limit_bytes=VMEM_LIMIT,
+                                collective_id=collective_id, has_side_effects=True)
 
 
 def cost(us, mib):
@@ -486,7 +601,7 @@
 
 TOKENS = VIDEOS * ROWS
 PROBS = 6 * GROUP
-EXCHANGE = (N_DEV, 2, HALF, 32, WIDTH)
+SWAP = (N_DEV, VIDEOS, 32, WIDTH)
 ROW_QKV, ROW_OUT, ROW_UP, ROW_DOWN = 0, 3 * WIDTH, 4 * WIDTH, 8 * WIDTH
 SUM_ROWS = 12 * WIDTH
 LAPS = 2
@@ -496,34 +611,30 @@
 T_FINISH = (2, 4, 5, 6)
 
 
-def spatial_forward_call(half, x, dy, weights, bias, perm, saved):
-    first = half * (HALF // NV)
+def spatial_forward_call(x, dy, weights, bias, perm):
     widths = (WIDTH, WIDTH, QKV, PROBS)
-    n_in = 9
     return pl.pallas_call(
-        functools.partial(spatial_forward_kernel, len(saved)), grid=(HALF // NV,), name="spatial_fwd",
-        in_specs=[rows_spec(WIDTH, first)] * 2 + weight_specs(0) + [full((GROUP, 2 * GROUP)), full((ROWS, ROWS))]
-        + [ANY] * len(saved),
-        out_specs=[pair_spec()] + [rows_spec(w, first) for w in widths],
-        out_shape=[sds(EXCHANGE, BF16)] + [sds((TOKENS, w), BF16) for w in widths],
-        scratch_shapes=[vm(HIDDEN), vm(PROBS, F32)],
-        input_output_aliases={n_in + i: 1 + i for i in range(len(saved))},
-        compiler_params=params(), cost_estimate=cost(25, 16),
-    )(x, dy, *weights, bias, perm, *saved)
-
-
-def temporal_call(acts, weights, bias, sums):
-    n_in = 7
+        spatial_forward_kernel, grid=(STEPS,), name="spatial_fwd",
+        in_specs=[rows_spec(WIDTH)] * 2 + weight_specs(0) + [full((GROUP, 2 * GROUP)), full((ROWS, ROWS))],
+        out_specs=[ANY, swap_spec()] + [rows_spec(w) for w in widths],
+        out_shape=[sds(SWAP, BF16)] * 2 + [sds((TOKENS, w), BF16) for w in widths],
+        scratch_shapes=[vm(HIDDEN), vm(PROBS, F32), pltpu.VMEM((2, N_DEV, NV, 32, WIDTH), BF16)] + EXCHANGE_SEMS,
+        compiler_params=params(1), cost_estimate=cost(50, 40),
+    )(x, dy, *weights, bias, perm)
+
+
+def temporal_call(mid, dyp, weights, bias):
     return pl.pallas_call(
-        functools.partial(temporal_kernel, len(sums)), grid=(HALF // NV,), name="temporal",
-        in_specs=[pair_spec()] + weight_specs(1) + [full((GROUP, 2 * GROUP))] + [full((SUM_ROWS + 8, WIDTH))] * len(sums),
-        out_specs=[pair_spec(), full((SUM_ROWS + 8, WIDTH))],
-        out_shape=[sds(EXCHANGE, BF16), sds((SUM_ROWS + 8, WIDTH), F32)],
+        temporal_kernel, grid=(STEPS,), name="temporal",
+        in_specs=[swap_spec(), ANY] + weight_specs(1) + [full((GROUP, 2 * GROUP))],
+        out_specs=[ANY, full((SUM_ROWS + 8, WIDTH))],
+        out_shape=[sds((N_DEV, 2) + SWAP[1:], BF16), sds((SUM_ROWS + 8, WIDTH), F32)],
         scratch_shapes=[vm(w) for w in (WIDTH, WIDTH, WIDTH, QKV, PROBS, WIDTH, WIDTH, HIDDEN, HIDDEN, WIDTH, QKV, PROBS)]
-        + [vm(HIDDEN, F32), vm(PROBS, F32)],
-        input_output_aliases={n_in + i: 1 + i for i in range(len(sums))},
-        compiler_params=params(), cost_estimate=cost(60, 20),
-    )(acts, *weights, bias, *sums)
+        + [vm(HIDDEN, F32), vm(PROBS, F32), pltpu.VMEM(SWAP, BF16)]
+        + [pltpu.VMEM((2, N_DEV, NV, 32, WIDTH), BF16)] * 2 + EXCHANGE_SEMS * 2
+        + [pltpu.SemaphoreType.DMA((STEPS, N_DEV))] * 2 + [pltpu.SemaphoreType.DMA],
+        compiler_params=params(2), cost_estimate=cost(110, 20),
+    )(mid, dyp, *weights, bias)
 
 
 def spatial_backward_call(back, x, saved, weights, perm, sum_t):
@@ -538,25 +649,18 @@
         + [pltpu.VMEM((8, WIDTH), F32), pltpu.VMEM((N_DEV, 16, WIDTH), F32)]
         + [pltpu.SemaphoreType.DMA((2, 6, LAPS, 2))] * 2 + [pltpu.SemaphoreType.REGULAR((3, LAPS, 2))] * 2
         + [pltpu.SemaphoreType.DMA((2, N_DEV)), pltpu.SemaphoreType.DMA((4,))],
-        compiler_params=pltpu.CompilerParams(dimension_semantics=("arbitrary",), vmem_limit_bytes=VMEM_LIMIT,
-                                             collective_id=1, has_side_effects=True),
-        cost_estimate=cost(160, 60),
+        compiler_params=params(3), cost_estimate=cost(160, 60),
     )(back, x, *saved, *weights, perm, sum_t)
 
 
 def assemble_call(sum_s, sum_t, ln_sums):
-    def block(clip):
-        return lambda b, j: (b,) + clip(j)
     grads = [(2, WIDTH, QKV), (2, WIDTH, WIDTH), (2, WIDTH, HIDDEN), (2, HIDDEN, WIDTH), (2, 4, WIDTH)]
-    maps = [lambda j: (0, jnp.minimum(j, 2)), lambda j: (0, 0), lambda j: (0, jnp.clip(j - 4, 0, 3)),
-            lambda j: (jnp.clip(j - 8, 0, 3), 0)]
     return pl.pallas_call(
-        assemble_kernel, grid=(2, 12), name="assemble",
-        in_specs=[pl.BlockSpec((WIDTH, WIDTH), lambda b, j: (jnp.where(b == 0, j, 11), 0)),
-                  pl.BlockSpec((WIDTH, WIDTH), lambda b, j: (jnp.where(b == 0, 0, j), 0)),
+        assemble_kernel, grid=(2, 3), name="assemble",
+        in_specs=[pl.BlockSpec((4 * WIDTH, WIDTH), lambda b, j: (jnp.where(b == 1, j, 0), 0)),
+                  pl.BlockSpec((4 * WIDTH, WIDTH), lambda b, j: (jnp.where(b == 0, j, 2), 0)),
                   pl.BlockSpec((16, WIDTH), lambda b, j: (0, 0))],
-        out_specs=[pl.BlockSpec((None, WIDTH, WIDTH), block(m)) for m in maps]
-        + [pl.BlockSpec((None, 4, WIDTH), lambda b, j: (b, 0, 0))],
+        out_specs=[pl.BlockSpec((None,) + g[1:], lambda b, j: (1 - b, 0, 0)) for g in grads],
         out_shape=[sds(g, F32) for g in grads],
         compiler_params=pltpu.CompilerParams(dimension_semantics=("arbitrary", "arbitrary"), vmem_limit_bytes=VMEM_LIMIT),
         cost_estimate=cost(10, 28),
@@ -576,10 +680,6 @@
     return perm, np.concatenate([bias_s] * 2, 1), np.concatenate([bias_t] * 2, 1)
 
 
-def swap(arr):
-    return lax.all_to_all(arr, 'sp', 0, 0, tiled=True)
-
-
 def device_step(latents, cotangent, ln_params, w_qkv, w_out, w_up, w_down):
     perm, bias_s, bias_t = constants()
     perm = jnp.asarray(perm, BF16)
@@ -588,15 +688,8 @@
     x = latents.reshape(TOKENS, WIDTH)
     dy = cotangent.reshape(TOKENS, WIDTH)
 
-    act_a, *saved = spatial_forward_call(0, x, dy, weights, bias_s, perm, ())
-    act_a = swap(act_a)
-    act_b, *saved = spatial_forward_call(1, x, dy, weights, bias_s, perm, saved)
-    act_b = swap(act_b)
-    back_a, sum_t = temporal_call(act_a, weights, bias_t, ())
-    back_a = swap(back_a)
-    back_b, sum_t = temporal_call(act_b, weights, bias_t, (sum_t,))
-    back_b = swap(back_b)
-    back = jnp.concatenate([back_a, back_b], axis=2)
+    mid, dyp, *saved = spatial_forward_call(x, dy, weights, bias_s, perm)
+    back, sum_t = temporal_call(mid, dyp, weights, bias_t)
     y, dx, sum_t, sum_s, ln_sums = spatial_backward_call(back, x, saved, weights, perm, sum_t)
     g_qkv, g_out, g_up, g_down, g_ln = assemble_call(sum_s, sum_t, ln_sums)
     g_out = g_out.reshape(2, 6, 64, WIDTH)

time: 444 us -> 349 us (0.79); the launches traced: 437 us -> 349 us
  blocking collectives: 79.8 us -> 0 us
  Pallas kernels: 325 us -> 342 us
  waiting for transfers between devices: 14 us -> 0 us
  starting transfers between devices: 7.65 us -> 0 us
    all_to_all x2 -> x0, blocking collectives: 79.8 us -> none  [swap(): return lax.all_to_all(arr, 'sp', 0, 0, tiled=True)]
    pallas_call x5 -> x3, Pallas kernels: 173 us -> 190 us  [the longest x1 123 us: temporal_call(): pl.pallas_call(temporal_kernel, grid=(STEPS,), name='temporal', in_specs=...]
    all_to_all x2 -> x0, waiting for transfers between devices: 14 us -> none  [swap(): return lax.all_to_all(arr, 'sp', 0, 0, tiled=True)]
    all_to_all x2 -> x0, starting transfers between devices: 7.65 us -> none  [swap(): return lax.all_to_all(arr, 'sp', 0, 0, tiled=True)]
  transfers between devices with their start and end apart: 2 -> 0, of which waited for: 1 -> 0; matrix products, arithmetic and copies ran while one was open for 0% -> 0% of each run, Pallas kernels for 17% -> 0%
where the time goes in v2:
time: 349 us
  Pallas kernels  342 us (98%)
  local copies, waits for them, and re-layouts  5.81 us (2%)
    pallas_call x1, Pallas kernels, spatial_backward_call(): pl.pallas_call(spatial_backward_kernel, grid=(VIDEOS // NV,), name='spati...  153 us
    pallas_call x1, Pallas kernels, temporal_call(): pl.pallas_call(temporal_kernel, grid=(STEPS,), name='temporal', in_specs=...  123 us
    pallas_call x1, Pallas kernels, spatial_forward_call(): pl.pallas_call(spatial_forward_kernel, grid=(STEPS,), name='spatial_fwd',...  53.4 us
    pallas_call x1, Pallas kernels, assemble_call(): pl.pallas_call(assemble_kernel, grid=(2, 3), name='assemble', in_specs=[p...  13.7 us

profile of v2, /device:TPU:0, one launch (start us, length us, event | category | flops | bytes accessed | tf_op | source)
XLA Modules:
  0.0 348.7 jit_solution(12171897069729523917)
XLA Ops:
  0.6 53.4 %spatial_fwd.1 = (bf16[8,16,32,384]{3,2,1,0:T(8,128)(2,1)}, bf16[8,16,32,384]{3,2,1,0:T(8,128)(2,1)}, bf16[4096,384]{1,0:T(8,128)(2,1)}, bf16[4096,384]{1,0:T(8,...) custom-call(bf16[4096,384]{1,0:T(8,128)(2,1)} %bitcast.9, bf16[4096,384]{1,0:T(8,128)(2,1)} %bitcast.8, ...), custom_call_target="tpu_custom_call" | custom-call | flops 44999999488 | bytes 41943040 | tf_op jit(solution)/shard_map/spatial_fwd/pallas_call | solution.py:616
  54.0 122.5 %temporal.1 = (bf16[8,2,16,32,384]{4,3,2,1,0:T(8,128)(2,1)}, f32[4616,384]{1,0:T(8,128)}) custom-call(bf16[8,16,32,384]{3,2,1,0:T(8,128)(2,1)} %get-tuple-element.25.mid_ref, bf16[8,16,32,384]{3,2,1,0:T(8,128)(2,1)} %get-tuple-element.26.dyp_ref, bf16[2,4,384]{2,1,0:T(4,128)(2,1)} %refs_6_.1, bf16[2,384,1152]{2,1,0:T(8,128)(2,1)} %refs_7_.1, ...), custom_call_target="tpu_custom_call" | custom-call | flops 99000000512 | bytes 20971520 | tf_op jit(solution)/shard_map/temporal/pallas_call | solution.py:627
  176.6 152.6 %spatial_bwd.1 = (bf16[4096,384]{1,0:T(8,128)(2,1)}, bf16[4096,384]{1,0:T(8,128)(2,1)}, f32[4608,384]{1,0:T(8,128)}, f32[4608,384]{1,0:T(8,128)}, f32[16,384]{1,0:T(8,128)}) custom-call(bf16[8,2,16,32,384]{4,3,2,1,0:T(8,128)(2,1)} %get-tuple-element.27.refs_0_, bf16[4096,384]{1,0:T(8,128)(2,1)} %bitcast.10, bf16[4096,384]{1,0:T(8,128)(2,1)} %get-tuple-element.28.refs_2_, ...), custom_call_target="tpu_custom_call" | custom-call | flops 143999991808 | bytes 62914560 | tf_op jit(solution)/shard_map/spatial_bwd/pallas_call | solution.py:641
  329.2 13.7 %assemble.1 = (f32[2,384,1152]{2,1,0:T(8,128)}, f32[2,384,384]{2,1,0:T(8,128)}, f32[2,384,1536]{2,1,0:T(8,128)}, f32[2,1536,384]{2,1,0:T(8,128)}, f32[2,4,384]{2,1,0:T(4,128)}) custom-call(f32[4608,384]{1,0:T(8,128)} %get-tuple-element.35.s_ref, f32[4608,384]{1,0:T(8,128)} %get-tuple-element.36.t_ref, f32[16,384]{1,0:T(8,128)} %get-tuple-element.37.ln_ref), custom_call_target="tpu_custom_call" | custom-call | flops 8999999488 | bytes 29360128 | tf_op jit(solution)/shard_map/assemble/pallas_call | solution.py:658
  342.8 0.0 copy-start
  342.9 4.1 %copy.19 = bf16[16,8,32,384]{3,2,1,0:T(8,128)(2,1)} copy(bf16[16,8,32,384]{3,2,1,0:T(8,128)(2,1)} %bitcast.7) | data formatting | bytes 6291456
  347.0 0.0 copy-done
  347.0 1.7 copy.20
Async XLA Ops:
  342.8 4.2 %copy-start = (bf16[4096,384]{1,0:T(8,128)(2,1)S(1)}, bf16[4096,384]{1,0:T(8,128)(2,1)}, u32[]{:S(2)}) copy-start(bf16[4096,384]{1,0:T(8,128)(2,1)} %get-tuple-element.34) | copy-start | bytes 9437188

commit v3 on v2

--- a/solution.py
+++ b/solution.py
@@ -381,63 +381,121 @@
 
 
 def span(k, idx, n):
-    return pl.ds(pl.multiple_of(k * LAP_ROWS + idx * BLOCK, 16), n * BLOCK)
+    return pl.ds(pl.multiple_of(k * LAP_ROWS + idx * BLOCK, 8), n * BLOCK)
 
 
 def slot(k, idx, n):
     return pl.ds((k * SLOTS + idx) * BLOCK, n * BLOCK)
 
 
-def reduce_copies(phase, k, w_ref, r_ref, sems):
-    _, y, x, c, partner, xn, yn = position()
-    own0, own1 = c * 8 + x * 2, c * 8 + 4 + y * 2
-    moves = (
-        [((1 - c) * 8, 8, 0, partner)],
-        [(c * 8 + (1 - x) * 2, 2, 8, xn), (c * 8 + 4 + (1 - y) * 2, 2, 10, yn)],
-        [(own0 + 1 - y, 1, 12, yn), (own1 + 1 - x, 1, 13, xn)],
-        [(own0 + y, 1, None, yn), (own1 + x, 1, None, xn)],
-        [(own0, 2, None, xn), (own1, 2, None, yn)],
-        [(c * 8, 8, None, partner)],
-    )[phase]
-    copies = []
-    for j, (idx, n, place, device) in enumerate(moves):
-        src = w_ref.at[span(k, idx, n), :]
-        dst = src if place is None else r_ref.at[slot(k, place, n), :]
-        copies.append(pltpu.make_async_remote_copy(
-            src_ref=src, dst_ref=dst, send_sem=sems.at[0, phase, k, j], recv_sem=sems.at[1, phase, k, j],
-            device_id={'sp': device}, device_id_type=pl.DeviceIdType.MESH))
-    return copies
-
-
-def reduce_peers(phase):
-    _, _, _, _, partner, xn, yn = position()
-    return ([partner], [xn, yn], [yn, xn])[phase]
-
-
-def reduce_start(phase, k, w_ref, r_ref, sems, credits):
-    copies = reduce_copies(phase, k, w_ref, r_ref, sems)
-    for j, copy in enumerate(copies):
-        if phase >= 3:
-            pl.semaphore_wait(credits.at[5 - phase, k, j], 1)
-        copy.start()
-
-
-def reduce_finish(phase, k, w_ref, r_ref, sems, credits):
-    for j, copy in enumerate(reduce_copies(phase, k, w_ref, r_ref, sems)):
-        copy.wait()
-        if phase < 3:
-            pl.semaphore_signal(credits.at[phase, k, j], inc=1, device_id={'sp': reduce_peers(phase)[j]},
-                                device_id_type=pl.DeviceIdType.MESH)
-    _, y, x, c, _, _, _ = position()
-    own0, own1 = c * 8 + x * 2, c * 8 + 4 + y * 2
-    adds = ([(c * 8, 8, 0)], [(own0, 2, 8), (own1, 2, 10)], [(own0 + y, 1, 12), (own1 + x, 1, 13)], (), (), ())[phase]
-    for idx, n, place in adds:
-        def body(i, carry):
-            w_rows = pl.ds(pl.multiple_of(k * LAP_ROWS + (idx + i) * BLOCK, 16), BLOCK)
-            r_rows = pl.ds(pl.multiple_of((k * SLOTS + place + i) * BLOCK, 16), BLOCK)
-            w_ref[w_rows, :] += r_ref[r_rows, :]
-            return carry
-        lax.fori_loop(0, n, body, 0)
+class Reduce:
+    def __init__(self, sum_ref, first_ref, landing_ref, sems, credits, block, out_sems):
+        self.sum, self.first, self.landing = sum_ref, first_ref, landing_ref
+        self.sems, self.credits, self.block, self.out_sems = sems, credits, block, out_sems
+
+    def moves(self, phase):
+        _, y, x, c, partner, xn, yn = position()
+        own0, own1 = c * 8 + x * 2, c * 8 + 4 + y * 2
+        return (
+            [((1 - c) * 8, 8, 0, partner)],
+            [(c * 8 + (1 - x) * 2, 2, 8, xn), (c * 8 + 4 + (1 - y) * 2, 2, 10, yn)],
+            [(own0 + 1 - y, 1, 12, yn), (own1 + 1 - x, 1, 13, xn)],
+            [(own0 + y, 1, None, yn), (own1 + x, 1, None, xn)],
+            [(own0, 2, None, xn), (own1, 2, None, yn)],
+            [(c * 8, 8, None, partner)],
+        )[phase]
+
+    def copies(self, phase, k):
+        source = self.first if phase == 0 else self.sum
+        copies = []
+        for j, (idx, n, place, device) in enumerate(self.moves(phase)):
+            dst = self.sum.at[span(k, idx, n), :] if place is None else self.landing.at[slot(k, place, n), :]
+            copies.append(remote(source.at[span(k, idx, n), :], dst, self.sems.at[0, phase, k, j],
+                                 self.sems.at[1, phase, k, j], device))
+        return copies
+
+    def start(self, phase, k):
+        for j, copy in enumerate(self.copies(phase, k)):
+            if phase >= 3:
+                pl.semaphore_wait(self.credits.at[5 - phase, k, j], 1)
+            copy.start()
+
+    def finish(self, phase, k):
+        for j, copy in enumerate(self.copies(phase, k)):
+            copy.wait()
+            if phase < 3:
+                pl.semaphore_signal(self.credits.at[phase, k, j], inc=1, device_id={'sp': self.moves(phase)[j][3]},
+                                    device_id_type=pl.DeviceIdType.MESH)
+        _, y, x, c, _, _, _ = position()
+        own0, own1 = c * 8 + x * 2, c * 8 + 4 + y * 2
+        adds = ([(c * 8, 8, 0)], [(own0, 2, 8), (own1, 2, 10)], [(own0 + y, 1, 12), (own1 + x, 1, 13)], (), (), ())
+        for idx, n, place in adds[phase]:
+            def body(i, carry):
+                rows = pl.ds(pl.multiple_of((k * SLOTS + place + i) * BLOCK, 8), BLOCK)
+                self.sum[span(k, idx + i, 1), :] += self.landing[rows, :]
+                return carry
+            lax.fori_loop(0, n, body, 0)
+        if phase == 5:
+            for r in self.pieces(k):
+                if r >= 8:
+                    rows = pl.ds(r * WIDTH, WIDTH)
+                    self.sum[rows, :] = self.sum[rows, :].T
+
+    def pieces(self, k):
+        return range(k * LAP_ROWS // WIDTH, (k + 1) * LAP_ROWS // WIDTH)
+
+    def out_copy(self, r, outs):
+        qkv_ref, out_ref, up_ref, down_ref = outs
+        b = self.block
+        if r < 3:
+            dst = qkv_ref.at[b, :, pl.ds(r * WIDTH, WIDTH)]
+        elif r == 3:
+            dst = out_ref.at[b]
+        elif r < 8:
+            dst = up_ref.at[b, :, pl.ds((r - 4) * WIDTH, WIDTH)]
+        else:
+            dst = down_ref.at[b, pl.ds((r - 8) * WIDTH, WIDTH), :]
+        return pltpu.make_async_copy(self.sum.at[pl.ds(r * WIDTH, WIDTH), :], dst, self.out_sems.at[r])
+
+
+def reduce_plan():
+    lasts = (1.4, 4.75, 2.4, 2.4, 4.75, 1.4)
+    free, running, plan, now = [0.0, 0.0], {}, [], 0.0
+
+    def start(lap, phase):
+        link = 0 if phase in (0, 5) else 1
+        free[link] = max(free[link], now) + lasts[phase]
+        running[lap] = (phase, free[link] + 2.5)
+
+    def turn(due):
+        turns = []
+        for lap in sorted(running, key=lambda lap: running[lap][1]):
+            phase, end = running[lap]
+            if end <= due:
+                turns.append((lap, phase))
+        for lap, phase in turns:
+            del running[lap]
+            if phase < 5:
+                start(lap, phase + 1)
+        return turns
+
+    begin = {0: [('t', k) for k in (1, 2, 3, 0)], STEPS: [('s', k) for k in (1, 2, 3)]}
+    for step in range(2 * STEPS):
+        turns = turn(now)
+        fresh = begin.get(step, [])
+        for lap in fresh:
+            start(lap, 0)
+        plan.append((turns, fresh))
+        now += 6.2 if step < STEPS else 4.2
+    start(('s', 0), 0)
+    turns, fresh = [], [('s', 0)]
+    while running:
+        plan.append((turns, fresh))
+        fresh = []
+        now = max(now, min(end for _, end in running.values()))
+        turns = turn(now)
+    plan.append((turns, fresh))
+    return plan
 
 
 def ln_copies(ln_ref, sems):
@@ -450,14 +508,33 @@
 def spatial_backward_kernel(*refs):
     (back_ref, x_ref, h_ref, o_ref, qkv_ref, p_ref,
      ln_ref, wqkv_ref, wout_ref, wup_ref, wdown_ref, perm_ref, gt_ref) = refs[:13]
-    (y_ref, dx_ref, rt_ref, rs_ref, lnsum_ref, dv_ref, a_ref, m_ref, act_ref, dup_ref, do_ref, dqkv_ref, dp_ref, gp_ref,
-     sum_ref, t_ref, rb_s_ref, rb_t_ref, ln_s_ref, ln_all_ref, sems_s, sems_t, credits_s, credits_t,
-     sems_ln, sems_io) = refs[13:]
-    step, last = pl.program_id(0), pl.num_programs(0) - 1
+    (y_ref, dx_ref, gqkv_ref, gout_ref, gup_ref, gdown_ref, gln_ref,
+     dv_ref, a_ref, m_ref, act_ref, dup_ref, do_ref, dqkv_ref, dp_ref, gp_ref, dh_all_ref, do_all_ref,
+     sum_ref, t_ref, land_s_ref, land_t_ref, ln_s_ref, ln_all_ref, sems_s, sems_t, credits_s, credits_t,
+     sems_out_s, sems_out_t, sems_ln, sems_in) = refs[13:]
+    step = pl.program_id(0)
     me = lax.axis_index('sp')
-    load_t = pltpu.make_async_copy(gt_ref.at[pl.ds(0, SUM_ROWS), :], t_ref, sems_io.at[0])
-    load_ln = pltpu.make_async_copy(gt_ref.at[pl.ds(SUM_ROWS, 8), :], ln_all_ref.at[me, pl.ds(0, 8), :], sems_io.at[1])
-    args_t, args_s = (t_ref, rb_t_ref, sems_t, credits_t), (sum_ref, rb_s_ref, sems_s, credits_s)
+    load_t = pltpu.make_async_copy(gt_ref.at[pl.ds(0, SUM_ROWS), :], t_ref, sems_in.at[0])
+    load_ln = pltpu.make_async_copy(gt_ref.at[pl.ds(SUM_ROWS, 8), :], ln_all_ref.at[me, pl.ds(0, 8), :], sems_in.at[1])
+    sums = {'t': Reduce(t_ref, gt_ref, land_t_ref, sems_t, credits_t, 1, sems_out_t),
+            's': Reduce(sum_ref, sum_ref, land_s_ref, sems_s, credits_s, 0, sems_out_s)}
+    outs = (gqkv_ref, gout_ref, gup_ref, gdown_ref)
+    plan = reduce_plan()
+    written = []
+
+    def advance(turns, fresh):
+        for (which, k), phase in turns:
+            sums[which].finish(phase, k)
+        for which, k in fresh:
+            sums[which].start(0, k)
+        for (which, k), phase in turns:
+            if phase < 5:
+                sums[which].start(phase + 1, k)
+        while written:
+            which, k = written.pop()
+            for r in sums[which].pieces(k):
+                sums[which].out_copy(r, outs).start()
+        written.extend(lap for lap, phase in turns if phase == 5)
 
     @pl.when(step == 0)
     def _():
@@ -471,95 +548,61 @@
     def _():
         load_t.wait()
         load_ln.wait()
-        for k in range(LAPS):
-            reduce_start(0, k, *args_t)
-
-    for phase, at in enumerate(T_FINISH):
-        @pl.when(step == at)
-        def _(phase=phase):
-            for k in range(LAPS):
-                reduce_finish(phase, k, *args_t)
-                reduce_start(phase + 1, k, *args_t)
+
+    for at in range(2 * STEPS):
+        if any(plan[at]) or written:
+            @pl.when(step == at)
+            def _(at=at):
+                advance(*plan[at])
 
     gain1, shift1, gain2, shift2 = gains(ln_ref)
-    for v in range(NV):
-        rows = pl.ds(v * ROWS, ROWS)
-        dv_ref[rows, :] = dot_tn(perm_ref[...], back_ref[:, 1, v].reshape(ROWS, WIDTH)).astype(BF16)
-        y_ref[rows, :] = dot_tn(perm_ref[...], back_ref[:, 0, v].reshape(ROWS, WIDTH)).astype(BF16)
-    normed1, _ = norm_stats(x_ref[...].astype(F32))
-    a_ref[...] = (normed1 * gain1 + shift1).astype(BF16)
-    normed, inv_std = up_forward(h_ref[...].astype(F32), gain2, shift2, m_ref, wup_ref, act_ref, gp_ref)
-    g_gain2, g_shift2 = tail_backward(dv_ref, o_ref, m_ref, normed, inv_std, gain2, gp_ref, act_ref, dup_ref, do_ref,
-                                      wout_ref, wup_ref, wdown_ref, sum_ref)
-    attend_back(qkv_ref, p_ref, do_ref, dqkv_ref, dp_ref)
-    d_in, g_gain1, g_shift1 = qkv_backward(x_ref[...].astype(F32), a_ref, dv_ref, dqkv_ref, gain1, wqkv_ref, sum_ref)
-    add_ln_sums(ln_s_ref, 0, (g_gain1, g_shift1, g_gain2, g_shift2))
-    dx_ref[...] = d_in
-
-    @pl.when(step == last)
+
+    @pl.when(step < STEPS)
+    def _():
+        mine = pl.ds(pl.multiple_of(step * STEP_ROWS, STEP_ROWS), STEP_ROWS)
+        for v in range(NV):
+            rows = pl.ds(v * ROWS, ROWS)
+            dv_ref[rows, :] = dot_tn(perm_ref[...], back_ref[:, 1, v].reshape(ROWS, WIDTH)).astype(BF16)
+            y_ref[rows, :] = dot_tn(perm_ref[...], back_ref[:, 0, v].reshape(ROWS, WIDTH)).astype(BF16)
+        normed, inv_std = up_forward(h_ref[...].astype(F32), gain2, shift2, m_ref, wup_ref, act_ref, gp_ref)
+        g_gain2, g_shift2 = tail_backward(dv_ref, o_ref, m_ref, normed, inv_std, gain2, gp_ref, act_ref, dup_ref, do_ref,
+                                          wout_ref, wup_ref, wdown_ref, sum_ref)
+        dh_all_ref[mine, :] = dv_ref[...]
+        do_all_ref[mine, :] = do_ref[...]
+        add_ln_sums(ln_s_ref, 2, (g_gain2, g_shift2))
+
+    @pl.when(step >= STEPS)
+    def _():
+        mine = pl.ds(pl.multiple_of((step - STEPS) * STEP_ROWS, STEP_ROWS), STEP_ROWS)
+        dv_ref[...] = dh_all_ref[mine, :]
+        do_ref[...] = do_all_ref[mine, :]
+        normed1, _ = norm_stats(x_ref[...].astype(F32))
+        a_ref[...] = (normed1 * gain1 + shift1).astype(BF16)
+        attend_back(qkv_ref, p_ref, do_ref, dqkv_ref, dp_ref)
+        d_in, g_gain1, g_shift1 = qkv_backward(x_ref[...].astype(F32), a_ref, dv_ref, dqkv_ref, gain1, wqkv_ref, sum_ref)
+        add_ln_sums(ln_s_ref, 0, (g_gain1, g_shift1))
+        dx_ref[...] = d_in
+
+    @pl.when(step == 2 * STEPS - 1)
     def _():
         ln_all_ref[me, pl.ds(8, 8), :] = ln_s_ref[...]
-        for copy in ln_copies(ln_all_ref, sems_ln):
-            copy.start()
-        for k in range(LAPS):
-            reduce_start(0, k, *args_s)
-        for k in range(LAPS):
-            reduce_finish(4, k, *args_t)
-            reduce_start(5, k, *args_t)
-        for phase in range(5):
-            for k in range(LAPS):
-                reduce_finish(phase, k, *args_s)
-                reduce_start(phase + 1, k, *args_s)
-            if phase == 0:
-                for k in range(LAPS):
-                    reduce_finish(5, k, *args_t)
-                pltpu.make_async_copy(t_ref, rt_ref, sems_io.at[0]).start()
-            if phase == 1:
+        for n, (turns, fresh) in enumerate(plan[2 * STEPS:]):
+            advance(turns, fresh)
+            if n == 0:
+                for copy in ln_copies(ln_all_ref, sems_ln):
+                    copy.start()
+            if n == 3:
                 for copy in ln_copies(ln_all_ref, sems_ln):
                     copy.wait()
                 total = ln_all_ref[0]
                 for d in range(1, N_DEV):
                     total += ln_all_ref[d]
-                lnsum_ref[...] = total
-        outs = []
-        for k in range(LAPS):
-            reduce_finish(5, k, *args_s)
-            lap = pl.ds(k * LAP_ROWS, LAP_ROWS)
-            outs.append(pltpu.make_async_copy(sum_ref.at[lap, :], rs_ref.at[lap, :], sems_io.at[1 + k]))
-            outs[-1].start()
-        pltpu.make_async_copy(t_ref, rt_ref, sems_io.at[0]).wait()
-        for copy in outs:
-            copy.wait()
-
-
-def assemble_kernel(s_ref, t_ref, ln_ref, qkv_ref, out_ref, up_ref, down_ref, gln_ref):
-    third = pl.program_id(1)
-
-    def place(src_ref, ln_row):
-        @pl.when(third == 0)
-        def _():
-            for c in range(3):
-                qkv_ref[:, pl.ds(c * WIDTH, WIDTH)] = src_ref[pl.ds(c * WIDTH, WIDTH), :]
-            out_ref[...] = src_ref[pl.ds(3 * WIDTH, WIDTH), :]
-            gln_ref[...] = ln_ref[ln_row:ln_row + 4, :]
-
-        @pl.when(third == 1)
-        def _():
-            for c in range(4):
-                up_ref[:, pl.ds(c * WIDTH, WIDTH)] = src_ref[pl.ds(c * WIDTH, WIDTH), :]
-
-        @pl.when(third == 2)
-        def _():
-            for c in range(4):
-                down_ref[pl.ds(c * WIDTH, WIDTH), :] = src_ref[pl.ds(c * WIDTH, WIDTH), :].T
-
-    @pl.when(pl.program_id(0) == 0)
-    def _():
-        place(t_ref, 0)
-
-    @pl.when(pl.program_id(0) == 1)
-    def _():
-        place(s_ref, 8)
+                gln_ref[0] = total[8:12]
+                gln_ref[1] = total[0:4]
+        advance((), ())
+        for which in 'ts':
+            for r in range(12):
+                sums[which].out_copy(r, outs).wait()
 
 
 def full(shape):
@@ -604,11 +647,10 @@
 SWAP = (N_DEV, VIDEOS, 32, WIDTH)
 ROW_QKV, ROW_OUT, ROW_UP, ROW_DOWN = 0, 3 * WIDTH, 4 * WIDTH, 8 * WIDTH
 SUM_ROWS = 12 * WIDTH
-LAPS = 2
+LAPS = 4
 LAP_ROWS = SUM_ROWS // LAPS
 BLOCK = LAP_ROWS // 16
 SLOTS = 14
-T_FINISH = (2, 4, 5, 6)
 
 
 def spatial_forward_call(x, dy, weights, bias, perm):
@@ -638,33 +680,27 @@
 
 
 def spatial_backward_call(back, x, saved, weights, perm, sum_t):
+    def early(width):
+        return pl.BlockSpec((STEP_ROWS, width), lambda i: (jnp.minimum(i, STEPS - 1), 0))
+
+    def late(width):
+        return pl.BlockSpec((STEP_ROWS, width), lambda i: (jnp.maximum(i - STEPS, 0), 0))
+
+    grads = [(2, WIDTH, QKV), (2, WIDTH, WIDTH), (2, WIDTH, HIDDEN), (2, HIDDEN, WIDTH)]
     return pl.pallas_call(
-        spatial_backward_kernel, grid=(VIDEOS // NV,), name="spatial_bwd",
-        in_specs=[pl.BlockSpec((N_DEV, 2, NV, 32, WIDTH), lambda i: (0, 0, i, 0, 0))]
-        + [rows_spec(w) for w in (WIDTH, WIDTH, WIDTH, QKV, PROBS)] + weight_specs(0) + [full((ROWS, ROWS)), ANY],
-        out_specs=[rows_spec(WIDTH)] * 2 + [ANY, ANY, full((16, WIDTH))],
-        out_shape=[sds((TOKENS, WIDTH), BF16)] * 2 + [sds((SUM_ROWS, WIDTH), F32)] * 2 + [sds((16, WIDTH), F32)],
+        spatial_backward_kernel, grid=(2 * STEPS,), name="spatial_bwd",
+        in_specs=[pl.BlockSpec((N_DEV, 2, NV, 32, WIDTH), lambda i: (0, 0, jnp.minimum(i, STEPS - 1), 0, 0))]
+        + [late(WIDTH), early(WIDTH), early(WIDTH), late(QKV), late(PROBS)] + weight_specs(0) + [full((ROWS, ROWS)), ANY],
+        out_specs=[early(WIDTH), late(WIDTH)] + [ANY] * 4 + [full((2, 4, WIDTH))],
+        out_shape=[sds((TOKENS, WIDTH), BF16)] * 2 + [sds(g, F32) for g in grads] + [sds((2, 4, WIDTH), F32)],
         scratch_shapes=[vm(w) for w in (WIDTH, WIDTH, WIDTH, HIDDEN, HIDDEN, WIDTH, QKV, PROBS)] + [vm(HIDDEN, F32)]
+        + [pltpu.VMEM((TOKENS, WIDTH), BF16)] * 2
         + [pltpu.VMEM((SUM_ROWS, WIDTH), F32)] * 2 + [pltpu.VMEM((LAPS * SLOTS * BLOCK, WIDTH), F32)] * 2
         + [pltpu.VMEM((8, WIDTH), F32), pltpu.VMEM((N_DEV, 16, WIDTH), F32)]
         + [pltpu.SemaphoreType.DMA((2, 6, LAPS, 2))] * 2 + [pltpu.SemaphoreType.REGULAR((3, LAPS, 2))] * 2
-        + [pltpu.SemaphoreType.DMA((2, N_DEV)), pltpu.SemaphoreType.DMA((4,))],
+        + [pltpu.SemaphoreType.DMA((12,))] * 2 + [pltpu.SemaphoreType.DMA((2, N_DEV)), pltpu.SemaphoreType.DMA((2,))],
         compiler_params=params(3), cost_estimate=cost(160, 60),
     )(back, x, *saved, *weights, perm, sum_t)
-
-
-def assemble_call(sum_s, sum_t, ln_sums):
-    grads = [(2, WIDTH, QKV), (2, WIDTH, WIDTH), (2, WIDTH, HIDDEN), (2, HIDDEN, WIDTH), (2, 4, WIDTH)]
-    return pl.pallas_call(
-        assemble_kernel, grid=(2, 3), name="assemble",
-        in_specs=[pl.BlockSpec((4 * WIDTH, WIDTH), lambda b, j: (jnp.where(b == 1, j, 0), 0)),
-                  pl.BlockSpec((4 * WIDTH, WIDTH), lambda b, j: (jnp.where(b == 0, j, 2), 0)),
-                  pl.BlockSpec((16, WIDTH), lambda b, j: (0, 0))],
-        out_specs=[pl.BlockSpec((None,) + g[1:], lambda b, j: (1 - b, 0, 0)) for g in grads],
-        out_shape=[sds(g, F32) for g in grads],
-        compiler_params=pltpu.CompilerParams(dimension_semantics=("arbitrary", "arbitrary"), vmem_limit_bytes=VMEM_LIMIT),
-        cost_estimate=cost(10, 28),
-    )(sum_s, sum_t, ln_sums)
 
 
 def constants():
@@ -690,8 +726,7 @@
 
     mid, dyp, *saved = spatial_forward_call(x, dy, weights, bias_s, perm)
     back, sum_t = temporal_call(mid, dyp, weights, bias_t)
-    y, dx, sum_t, sum_s, ln_sums = spatial_backward_call(back, x, saved, weights, perm, sum_t)
-    g_qkv, g_out, g_up, g_down, g_ln = assemble_call(sum_s, sum_t, ln_sums)
+    y, dx, g_qkv, g_out, g_up, g_down, g_ln = spatial_backward_call(back, x, saved, weights, perm, sum_t)
     g_out = g_out.reshape(2, 6, 64, WIDTH)
     shape = latents.shape
     return y.reshape(shape), dx.reshape(shape), g_ln, g_qkv, g_out, g_up, g_down

time: 349 us -> 333 us (0.954)
  Pallas kernels: 342 us -> 315 us
  local copies, waits for them, and re-layouts: 5.81 us -> 16.8 us
    pallas_call x2 -> x1, Pallas kernels: 166 us -> 140 us  [spatial_backward_call(): pl.pallas_call(spatial_backward_kernel, grid=(2 * STEPS,), name='spatial_...]
    unnamed x4 -> x23, local copies, waits for them, and re-layouts: 5.81 us -> 16.8 us
where the time goes in v3:
time: 333 us
  Pallas kernels  315 us (95%)
  local copies, waits for them, and re-layouts  16.8 us (5%)
    pallas_call x1, Pallas kernels, spatial_backward_call(): pl.pallas_call(spatial_backward_kernel, grid=(2 * STEPS,), name='spatial_...  140 us
    pallas_call x1, Pallas kernels, temporal_call(): pl.pallas_call(temporal_kernel, grid=(STEPS,), name='temporal', in_specs=...  123 us
    pallas_call x1, Pallas kernels, spatial_forward_call(): pl.pallas_call(spatial_forward_kernel, grid=(STEPS,), name='spatial_fwd',...  53.3 us
    unnamed x23, local copies, waits for them, and re-layouts  16.8 us

profile of v3, /device:TPU:0, one launch (start us, length us, event | category | flops | bytes accessed | tf_op | source)
XLA Modules:
  0.0 333.0 jit_solution(16284619005242269606)
XLA Ops:
  0.6 53.3 %spatial_fwd.1 = (bf16[8,16,32,384]{3,2,1,0:T(8,128)(2,1)}, bf16[8,16,32,384]{3,2,1,0:T(8,128)(2,1)}, bf16[4096,384]{1,0:T(8,128)(2,1)}, bf16[4096,384]{1,0:T(8,...) custom-call(bf16[4096,384]{1,0:T(8,128)(2,1)} %bitcast.14, bf16[4096,384]{1,0:T(8,128)(2,1)} %bitcast.13, ...), custom_call_target="tpu_custom_call" | custom-call | flops 44999999488 | bytes 41943040 | tf_op jit(solution)/shard_map/spatial_fwd/pallas_call | solution.py:658
  54.0 122.5 %temporal.1 = (bf16[8,2,16,32,384]{4,3,2,1,0:T(8,128)(2,1)}, f32[4616,384]{1,0:T(8,128)}) custom-call(bf16[8,16,32,384]{3,2,1,0:T(8,128)(2,1)} %get-tuple-element.22.mid_ref, bf16[8,16,32,384]{3,2,1,0:T(8,128)(2,1)} %get-tuple-element.23.dyp_ref, bf16[2,4,384]{2,1,0:T(4,128)(2,1)} %refs_6_.1, bf16[2,384,1152]{2,1,0:T(8,128)(2,1)} %refs_7_.1, ...), custom_call_target="tpu_custom_call" | custom-call | flops 99000000512 | bytes 20971520 | tf_op jit(solution)/shard_map/temporal/pallas_call | solution.py:669
  176.5 139.6 %spatial_bwd.1 = (bf16[4096,384]{1,0:T(8,128)(2,1)}, bf16[4096,384]{1,0:T(8,128)(2,1)}, f32[2,384,1152]{2,1,0:T(8,128)}, f32[2,384,384]{2,1,0:T(8,128)}, f32[2,3...) custom-call(bf16[8,2,16,32,384]{4,3,2,1,0:T(8,128)(2,1)} %get-tuple-element.24.refs_0_, ...), custom_call_target="tpu_custom_call" | custom-call | flops 143999991808 | bytes 62914560 | tf_op jit(solution)/shard_map/spatial_bwd/pallas_call | solution.py:690
  316.1 0.0 copy-start.1
  316.1 4.1 %copy.24 = bf16[16,8,32,384]{3,2,1,0:T(8,128)(2,1)} copy(bf16[16,8,32,384]{3,2,1,0:T(8,128)(2,1)} %bitcast.11) | data formatting | bytes 6291456
  320.3 0.0 copy-done.1
  320.3 0.0 copy-start.3
  320.3 0.0 copy-start
  320.3 1.7 copy.25
  322.0 0.0 copy-done.3
  322.0 0.0 slice-start.2
  322.0 0.6 copy.26
  322.6 0.9 copy-done
  323.4 0.0 copy-start.2
  323.4 0.0 slice-start.3
  323.4 1.8 copy.27
  325.2 1.0 copy-done.2
  326.2 1.0 copy.28
  327.3 0.0 slice-done.2
  327.3 0.0 slice-done.3
  327.3 2.4 copy.29
  329.7 0.8 slice-done
  330.5 0.3 slice-done.1
  330.8 2.2 copy.30
  (4 shorter events, 0.0 us)
Async XLA Ops:
  316.1 4.2 %copy-start.1 = (bf16[4096,384]{1,0:T(8,128)(2,1)S(1)}, bf16[4096,384]{1,0:T(8,128)(2,1)}, u32[]{:S(2)}) copy-start(bf16[4096,384]{1,0:T(8,128)(2,1)} %get-tuple-element.31) | copy-start | bytes 9437188
  320.3 1.7 copy-start.3
  320.3 3.2 copy-start
  322.0 5.3 %slice-start.2 = ((s8[4718592]{0:T(1024)(128)(4,1)}), s8[4194304]{0:T(1024)(128)(4,1)S(1)}, s32[]{:S(2)}) async-start(s8[4718592]{0:T(1024)(128)(4,1)} %bitcast.8), calls=%async_computation.2 | async-start | bytes 8388608
  323.4 2.8 copy-start.2
  323.4 3.8 %slice-start.3 = ((s8[4718592]{0:T(1024)(128)(4,1)}), s8[524288]{0:T(1024)(128)(4,1)S(1)}, s32[]{:S(2)}) async-start(s8[4718592]{0:T(1024)(128)(4,1)} %bitcast.8), calls=%async_computation.3 | async-start | bytes 1048576
  326.2 4.3 %slice-start = ((s8[4718592]{0:T(1024)(128)(4,1)}), s8[4194304]{0:T(1024)(128)(4,1)S(1)}, s32[]{:S(2)}) async-start(s8[4718592]{0:T(1024)(128)(4,1)} %bitcast.6), calls=%async_computation | async-start | bytes 8388608
  327.3 3.5 %slice-start.1 = ((s8[4718592]{0:T(1024)(128)(4,1)}), s8[524288]{0:T(1024)(128)(4,1)S(1)}, s32[]{:S(2)}) async-start(s8[4718592]{0:T(1024)(128)(4,1)} %bitcast.6), calls=%async_computation.1 | async-start | bytes 1048576

commit v4 on v3

--- a/solution.py
+++ b/solution.py
@@ -23,6 +23,7 @@
 SCALE = 0.125
 LOG2E = 1.4426950408889634
 STEPS = VIDEOS // NV
+EARLY = 3
 GELU_C = 0.7978845608028654
 GELU_C3 = GELU_C * 0.044715
 VMEM_LIMIT = 62 * 1024 * 1024
@@ -59,8 +60,8 @@
     x2 = x * x
     t = jnp.tanh(x * (GELU_C + GELU_C3 * x2))
     half = 0.5 + 0.5 * t
-    slope = half + (x * (0.5 - 0.5 * (t * t))) * (GELU_C + (3.0 * GELU_C3) * x2)
-    return x * half, slope
+    act = x * half
+    return act, half + (act * (1.0 - t)) * (GELU_C + (3.0 * GELU_C3) * x2)
 
 
 def gelu_value(x):
@@ -226,9 +227,11 @@
 
 
 def spatial_forward_kernel(x_ref, dy_ref, ln_ref, wqkv_ref, wout_ref, wup_ref, wdown_ref, bias_ref, perm_ref,
-                           mid_ref, dyp_ref, h_ref, o_ref, qkv_ref, p_ref, act_ref, s_ref, stage_ref, *sems):
+                           mid_ref, dy_early_ref, dyp_ref, h_ref, o_ref, qkv_ref, p_ref, act_ref, s_ref,
+                           stage_ref, dy_stage_ref, *sems):
     step = pl.program_id(0)
-    exchange = Exchange(stage_ref, lambda src, i: mid_ref.at[src, videos_of(i)], sems)
+    exchange = Exchange(stage_ref, lambda src, i: mid_ref.at[src, videos_of(i)], sems[0:3])
+    exchange_dy = Exchange(dy_stage_ref, lambda src, i: dy_early_ref.at[src, videos_of(i)], sems[3:6])
 
     @pl.when(step == 0)
     def _():
@@ -238,12 +241,23 @@
         moved = dot_nn(perm_ref[...], dy_ref[pl.ds(v * ROWS, ROWS), :]).astype(BF16)
         for d in range(N_DEV):
             dyp_ref[d, v] = moved[d * 32:(d + 1) * 32]
+
+    @pl.when(step < EARLY)
+    def _():
+        exchange_dy.free_slot(step)
+        dy_stage_ref[step % 2] = dyp_ref[...]
+
     gain1, shift1, gain2, shift2 = gains(ln_ref)
     normed, _ = norm_stats(x_ref[...].astype(F32))
     a_in = (normed * gain1 + shift1).astype(BF16)
     for c in range(3):
         cols = pl.ds(c * WIDTH, WIDTH)
         qkv_ref[:, cols] = dot_nn(a_in, wqkv_ref[:, cols]).astype(BF16)
+
+    @pl.when(step < EARLY)
+    def _():
+        exchange_dy.start(step)
+
     attend(qkv_ref, bias_ref, p_ref, o_ref, s_ref)
     h_ref[...] = (x_ref[...].astype(F32) + dot_nn(o_ref[...], wout_ref[...])).astype(BF16)
     normed, _ = norm_stats(h_ref[...].astype(F32))
@@ -260,6 +274,7 @@
 
     @pl.when(step == STEPS - 1)
     def _():
+        exchange_dy.finish(EARLY)
         exchange.finish(STEPS)
 
 
@@ -307,7 +322,7 @@
         ref[first + r:first + r + 1, :] += g
 
 
-def temporal_kernel(mid_ref, dyp_ref, ln_ref, wqkv_ref, wout_ref, wup_ref, wdown_ref, bias_ref,
+def temporal_kernel(mid_ref, dy_early_ref, dyp_ref, ln_ref, wqkv_ref, wout_ref, wup_ref, wdown_ref, bias_ref,
                     back_ref, sum_ref, u_ref, dv_ref, a_ref, qkv_ref, p_ref, o_ref, m_ref, act_ref,
                     dup_ref, do_ref, dqkv_ref, dp_ref, gp_ref, s_ref, dy_ref, y_stage, dm_stage, *sems):
     step = pl.program_id(0)
@@ -320,13 +335,16 @@
         return remote(dyp_ref.at[peer(d), videos_of(i)], dy_ref.at[me, videos_of(i)], dy_send.at[i, d], dy_recv.at[i, d],
                       peer(d))
 
-    dy_local = pltpu.make_async_copy(dyp_ref.at[me], dy_ref.at[me], dy_own)
+    late = pl.ds(EARLY * NV, VIDEOS - EARLY * NV)
+    dy_local = pltpu.make_async_copy(dyp_ref.at[me, late], dy_ref.at[me, late], dy_own.at[0])
+    dy_early = pltpu.make_async_copy(dy_early_ref, dy_ref.at[:, pl.ds(0, EARLY * NV)], dy_own.at[1])
 
     @pl.when(step == 0)
     def _():
         enter()
+        dy_early.start()
         dy_local.start()
-        for i in range(STEPS):
+        for i in range(EARLY, STEPS):
             for d in range(1, N_DEV):
                 dy_copy(i, d).start()
         sum_ref[...] = jnp.zeros_like(sum_ref)
@@ -352,11 +370,15 @@
 
     @pl.when(step == 0)
     def _():
+        dy_early.wait()
         dy_local.wait()
 
-    for d in range(1, N_DEV):
-        remote(dyp_ref.at[0, videos_of(step)], dy_ref.at[peer(N_DEV - d), videos_of(step)], dy_send.at[step, d],
-               dy_recv.at[step, d], peer(d)).wait_recv()
+    @pl.when(step >= EARLY)
+    def _():
+        for d in range(1, N_DEV):
+            remote(dyp_ref.at[0, videos_of(step)], dy_ref.at[peer(N_DEV - d), videos_of(step)], dy_send.at[step, d],
+                   dy_recv.at[step, d], peer(d)).wait_recv()
+
     for v, g, s in places:
         dv_ref[pl.ds(v * ROWS + g * GROUP + s * 16, 16), :] = dy_ref[s, step * NV + v, pl.ds(g * 16, 16), :]
     send_y.start(step)
@@ -373,7 +395,7 @@
 
     @pl.when(step == STEPS - 1)
     def _():
-        for i in range(STEPS):
+        for i in range(EARLY, STEPS):
             for d in range(1, N_DEV):
                 dy_copy(i, d).wait_send()
         send_y.finish(STEPS)
@@ -465,36 +487,35 @@
     def start(lap, phase):
         link = 0 if phase in (0, 5) else 1
         free[link] = max(free[link], now) + lasts[phase]
-        running[lap] = (phase, free[link] + 2.5)
+        running[lap] = (phase, free[link] + 2.0)
 
     def turn(due):
-        turns = []
-        for lap in sorted(running, key=lambda lap: running[lap][1]):
-            phase, end = running[lap]
-            if end <= due:
-                turns.append((lap, phase))
+        nonlocal now
+        turns = [(lap, phase) for lap, (phase, end) in sorted(running.items(), key=lambda item: item[1][1]) if end <= due]
         for lap, phase in turns:
-            del running[lap]
+            now = max(now, running.pop(lap)[1])
             if phase < 5:
                 start(lap, phase + 1)
         return turns
 
-    begin = {0: [('t', k) for k in (1, 2, 3, 0)], STEPS: [('s', k) for k in (1, 2, 3)]}
+    def begin(laps):
+        for lap in laps:
+            start(lap, 0)
+        return [], laps
+
     for step in range(2 * STEPS):
-        turns = turn(now)
-        fresh = begin.get(step, [])
-        for lap in fresh:
-            start(lap, 0)
-        plan.append((turns, fresh))
-        now += 6.2 if step < STEPS else 4.2
-    start(('s', 0), 0)
-    turns, fresh = [], [('s', 0)]
+        turns = []
+        if step == STEPS:
+            turns.append(begin([('s', 1), ('s', 2), ('s', 3)]))
+        if step == 0:
+            turns.append(begin([('t', 1), ('t', 2), ('t', 3), ('t', 0)]))
+        turns.append((turn(now), []))
+        plan.append([t for t in turns if any(t)])
+        now += 6.0 if step < STEPS else 4.3
+    turns = [begin([('s', 0)])]
     while running:
-        plan.append((turns, fresh))
-        fresh = []
-        now = max(now, min(end for _, end in running.values()))
-        turns = turn(now)
-    plan.append((turns, fresh))
+        turns.append((turn(min(end for _, end in running.values())), []))
+    plan.append(turns)
     return plan
 
 
@@ -541,19 +562,20 @@
         enter()
         load_t.start()
         load_ln.start()
+        advance(*plan[0][0])
         sum_ref[...] = jnp.zeros_like(sum_ref)
         ln_s_ref[...] = jnp.zeros_like(ln_s_ref)
-
-    @pl.when(step == 1)
-    def _():
         load_t.wait()
         load_ln.wait()
-
-    for at in range(2 * STEPS):
-        if any(plan[at]) or written:
+        for turns in plan[0][1:]:
+            advance(*turns)
+
+    for at in range(1, 2 * STEPS):
+        if plan[at]:
             @pl.when(step == at)
             def _(at=at):
-                advance(*plan[at])
+                for turns in plan[at]:
+                    advance(*turns)
 
     gain1, shift1, gain2, shift2 = gains(ln_ref)
 
@@ -586,7 +608,7 @@
     @pl.when(step == 2 * STEPS - 1)
     def _():
         ln_all_ref[me, pl.ds(8, 8), :] = ln_s_ref[...]
-        for n, (turns, fresh) in enumerate(plan[2 * STEPS:]):
+        for n, (turns, fresh) in enumerate(plan[2 * STEPS]):
             advance(turns, fresh)
             if n == 0:
                 for copy in ln_copies(ln_all_ref, sems_ln):
@@ -645,6 +667,7 @@
 TOKENS = VIDEOS * ROWS
 PROBS = 6 * GROUP
 SWAP = (N_DEV, VIDEOS, 32, WIDTH)
+SWAP_EARLY = (N_DEV, EARLY * NV, 32, WIDTH)
 ROW_QKV, ROW_OUT, ROW_UP, ROW_DOWN = 0, 3 * WIDTH, 4 * WIDTH, 8 * WIDTH
 SUM_ROWS = 12 * WIDTH
 LAPS = 4
@@ -658,25 +681,26 @@
     return pl.pallas_call(
         spatial_forward_kernel, grid=(STEPS,), name="spatial_fwd",
         in_specs=[rows_spec(WIDTH)] * 2 + weight_specs(0) + [full((GROUP, 2 * GROUP)), full((ROWS, ROWS))],
-        out_specs=[ANY, swap_spec()] + [rows_spec(w) for w in widths],
-        out_shape=[sds(SWAP, BF16)] * 2 + [sds((TOKENS, w), BF16) for w in widths],
-        scratch_shapes=[vm(HIDDEN), vm(PROBS, F32), pltpu.VMEM((2, N_DEV, NV, 32, WIDTH), BF16)] + EXCHANGE_SEMS,
+        out_specs=[ANY, ANY, swap_spec()] + [rows_spec(w) for w in widths],
+        out_shape=[sds(SWAP, BF16), sds(SWAP_EARLY, BF16), sds(SWAP, BF16)] + [sds((TOKENS, w), BF16) for w in widths],
+        scratch_shapes=[vm(HIDDEN), vm(PROBS, F32)] + [pltpu.VMEM((2, N_DEV, NV, 32, WIDTH), BF16)] * 2
+        + EXCHANGE_SEMS * 2,
         compiler_params=params(1), cost_estimate=cost(50, 40),
     )(x, dy, *weights, bias, perm)
 
 
-def temporal_call(mid, dyp, weights, bias):
+def temporal_call(mid, dy_early, dyp, weights, bias):
     return pl.pallas_call(
         temporal_kernel, grid=(STEPS,), name="temporal",
-        in_specs=[swap_spec(), ANY] + weight_specs(1) + [full((GROUP, 2 * GROUP))],
+        in_specs=[swap_spec(), ANY, ANY] + weight_specs(1) + [full((GROUP, 2 * GROUP))],
         out_specs=[ANY, full((SUM_ROWS + 8, WIDTH))],
         out_shape=[sds((N_DEV, 2) + SWAP[1:], BF16), sds((SUM_ROWS + 8, WIDTH), F32)],
         scratch_shapes=[vm(w) for w in (WIDTH, WIDTH, WIDTH, QKV, PROBS, WIDTH, WIDTH, HIDDEN, HIDDEN, WIDTH, QKV, PROBS)]
         + [vm(HIDDEN, F32), vm(PROBS, F32), pltpu.VMEM(SWAP, BF16)]
         + [pltpu.VMEM((2, N_DEV, NV, 32, WIDTH), BF16)] * 2 + EXCHANGE_SEMS * 2
-        + [pltpu.SemaphoreType.DMA((STEPS, N_DEV))] * 2 + [pltpu.SemaphoreType.DMA],
+        + [pltpu.SemaphoreType.DMA((STEPS, N_DEV))] * 2 + [pltpu.SemaphoreType.DMA((2,))],
         compiler_params=params(2), cost_estimate=cost(110, 20),
-    )(mid, dyp, *weights, bias)
+    )(mid, dy_early, dyp, *weights, bias)
 
 
 def spatial_backward_call(back, x, saved, weights, perm, sum_t):
@@ -724,8 +748,8 @@
     x = latents.reshape(TOKENS, WIDTH)
     dy = cotangent.reshape(TOKENS, WIDTH)
 
-    mid, dyp, *saved = spatial_forward_call(x, dy, weights, bias_s, perm)
-    back, sum_t = temporal_call(mid, dyp, weights, bias_t)
+    mid, dy_early, dyp, *saved = spatial_forward_call(x, dy, weights, bias_s, perm)
+    back, sum_t = temporal_call(mid, dy_early, dyp, weights, bias_t)
     y, dx, g_qkv, g_out, g_up, g_down, g_ln = spatial_backward_call(back, x, saved, weights, perm, sum_t)
     g_out = g_out.reshape(2, 6, 64, WIDTH)
     shape = latents.shape

time: 333 us -> 334 us (level)
    pallas_call x1, Pallas kernels: 123 us -> 114 us  [temporal_call(): pl.pallas_call(temporal_kernel, grid=(STEPS,), name='temporal', in_specs=...]
    pallas_call x1, Pallas kernels: 53.3 us -> 58.8 us  [spatial_forward_call(): pl.pallas_call(spatial_forward_kernel, grid=(STEPS,), name='spatial_fwd',...]
    pallas_call x1, Pallas kernels: 140 us -> 144 us  [spatial_backward_call(): pl.pallas_call(spatial_backward_kernel, grid=(2 * STEPS,), name='spatial_...]
where the time goes in v4:
time: 334 us
  Pallas kernels  317 us (95%)
  local copies, waits for them, and re-layouts  16.8 us (5%)
    pallas_call x1, Pallas kernels, spatial_backward_call(): pl.pallas_call(spatial_backward_kernel, grid=(2 * STEPS,), name='spatial_...  144 us
    pallas_call x1, Pallas kernels, temporal_call(): pl.pallas_call(temporal_kernel, grid=(STEPS,), name='temporal', in_specs=...  114 us
    pallas_call x1, Pallas kernels, spatial_forward_call(): pl.pallas_call(spatial_forward_kernel, grid=(STEPS,), name='spatial_fwd',...  58.8 us
    unnamed x23, local copies, waits for them, and re-layouts  16.8 us

profile of v4, /device:TPU:0, one launch (start us, length us, event | category | flops | bytes accessed | tf_op | source)
XLA Modules:
  0.0 334.3 jit_solution(6658754804120414385)
XLA Ops:
  0.6 58.8 %spatial_fwd.1 = (bf16[8,16,32,384]{3,2,1,0:T(8,128)(2,1)}, bf16[8,6,32,384]{3,2,1,0:T(8,128)(2,1)}, bf16[8,16,32,384]{3,2,1,0:T(8,128)(2,1)}, bf16[4096,384]{1,...) custom-call(bf16[4096,384]{1,0:T(8,128)(2,1)} %bitcast.14, ...), custom_call_target="tpu_custom_call" | custom-call | flops 44999999488 | bytes 41943040 | tf_op jit(solution)/shard_map/spatial_fwd/pallas_call | solution.py:681
  59.4 113.8 %temporal.1 = (bf16[8,2,16,32,384]{4,3,2,1,0:T(8,128)(2,1)}, f32[4616,384]{1,0:T(8,128)}) custom-call(bf16[8,16,32,384]{3,2,1,0:T(8,128)(2,1)} %get-tuple-element.23.mid_ref, bf16[8,6,32,384]{3,2,1,0:T(8,128)(2,1)} %get-tuple-element.24.dy_early_ref, bf16[8,16,32,384]{3,2,1,0:T(8,128)(2,1)} %get-tuple-element.25.dyp_ref, bf16[2,4,384]{2,1,0:T(4,128)(2,1)} %refs_6_.1, ...), custom_call_target="tpu_custom_call" | custom-call | flops 99000000512 | bytes 20971520 | tf_op jit(solution)/shard_map/temporal/pallas_call | solution.py:693
  173.2 144.2 %spatial_bwd.1 = (bf16[4096,384]{1,0:T(8,128)(2,1)}, bf16[4096,384]{1,0:T(8,128)(2,1)}, f32[2,384,1152]{2,1,0:T(8,128)}, f32[2,384,384]{2,1,0:T(8,128)}, f32[2,3...) custom-call(bf16[8,2,16,32,384]{4,3,2,1,0:T(8,128)(2,1)} %get-tuple-element.26.refs_0_, ...), custom_call_target="tpu_custom_call" | custom-call | flops 143999991808 | bytes 62914560 | tf_op jit(solution)/shard_map/spatial_bwd/pallas_call | solution.py:714
  317.4 0.0 copy-start.1
  317.4 4.1 %copy.24 = bf16[16,8,32,384]{3,2,1,0:T(8,128)(2,1)} copy(bf16[16,8,32,384]{3,2,1,0:T(8,128)(2,1)} %bitcast.11) | data formatting | bytes 6291456
  321.6 0.0 copy-done.1
  321.6 0.0 copy-start.3
  321.6 0.0 copy-start
  321.6 1.7 copy.25
  323.2 0.0 copy-done.3
  323.2 0.0 slice-start.2
  323.3 0.6 copy.26
  323.9 0.9 copy-done
  324.7 0.0 copy-start.2
  324.7 0.0 slice-start.3
  324.7 1.8 copy.27
  326.5 1.0 copy-done.2
  327.5 1.0 copy.28
  328.6 0.0 slice-done.2
  328.6 0.0 slice-done.3
  328.6 2.4 copy.29
  331.0 0.8 slice-done
  331.8 0.3 slice-done.1
  332.1 2.2 copy.30
  (4 shorter events, 0.0 us)
Async XLA Ops:
  317.4 4.2 %copy-start.1 = (bf16[4096,384]{1,0:T(8,128)(2,1)S(1)}, bf16[4096,384]{1,0:T(8,128)(2,1)}, u32[]{:S(2)}) copy-start(bf16[4096,384]{1,0:T(8,128)(2,1)} %get-tuple-element.33) | copy-start | bytes 9437188
  321.6 1.7 copy-start.3
  321.6 3.2 copy-start
  323.2 5.3 %slice-start.2 = ((s8[4718592]{0:T(1024)(128)(4,1)}), s8[4194304]{0:T(1024)(128)(4,1)S(1)}, s32[]{:S(2)}) async-start(s8[4718592]{0:T(1024)(128)(4,1)} %bitcast.8), calls=%async_computation.2 | async-start | bytes 8388608
  324.7 2.8 copy-start.2
  324.7 3.8 %slice-start.3 = ((s8[4718592]{0:T(1024)(128)(4,1)}), s8[524288]{0:T(1024)(128)(4,1)S(1)}, s32[]{:S(2)}) async-start(s8[4718592]{0:T(1024)(128)(4,1)} %bitcast.8), calls=%async_computation.3 | async-start | bytes 1048576
  327.5 4.3 %slice-start = ((s8[4718592]{0:T(1024)(128)(4,1)}), s8[4194304]{0:T(1024)(128)(4,1)S(1)}, s32[]{:S(2)}) async-start(s8[4718592]{0:T(1024)(128)(4,1)} %bitcast.6), calls=%async_computation | async-start | bytes 8388608
  328.6 3.5 %slice-start.1 = ((s8[4718592]{0:T(1024)(128)(4,1)}), s8[524288]{0:T(1024)(128)(4,1)S(1)}, s32[]{:S(2)}) async-start(s8[4718592]{0:T(1024)(128)(4,1)} %bitcast.6), calls=%async_computation.1 | async-start | bytes 1048576

commit v5 on v3

--- a/solution.py
+++ b/solution.py
@@ -1,4 +1,4 @@
-import functools
+import itertools
 
 import jax
 import jax.numpy as jnp
@@ -55,12 +55,9 @@
     return d_in, d_gain, d_shift
 
 
-def gelu_parts(x):
-    x2 = x * x
-    t = jnp.tanh(x * (GELU_C + GELU_C3 * x2))
+def gelu_slope(x, t):
     half = 0.5 + 0.5 * t
-    slope = half + (x * (0.5 - 0.5 * (t * t))) * (GELU_C + (3.0 * GELU_C3) * x2)
-    return x * half, slope
+    return half + ((x * half) * (1.0 - t)) * (GELU_C + (3.0 * GELU_C3) * (x * x))
 
 
 def gelu_value(x):
@@ -154,11 +151,19 @@
 def position():
     me = lax.axis_index('sp')
     y, x, c = me // 4, (me // 2) % 2, me % 2
-    return me, y, x, c, 4 * y + 2 * x + 1 - c, 4 * y + 2 * (1 - x) + c, 4 * (1 - y) + 2 * x + c
+    return me, y, x, c, me + 1 - 2 * c, me + 2 - 4 * x, me + 4 - 8 * y
+
+
+def flip(bit, by):
+    return bit + by - 2 * bit * by
 
 
 def peer(d):
-    return lax.rem(lax.axis_index('sp') + d, N_DEV)
+    _, y, x, c, _, _, _ = position()
+    return 4 * flip(y, d // 4) + 2 * flip(x, (d // 2) % 2) + flip(c, d % 2)
+
+
+ORDER = (*range(2, N_DEV), 1)
 
 
 def enter():
@@ -178,42 +183,47 @@
 
 
 class Exchange:
-    def __init__(self, stage, landing, sems):
+    def __init__(self, stage, landing, sems, local=True):
         self.stage, self.landing, (self.send, self.recv, self.own) = stage, landing, sems
+        self.slots, self.has_local = stage.shape[0], local
 
     def copies(self, i):
-        me, slot = lax.axis_index('sp'), i % 2
+        me, slot = lax.axis_index('sp'), lax.rem(i, self.slots)
         return [remote(self.stage.at[slot, peer(d)], self.landing(me, i), self.send.at[slot, d], self.recv.at[i, d], peer(d))
-                for d in range(1, N_DEV)]
+                for d in ORDER]
 
     def local(self, i):
-        me, slot = lax.axis_index('sp'), i % 2
+        me, slot = lax.axis_index('sp'), lax.rem(i, self.slots)
         return pltpu.make_async_copy(self.stage.at[slot, me], self.landing(me, i), self.own.at[slot])
 
     def start(self, i):
         for copy in self.copies(i):
             copy.start()
-        self.local(i).start()
+        if self.has_local:
+            self.local(i).start()
 
     def wait_sent(self, i):
         for copy in self.copies(i):
             copy.wait_send()
-        self.local(i).wait()
+        if self.has_local:
+            self.local(i).wait()
 
     def wait_received(self, i):
-        slot = i % 2
         for d in range(1, N_DEV):
-            remote(self.stage.at[slot, 0], self.landing(peer(N_DEV - d), i), self.send.at[slot, d], self.recv.at[i, d],
+            remote(self.stage.at[0, 0], self.landing(peer(d), i), self.send.at[0, d], self.recv.at[i, d],
                    peer(d)).wait_recv()
 
     def free_slot(self, i):
-        @pl.when(i >= 2)
+        @pl.when(i >= self.slots)
         def _():
-            self.wait_sent(i - 2)
+            self.wait_sent(i - self.slots)
+
+    def finish_sends(self, n):
+        for j in range(self.slots):
+            self.wait_sent(jnp.int32(n - self.slots + j))
 
     def finish(self, n):
-        self.wait_sent(n - 2)
-        self.wait_sent(n - 1)
+        self.finish_sends(n)
 
         def body(i, carry):
             self.wait_received(i)
@@ -221,23 +231,21 @@
         lax.fori_loop(0, n, body, 0)
 
 
-EXCHANGE_SEMS = [pltpu.SemaphoreType.DMA((2, N_DEV)), pltpu.SemaphoreType.DMA((STEPS, N_DEV)),
-                 pltpu.SemaphoreType.DMA((2,))]
-
-
-def spatial_forward_kernel(x_ref, dy_ref, ln_ref, wqkv_ref, wout_ref, wup_ref, wdown_ref, bias_ref, perm_ref,
-                           mid_ref, dyp_ref, h_ref, o_ref, qkv_ref, p_ref, act_ref, s_ref, stage_ref, *sems):
-    step = pl.program_id(0)
-    exchange = Exchange(stage_ref, lambda src, i: mid_ref.at[src, videos_of(i)], sems)
-
-    @pl.when(step == 0)
-    def _():
-        enter()
-
+def exchange_sems(slots):
+    return [pltpu.SemaphoreType.DMA((slots, N_DEV)), pltpu.SemaphoreType.DMA((STEPS, N_DEV)),
+            pltpu.SemaphoreType.DMA((slots,))]
+
+
+def spatial_forward_step(i, x_ref, dy_ref, ln_ref, wqkv_ref, wout_ref, wup_ref, wdown_ref, bias_ref, perm_ref,
+                         h_ref, o_ref, qkv_ref, p_ref, act_ref, s_ref, send_mid, send_dy, mid_ref, dyx_ref):
+    me = lax.axis_index('sp')
+    slot = lax.rem(i, send_mid.slots)
+    send_mid.free_slot(i)
+    send_dy.free_slot(i)
     for v in range(NV):
         moved = dot_nn(perm_ref[...], dy_ref[pl.ds(v * ROWS, ROWS), :]).astype(BF16)
         for d in range(N_DEV):
-            dyp_ref[d, v] = moved[d * 32:(d + 1) * 32]
+            send_dy.stage[slot, d, v] = moved[d * 32:(d + 1) * 32]
     gain1, shift1, gain2, shift2 = gains(ln_ref)
     normed, _ = norm_stats(x_ref[...].astype(F32))
     a_in = (normed * gain1 + shift1).astype(BF16)
@@ -251,16 +259,15 @@
     for c in range(CHUNKS):
         act_ref[:, cut(c)] = gelu_value(dot_nn(m_in, wup_ref[:, cut(c)])).astype(BF16)
     out = (h_ref[...].astype(F32) + dot_nn(act_ref[...], wdown_ref[...])).astype(BF16)
-    exchange.free_slot(step)
     for v in range(NV):
         moved = dot_nn(perm_ref[...], out[v * ROWS:(v + 1) * ROWS]).astype(BF16)
         for d in range(N_DEV):
-            stage_ref[step % 2, d, v] = moved[d * 32:(d + 1) * 32]
-    exchange.start(step)
-
-    @pl.when(step == STEPS - 1)
-    def _():
-        exchange.finish(STEPS)
+            send_mid.stage[slot, d, v] = moved[d * 32:(d + 1) * 32]
+    for v in range(NV):
+        dyx_ref[me, i * NV + v] = send_dy.stage[slot, me, v]
+        mid_ref[me, i * NV + v] = send_mid.stage[slot, me, v]
+    send_mid.start(i)
+    send_dy.start(i)
 
 
 def add_blocks(sum_ref, first, product):
@@ -269,12 +276,12 @@
         sum_ref[rows, :] += product[:, c * WIDTH:(c + 1) * WIDTH]
 
 
-def tail_backward(dv_ref, o_ref, m_ref, normed, inv_std, gain2, gp_ref, act_ref, dup_ref, do_ref,
+def tail_backward(dv_ref, o_ref, m_ref, normed, inv_std, gain2, pre_ref, tanh_ref, act_ref, dup_ref, do_ref,
                   wout_ref, wup_ref, wdown_ref, sum_ref):
     add_blocks(sum_ref, ROW_DOWN, dot_tn(dv_ref[...], act_ref[...]))
     for c in range(CHUNKS):
         d_act = dot_nt(dv_ref[...], wdown_ref[cut(c), :]).astype(BF16).astype(F32)
-        dup_ref[:, cut(c)] = (d_act * gp_ref[:, cut(c)]).astype(BF16)
+        dup_ref[:, cut(c)] = (d_act * gelu_slope(pre_ref[:, cut(c)], tanh_ref[:, cut(c)])).astype(BF16)
     add_blocks(sum_ref, ROW_UP, dot_tn(m_ref[...], dup_ref[...]))
     d_m = dot_nt(dup_ref[...], wup_ref[...]).astype(BF16).astype(F32)
     d_h, g_gain, g_shift = norm_back(d_m, normed, inv_std, gain2)
@@ -292,13 +299,15 @@
     return (d_in + dh_ref[...].astype(F32)).astype(BF16), g_gain, g_shift
 
 
-def up_forward(h32, gain2, shift2, m_ref, wup_ref, act_ref, gp_ref):
+def up_forward(h32, gain2, shift2, m_ref, wup_ref, act_ref, pre_ref, tanh_ref):
     normed, inv_std = norm_stats(h32)
     m_ref[...] = (normed * gain2 + shift2).astype(BF16)
     for c in range(CHUNKS):
-        act, slope = gelu_parts(dot_nn(m_ref[...], wup_ref[:, cut(c)]))
-        act_ref[:, cut(c)] = act.astype(BF16)
-        gp_ref[:, cut(c)] = slope
+        x = dot_nn(m_ref[...], wup_ref[:, cut(c)])
+        t = jnp.tanh(x * (GELU_C + GELU_C3 * (x * x)))
+        act_ref[:, cut(c)] = (x * (0.5 + 0.5 * t)).astype(BF16)
+        pre_ref[:, cut(c)] = x
+        tanh_ref[:, cut(c)] = t
     return normed, inv_std
 
 
@@ -307,34 +316,19 @@
         ref[first + r:first + r + 1, :] += g
 
 
-def temporal_kernel(mid_ref, dyp_ref, ln_ref, wqkv_ref, wout_ref, wup_ref, wdown_ref, bias_ref,
-                    back_ref, sum_ref, u_ref, dv_ref, a_ref, qkv_ref, p_ref, o_ref, m_ref, act_ref,
-                    dup_ref, do_ref, dqkv_ref, dp_ref, gp_ref, s_ref, dy_ref, y_stage, dm_stage, *sems):
-    step = pl.program_id(0)
-    me = lax.axis_index('sp')
-    send_y = Exchange(y_stage, lambda src, i: back_ref.at[src, 0, videos_of(i)], sems[0:3])
-    send_dm = Exchange(dm_stage, lambda src, i: back_ref.at[src, 1, videos_of(i)], sems[3:6])
-    dy_send, dy_recv, dy_own = sems[6:]
-
-    def dy_copy(i, d):
-        return remote(dyp_ref.at[peer(d), videos_of(i)], dy_ref.at[me, videos_of(i)], dy_send.at[i, d], dy_recv.at[i, d],
-                      peer(d))
-
-    dy_local = pltpu.make_async_copy(dyp_ref.at[me], dy_ref.at[me], dy_own)
-
-    @pl.when(step == 0)
-    def _():
-        enter()
-        dy_local.start()
-        for i in range(STEPS):
-            for d in range(1, N_DEV):
-                dy_copy(i, d).start()
-        sum_ref[...] = jnp.zeros_like(sum_ref)
-
+def temporal_step(i, ln_ref, wqkv_ref, wout_ref, wup_ref, wdown_ref, bias_ref, sum_ref, mid_ref, dyx_ref,
+                  send_mid, send_dy, send_y, send_dm, u_ref, dv_ref, a_ref, qkv_ref, p_ref, o_ref, m_ref, act_ref,
+                  dup_ref, do_ref, dqkv_ref, dp_ref, pre_ref, tanh_ref, s_ref):
+    send_mid.wait_received(i)
+    send_dy.wait_received(i)
+    send_y.free_slot(i)
+    send_dm.free_slot(i)
     gain1, shift1, gain2, shift2 = gains(ln_ref)
     places = [(v, g, s) for v in range(NV) for g in range(2) for s in range(N_DEV)]
     for v, g, s in places:
-        u_ref[pl.ds(v * ROWS + g * GROUP + s * 16, 16), :] = mid_ref[s, v, pl.ds(g * 16, 16), :]
+        dst = pl.ds(v * ROWS + g * GROUP + s * 16, 16)
+        u_ref[dst, :] = mid_ref[s, i * NV + v, pl.ds(g * 16, 16), :]
+        dv_ref[dst, :] = dyx_ref[s, i * NV + v, pl.ds(g * 16, 16), :]
     normed1, _ = norm_stats(u_ref[...].astype(F32))
     a_ref[...] = (normed1 * gain1 + shift1).astype(BF16)
     for c in range(3):
@@ -343,39 +337,59 @@
     attend(qkv_ref, bias_ref, p_ref, o_ref, s_ref)
     h = (u_ref[...].astype(F32) + dot_nn(o_ref[...], wout_ref[...])).astype(BF16)
     h32 = h.astype(F32)
-    normed, inv_std = up_forward(h32, gain2, shift2, m_ref, wup_ref, act_ref, gp_ref)
+    normed, inv_std = up_forward(h32, gain2, shift2, m_ref, wup_ref, act_ref, pre_ref, tanh_ref)
     out = (h32 + dot_nn(act_ref[...], wdown_ref[...])).astype(BF16)
-    send_y.free_slot(step)
     for v, g, s in places:
         src = v * ROWS + g * GROUP + s * 16
-        y_stage[step % 2, s, v, pl.ds(g * 16, 16), :] = out[src:src + 16]
-
-    @pl.when(step == 0)
-    def _():
-        dy_local.wait()
-
-    for d in range(1, N_DEV):
-        remote(dyp_ref.at[0, videos_of(step)], dy_ref.at[peer(N_DEV - d), videos_of(step)], dy_send.at[step, d],
-               dy_recv.at[step, d], peer(d)).wait_recv()
-    for v, g, s in places:
-        dv_ref[pl.ds(v * ROWS + g * GROUP + s * 16, 16), :] = dy_ref[s, step * NV + v, pl.ds(g * 16, 16), :]
-    send_y.start(step)
-    g_gain2, g_shift2 = tail_backward(dv_ref, o_ref, m_ref, normed, inv_std, gain2, gp_ref, act_ref, dup_ref, do_ref,
+        send_y.stage[lax.rem(i, send_y.slots), s, v, pl.ds(g * 16, 16), :] = out[src:src + 16]
+    send_y.start(i)
+    g_gain2, g_shift2 = tail_backward(dv_ref, o_ref, m_ref, normed, inv_std, gain2, pre_ref, tanh_ref, act_ref, dup_ref, do_ref,
                                       wout_ref, wup_ref, wdown_ref, sum_ref)
     attend_back(qkv_ref, p_ref, do_ref, dqkv_ref, dp_ref)
     d_in, g_gain1, g_shift1 = qkv_backward(u_ref[...].astype(F32), a_ref, dv_ref, dqkv_ref, gain1, wqkv_ref, sum_ref)
     add_ln_sums(sum_ref, SUM_ROWS, (g_gain1, g_shift1, g_gain2, g_shift2))
-    send_dm.free_slot(step)
     for v, g, s in places:
         src = v * ROWS + g * GROUP + s * 16
-        dm_stage[step % 2, s, v, pl.ds(g * 16, 16), :] = d_in[src:src + 16]
-    send_dm.start(step)
-
-    @pl.when(step == STEPS - 1)
-    def _():
-        for i in range(STEPS):
-            for d in range(1, N_DEV):
-                dy_copy(i, d).wait_send()
+        send_dm.stage[lax.rem(i, send_dm.slots), s, v, pl.ds(g * 16, 16), :] = d_in[src:src + 16]
+    send_dm.start(i)
+
+
+def forward_kernel(x_ref, dy_ref, *refs):
+    refs = iter(refs)
+
+    def take(n):
+        return list(itertools.islice(refs, n))
+
+    spatial_w, temporal_w, (bias_s_ref, bias_t_ref, perm_ref) = take(5), take(5), take(3)
+    back_ref, sum_ref, h_ref, o_ref, qkv_ref, p_ref = take(6)
+    mine, (pre_ref, tanh_ref, s_ref), (mid_ref, dyx_ref) = take(12), take(3), take(2)
+    mid_stage, dy_stage, y_stage, dm_stage = take(4)
+    mid_sems, dy_sems, y_sems, dm_sems = [take(3) for _ in BLOCKS[:4]]
+    step = pl.program_id(0)
+    send_mid = Exchange(mid_stage, lambda src, i: mid_ref.at[src, videos_of(i)], mid_sems, local=False)
+    send_dy = Exchange(dy_stage, lambda src, i: dyx_ref.at[src, videos_of(i)], dy_sems, local=False)
+    send_y = Exchange(y_stage, lambda src, i: back_ref.at[src, 0, videos_of(i)], y_sems)
+    send_dm = Exchange(dm_stage, lambda src, i: back_ref.at[src, 1, videos_of(i)], dm_sems)
+
+    @pl.when(step == 0)
+    def _():
+        enter()
+        sum_ref[...] = jnp.zeros_like(sum_ref)
+
+    @pl.when(step < STEPS)
+    def _():
+        spatial_forward_step(step, x_ref, dy_ref, *spatial_w, bias_s_ref, perm_ref, h_ref, o_ref, qkv_ref, p_ref,
+                             mine[7], s_ref, send_mid, send_dy, mid_ref, dyx_ref)
+
+    @pl.when(step >= STEPS)
+    def _():
+        temporal_step(step - STEPS, *temporal_w, bias_t_ref, sum_ref, mid_ref, dyx_ref,
+                      send_mid, send_dy, send_y, send_dm, *mine, pre_ref, tanh_ref, s_ref)
+
+    @pl.when(step == 2 * STEPS - 1)
+    def _():
+        send_mid.finish_sends(STEPS)
+        send_dy.finish_sends(STEPS)
         send_y.finish(STEPS)
         send_dm.finish(STEPS)
 
@@ -393,16 +407,21 @@
         self.sum, self.first, self.landing = sum_ref, first_ref, landing_ref
         self.sems, self.credits, self.block, self.out_sems = sems, credits, block, out_sems
 
+    def owned(self):
+        _, y, x, c, _, _, _ = position()
+        half = c * 8
+        return half, half + x * 2, half + 4 + y * 2
+
     def moves(self, phase):
         _, y, x, c, partner, xn, yn = position()
-        own0, own1 = c * 8 + x * 2, c * 8 + 4 + y * 2
+        half, own0, own1 = self.owned()
         return (
-            [((1 - c) * 8, 8, 0, partner)],
-            [(c * 8 + (1 - x) * 2, 2, 8, xn), (c * 8 + 4 + (1 - y) * 2, 2, 10, yn)],
+            [(8 - half, 8, 0, partner)],
+            [(own0 + 2 - x * 4, 2, 8, xn), (own1 + 2 - y * 4, 2, 10, yn)],
             [(own0 + 1 - y, 1, 12, yn), (own1 + 1 - x, 1, 13, xn)],
             [(own0 + y, 1, None, yn), (own1 + x, 1, None, xn)],
             [(own0, 2, None, xn), (own1, 2, None, yn)],
-            [(c * 8, 8, None, partner)],
+            [(half, 8, None, partner)],
         )[phase]
 
     def copies(self, phase, k):
@@ -426,20 +445,21 @@
             if phase < 3:
                 pl.semaphore_signal(self.credits.at[phase, k, j], inc=1, device_id={'sp': self.moves(phase)[j][3]},
                                     device_id_type=pl.DeviceIdType.MESH)
-        _, y, x, c, _, _, _ = position()
-        own0, own1 = c * 8 + x * 2, c * 8 + 4 + y * 2
-        adds = ([(c * 8, 8, 0)], [(own0, 2, 8), (own1, 2, 10)], [(own0 + y, 1, 12), (own1 + x, 1, 13)], (), (), ())
+        _, y, x, _, _, _, _ = position()
+        half, own0, own1 = self.owned()
+        adds = ([(half, 8, 0)], [(own0, 2, 8), (own1, 2, 10)], [(own0 + y, 1, 12), (own1 + x, 1, 13)], (), (), ())
         for idx, n, place in adds[phase]:
             def body(i, carry):
                 rows = pl.ds(pl.multiple_of((k * SLOTS + place + i) * BLOCK, 8), BLOCK)
                 self.sum[span(k, idx + i, 1), :] += self.landing[rows, :]
                 return carry
             lax.fori_loop(0, n, body, 0)
-        if phase == 5:
-            for r in self.pieces(k):
-                if r >= 8:
-                    rows = pl.ds(r * WIDTH, WIDTH)
-                    self.sum[rows, :] = self.sum[rows, :].T
+
+    def turn_down(self, k):
+        for r in self.pieces(k):
+            if r >= 8:
+                rows = pl.ds(r * WIDTH, WIDTH)
+                self.sum[rows, :] = self.sum[rows, :].T
 
     def pieces(self, k):
         return range(k * LAP_ROWS // WIDTH, (k + 1) * LAP_ROWS // WIDTH)
@@ -465,7 +485,7 @@
     def start(lap, phase):
         link = 0 if phase in (0, 5) else 1
         free[link] = max(free[link], now) + lasts[phase]
-        running[lap] = (phase, free[link] + 2.5)
+        running[lap] = (phase, free[link] + 1.5)
 
     def turn(due):
         turns = []
@@ -479,7 +499,8 @@
                 start(lap, phase + 1)
         return turns
 
-    begin = {0: [('t', k) for k in (1, 2, 3, 0)], STEPS: [('s', k) for k in (1, 2, 3)]}
+    tail_laps = range(1, LAPS)
+    begin = {0: [('t', k) for k in (*tail_laps, 0)], STEPS: [('s', k) for k in tail_laps]}
     for step in range(2 * STEPS):
         turns = turn(now)
         fresh = begin.get(step, [])
@@ -508,8 +529,8 @@
 def spatial_backward_kernel(*refs):
     (back_ref, x_ref, h_ref, o_ref, qkv_ref, p_ref,
      ln_ref, wqkv_ref, wout_ref, wup_ref, wdown_ref, perm_ref, gt_ref) = refs[:13]
-    (y_ref, dx_ref, gqkv_ref, gout_ref, gup_ref, gdown_ref, gln_ref,
-     dv_ref, a_ref, m_ref, act_ref, dup_ref, do_ref, dqkv_ref, dp_ref, gp_ref, dh_all_ref, do_all_ref,
+    (dx_ref, gqkv_ref, gout_ref, gup_ref, gdown_ref, gln_ref,
+     dv_ref, a_ref, m_ref, act_ref, dup_ref, do_ref, dqkv_ref, dp_ref, pre_ref, tanh_ref, dh_all_ref, do_all_ref,
      sum_ref, t_ref, land_s_ref, land_t_ref, ln_s_ref, ln_all_ref, sems_s, sems_t, credits_s, credits_t,
      sems_out_s, sems_out_t, sems_ln, sems_in) = refs[13:]
     step = pl.program_id(0)
@@ -520,7 +541,7 @@
             's': Reduce(sum_ref, sum_ref, land_s_ref, sems_s, credits_s, 0, sems_out_s)}
     outs = (gqkv_ref, gout_ref, gup_ref, gdown_ref)
     plan = reduce_plan()
-    written = []
+    ready, turned = [], []
 
     def advance(turns, fresh):
         for (which, k), phase in turns:
@@ -530,11 +551,17 @@
         for (which, k), phase in turns:
             if phase < 5:
                 sums[which].start(phase + 1, k)
-        while written:
-            which, k = written.pop()
+        ready.extend(lap for lap, phase in turns if phase == 5)
+
+    def write_totals():
+        while turned:
+            which, k = turned.pop()
             for r in sums[which].pieces(k):
                 sums[which].out_copy(r, outs).start()
-        written.extend(lap for lap, phase in turns if phase == 5)
+        if ready:
+            which, k = ready.pop(0)
+            sums[which].turn_down(k)
+            turned.append((which, k))
 
     @pl.when(step == 0)
     def _():
@@ -550,7 +577,7 @@
         load_ln.wait()
 
     for at in range(2 * STEPS):
-        if any(plan[at]) or written:
+        if any(plan[at]):
             @pl.when(step == at)
             def _(at=at):
                 advance(*plan[at])
@@ -562,10 +589,9 @@
         mine = pl.ds(pl.multiple_of(step * STEP_ROWS, STEP_ROWS), STEP_ROWS)
         for v in range(NV):
             rows = pl.ds(v * ROWS, ROWS)
-            dv_ref[rows, :] = dot_tn(perm_ref[...], back_ref[:, 1, v].reshape(ROWS, WIDTH)).astype(BF16)
-            y_ref[rows, :] = dot_tn(perm_ref[...], back_ref[:, 0, v].reshape(ROWS, WIDTH)).astype(BF16)
-        normed, inv_std = up_forward(h_ref[...].astype(F32), gain2, shift2, m_ref, wup_ref, act_ref, gp_ref)
-        g_gain2, g_shift2 = tail_backward(dv_ref, o_ref, m_ref, normed, inv_std, gain2, gp_ref, act_ref, dup_ref, do_ref,
+            dv_ref[rows, :] = dot_tn(perm_ref[...], back_ref[:, v].reshape(ROWS, WIDTH)).astype(BF16)
+        normed, inv_std = up_forward(h_ref[...].astype(F32), gain2, shift2, m_ref, wup_ref, act_ref, pre_ref, tanh_ref)
+        g_gain2, g_shift2 = tail_backward(dv_ref, o_ref, m_ref, normed, inv_std, gain2, pre_ref, tanh_ref, act_ref, dup_ref, do_ref,
                                           wout_ref, wup_ref, wdown_ref, sum_ref)
         dh_all_ref[mine, :] = dv_ref[...]
         do_all_ref[mine, :] = do_ref[...]
@@ -588,6 +614,7 @@
         ln_all_ref[me, pl.ds(8, 8), :] = ln_s_ref[...]
         for n, (turns, fresh) in enumerate(plan[2 * STEPS:]):
             advance(turns, fresh)
+            write_totals()
             if n == 0:
                 for copy in ln_copies(ln_all_ref, sems_ln):
                     copy.start()
@@ -599,12 +626,22 @@
                     total += ln_all_ref[d]
                 gln_ref[0] = total[8:12]
                 gln_ref[1] = total[0:4]
-        advance((), ())
+        while ready or turned:
+            write_totals()
         for which in 'ts':
             for r in range(12):
                 sums[which].out_copy(r, outs).wait()
 
 
+def finish_kernel(back_ref, perm_ref, *refs):
+    n = len(refs) // 2
+    ins, (y_ref, *outs) = refs[:n], refs[n:]
+    for v in range(NV):
+        y_ref[pl.ds(v * ROWS, ROWS), :] = dot_tn(perm_ref[...], back_ref[:, v].reshape(ROWS, WIDTH)).astype(BF16)
+    for in_ref, out_ref in zip(ins, outs):
+        out_ref[...] = in_ref[...]
+
+
 def full(shape):
     return pl.BlockSpec(shape, lambda i: (0,) * len(shape), pipeline_mode=pl.Buffered(1))
 
@@ -618,10 +655,6 @@
     return pl.BlockSpec((STEP_ROWS, width), lambda i: (i, 0))
 
 
-def swap_spec():
-    return pl.BlockSpec((N_DEV, NV, 32, WIDTH), lambda i: (0, i, 0, 0))
-
-
 ANY = pl.BlockSpec(memory_space=pl.ANY)
 
 
@@ -643,6 +676,7 @@
 
 
 TOKENS = VIDEOS * ROWS
+GRADS = [(2, WIDTH, QKV), (2, WIDTH, WIDTH), (2, WIDTH, HIDDEN), (2, HIDDEN, WIDTH)]
 PROBS = 6 * GROUP
 SWAP = (N_DEV, VIDEOS, 32, WIDTH)
 ROW_QKV, ROW_OUT, ROW_UP, ROW_DOWN = 0, 3 * WIDTH, 4 * WIDTH, 8 * WIDTH
@@ -653,30 +687,23 @@
 SLOTS = 14
 
 
-def spatial_forward_call(x, dy, weights, bias, perm):
+def forward_call(x, dy, weights, bias_s, bias_t, perm):
+    def early(width):
+        return pl.BlockSpec((STEP_ROWS, width), lambda i: (jnp.minimum(i, STEPS - 1), 0))
+
     widths = (WIDTH, WIDTH, QKV, PROBS)
+    stage = (N_DEV, NV, 32, WIDTH)
     return pl.pallas_call(
-        spatial_forward_kernel, grid=(STEPS,), name="spatial_fwd",
-        in_specs=[rows_spec(WIDTH)] * 2 + weight_specs(0) + [full((GROUP, 2 * GROUP)), full((ROWS, ROWS))],
-        out_specs=[ANY, swap_spec()] + [rows_spec(w) for w in widths],
-        out_shape=[sds(SWAP, BF16)] * 2 + [sds((TOKENS, w), BF16) for w in widths],
-        scratch_shapes=[vm(HIDDEN), vm(PROBS, F32), pltpu.VMEM((2, N_DEV, NV, 32, WIDTH), BF16)] + EXCHANGE_SEMS,
-        compiler_params=params(1), cost_estimate=cost(50, 40),
-    )(x, dy, *weights, bias, perm)
-
-
-def temporal_call(mid, dyp, weights, bias):
-    return pl.pallas_call(
-        temporal_kernel, grid=(STEPS,), name="temporal",
-        in_specs=[swap_spec(), ANY] + weight_specs(1) + [full((GROUP, 2 * GROUP))],
-        out_specs=[ANY, full((SUM_ROWS + 8, WIDTH))],
-        out_shape=[sds((N_DEV, 2) + SWAP[1:], BF16), sds((SUM_ROWS + 8, WIDTH), F32)],
+        forward_kernel, grid=(2 * STEPS,), name="forward",
+        in_specs=[early(WIDTH)] * 2 + weight_specs(0) + weight_specs(1) + [full((GROUP, 2 * GROUP))] * 2 + [full((ROWS, ROWS))],
+        out_specs=[ANY, full((SUM_ROWS + 8, WIDTH))] + [early(w) for w in widths],
+        out_shape=[sds((N_DEV, 2) + SWAP[1:], BF16), sds((SUM_ROWS + 8, WIDTH), F32)] + [sds((TOKENS, w), BF16) for w in widths],
         scratch_shapes=[vm(w) for w in (WIDTH, WIDTH, WIDTH, QKV, PROBS, WIDTH, WIDTH, HIDDEN, HIDDEN, WIDTH, QKV, PROBS)]
-        + [vm(HIDDEN, F32), vm(PROBS, F32), pltpu.VMEM(SWAP, BF16)]
-        + [pltpu.VMEM((2, N_DEV, NV, 32, WIDTH), BF16)] * 2 + EXCHANGE_SEMS * 2
-        + [pltpu.SemaphoreType.DMA((STEPS, N_DEV))] * 2 + [pltpu.SemaphoreType.DMA],
-        compiler_params=params(2), cost_estimate=cost(110, 20),
-    )(mid, dyp, *weights, bias)
+        + [vm(HIDDEN, F32)] * 2 + [vm(PROBS, F32)] + [pltpu.VMEM(SWAP, BF16)] * 2
+        + [pltpu.VMEM((6,) + stage, BF16)] * 2 + [pltpu.VMEM((4,) + stage, BF16)] * 2
+        + exchange_sems(6) * 2 + exchange_sems(4) * 2,
+        compiler_params=params(1), cost_estimate=cost(160, 60),
+    )(x, dy, *weights, *weights, bias_s, bias_t, perm)
 
 
 def spatial_backward_call(back, x, saved, weights, perm, sum_t):
@@ -686,14 +713,14 @@
     def late(width):
         return pl.BlockSpec((STEP_ROWS, width), lambda i: (jnp.maximum(i - STEPS, 0), 0))
 
-    grads = [(2, WIDTH, QKV), (2, WIDTH, WIDTH), (2, WIDTH, HIDDEN), (2, HIDDEN, WIDTH)]
+    grads = GRADS
     return pl.pallas_call(
         spatial_backward_kernel, grid=(2 * STEPS,), name="spatial_bwd",
-        in_specs=[pl.BlockSpec((N_DEV, 2, NV, 32, WIDTH), lambda i: (0, 0, jnp.minimum(i, STEPS - 1), 0, 0))]
+        in_specs=[pl.BlockSpec((N_DEV, None, NV, 32, WIDTH), lambda i: (0, 1, jnp.minimum(i, STEPS - 1), 0, 0))]
         + [late(WIDTH), early(WIDTH), early(WIDTH), late(QKV), late(PROBS)] + weight_specs(0) + [full((ROWS, ROWS)), ANY],
-        out_specs=[early(WIDTH), late(WIDTH)] + [ANY] * 4 + [full((2, 4, WIDTH))],
-        out_shape=[sds((TOKENS, WIDTH), BF16)] * 2 + [sds(g, F32) for g in grads] + [sds((2, 4, WIDTH), F32)],
-        scratch_shapes=[vm(w) for w in (WIDTH, WIDTH, WIDTH, HIDDEN, HIDDEN, WIDTH, QKV, PROBS)] + [vm(HIDDEN, F32)]
+        out_specs=[late(WIDTH)] + [ANY] * 4 + [full((2, 4, WIDTH))],
+        out_shape=[sds((TOKENS, WIDTH), BF16)] + [sds(g, F32) for g in grads] + [sds((2, 4, WIDTH), F32)],
+        scratch_shapes=[vm(w) for w in (WIDTH, WIDTH, WIDTH, HIDDEN, HIDDEN, WIDTH, QKV, PROBS)] + [vm(HIDDEN, F32)] * 2
         + [pltpu.VMEM((TOKENS, WIDTH), BF16)] * 2
         + [pltpu.VMEM((SUM_ROWS, WIDTH), F32)] * 2 + [pltpu.VMEM((LAPS * SLOTS * BLOCK, WIDTH), F32)] * 2
         + [pltpu.VMEM((8, WIDTH), F32), pltpu.VMEM((N_DEV, 16, WIDTH), F32)]
@@ -701,6 +728,22 @@
         + [pltpu.SemaphoreType.DMA((12,))] * 2 + [pltpu.SemaphoreType.DMA((2, N_DEV)), pltpu.SemaphoreType.DMA((2,))],
         compiler_params=params(3), cost_estimate=cost(160, 60),
     )(back, x, *saved, *weights, perm, sum_t)
+
+
+def finish_call(back, perm, dx, grads, g_ln):
+    flat = [g.reshape(-1, g.shape[-1]) for g in grads]
+    parts = [pl.BlockSpec((g.shape[0] // STEPS, g.shape[1]), lambda i: (i, 0)) for g in flat]
+    ln_spec = pl.BlockSpec((2, 4, WIDTH), lambda i: (0, 0, 0))
+    y, dx, *flat, g_ln = pl.pallas_call(
+        finish_kernel, grid=(STEPS,), name="finish",
+        in_specs=[pl.BlockSpec((N_DEV, None, NV, 32, WIDTH), lambda i: (0, 0, i, 0, 0)), full((ROWS, ROWS)), rows_spec(WIDTH)]
+        + parts + [ln_spec],
+        out_specs=[rows_spec(WIDTH)] * 2 + parts + [ln_spec],
+        out_shape=[sds((TOKENS, WIDTH), BF16)] * 2 + [sds(g.shape, F32) for g in flat] + [sds((2, 4, WIDTH), F32)],
+        compiler_params=pltpu.CompilerParams(dimension_semantics=("arbitrary",), vmem_limit_bytes=VMEM_LIMIT),
+        cost_estimate=cost(12, 40),
+    )(back, perm, dx, *flat, g_ln)
+    return y, dx, [f.reshape(g.shape) for f, g in zip(flat, grads)], g_ln
 
 
 def constants():
@@ -724,9 +767,9 @@
     x = latents.reshape(TOKENS, WIDTH)
     dy = cotangent.reshape(TOKENS, WIDTH)
 
-    mid, dyp, *saved = spatial_forward_call(x, dy, weights, bias_s, perm)
-    back, sum_t = temporal_call(mid, dyp, weights, bias_t)
-    y, dx, g_qkv, g_out, g_up, g_down, g_ln = spatial_backward_call(back, x, saved, weights, perm, sum_t)
+    back, sum_t, *saved = forward_call(x, dy, weights, bias_s, bias_t, perm)
+    dx, *grads, g_ln = spatial_backward_call(back, x, saved, weights, perm, sum_t)
+    y, dx, (g_qkv, g_out, g_up, g_down), g_ln = finish_call(back, perm, dx, grads, g_ln)
     g_out = g_out.reshape(2, 6, 64, WIDTH)
     shape = latents.shape
     return y.reshape(shape), dx.reshape(shape), g_ln, g_qkv, g_out, g_up, g_down

time: 333 us -> 314 us (0.943)
  local copies, waits for them, and re-layouts: 16.8 us -> 0 us
    unnamed x23 -> x0, local copies, waits for them, and re-layouts: 16.8 us -> none
where the time goes in v5:
time: 314 us
  Pallas kernels  313 us (100%)
    pallas_call x1, Pallas kernels, forward_call(): pl.pallas_call(forward_kernel, grid=(2 * STEPS,), name='forward', in_spec...  157 us
    pallas_call x1, Pallas kernels, spatial_backward_call(): pl.pallas_call(spatial_backward_kernel, grid=(2 * STEPS,), name='spatial_...  140 us
    pallas_call x1, Pallas kernels, finish_call(): pl.pallas_call(finish_kernel, grid=(STEPS,), name='finish', in_specs=[pl....  15.9 us

profile of v5, /device:TPU:0, one launch (start us, length us, event | category | flops | bytes accessed | tf_op | source)
XLA Modules:
  0.0 314.1 jit_solution(13585975576343774361)
XLA Ops:
  0.6 157.5 %forward.1 = (bf16[8,2,16,32,384]{4,3,2,1,0:T(8,128)(2,1)}, f32[4616,384]{1,0:T(8,128)}, bf16[4096,384]{1,0:T(8,128)(2,1)}, bf16[4096,384]{1,0:T(8,128)(2,1)}, b...) custom-call(bf16[4096,384]{1,0:T(8,128)(2,1)} %bitcast.14, bf16[4096,384]{1,0:T(8,128)(2,1)} %bitcast.13, ...), custom_call_target="tpu_custom_call" | custom-call | flops 143999991808 | bytes 62914560 | tf_op jit(solution)/shard_map/forward/pallas_call | solution.py:696
  158.1 139.9 %spatial_bwd.1 = (bf16[4096,384]{1,0:T(8,128)(2,1)}, f32[2,384,1152]{2,1,0:T(8,128)}, f32[2,384,384]{2,1,0:T(8,128)}, f32[2,384,1536]{2,1,0:T(8,128)}, f32[2,1536,384]{2,1,0:T(8,128)}, /*index=5*/f32[2,4,384]{2,1,0:T(4,128)}) custom-call(bf16[8,2,16,32,384]{4,3,2,1,0:T(8,128)(2,1)} %get-tuple-element.26.refs_0_.back_ref, bf16[4096,384]{1,0:T(8,128)(2,1)} %bitcast.15, ...), custom_call_target="tpu_custom_call" | custom-call | flops 143999991808 | bytes 62914560 | tf_op jit(solution)/shard_map/spatial_bwd/pallas_call | solution.py:717
  298.0 15.9 %finish.1 = (bf16[4096,384]{1,0:T(8,128)(2,1)}, bf16[4096,384]{1,0:T(8,128)(2,1)}, f32[768,1152]{1,0:T(8,128)}, f32[768,384]{1,0:T(8,128)}, f32[768,1536]{1,0:T(...) custom-call(bf16[8,2,16,32,384]{4,3,2,1,0:T(8,128)(2,1)} %get-tuple-element.26.refs_0_.back_ref, ...), custom_call_target="tpu_custom_call" | custom-call | flops 10800000000 | bytes 41943040 | tf_op jit(solution)/shard_map/finish/pallas_call | solution.py:737

commit v6 on v5

--- a/solution.py
+++ b/solution.py
@@ -485,7 +485,7 @@
     def start(lap, phase):
         link = 0 if phase in (0, 5) else 1
         free[link] = max(free[link], now) + lasts[phase]
-        running[lap] = (phase, free[link] + 1.5)
+        running[lap] = (phase, free[link] + 1.0)
 
     def turn(due):
         turns = []
@@ -636,8 +636,7 @@
 def finish_kernel(back_ref, perm_ref, *refs):
     n = len(refs) // 2
     ins, (y_ref, *outs) = refs[:n], refs[n:]
-    for v in range(NV):
-        y_ref[pl.ds(v * ROWS, ROWS), :] = dot_tn(perm_ref[...], back_ref[:, v].reshape(ROWS, WIDTH)).astype(BF16)
+    y_ref[...] = dot_tn(perm_ref[...], back_ref[...].reshape(ROWS, WIDTH)).astype(BF16)
     for in_ref, out_ref in zip(ins, outs):
         out_ref[...] = in_ref[...]
 
@@ -732,13 +731,14 @@
 
 def finish_call(back, perm, dx, grads, g_ln):
     flat = [g.reshape(-1, g.shape[-1]) for g in grads]
-    parts = [pl.BlockSpec((g.shape[0] // STEPS, g.shape[1]), lambda i: (i, 0)) for g in flat]
+    parts = [pl.BlockSpec((g.shape[0] // VIDEOS, g.shape[1]), lambda i: (i, 0)) for g in flat]
+    video = pl.BlockSpec((ROWS, WIDTH), lambda i: (i, 0))
     ln_spec = pl.BlockSpec((2, 4, WIDTH), lambda i: (0, 0, 0))
     y, dx, *flat, g_ln = pl.pallas_call(
-        finish_kernel, grid=(STEPS,), name="finish",
-        in_specs=[pl.BlockSpec((N_DEV, None, NV, 32, WIDTH), lambda i: (0, 0, i, 0, 0)), full((ROWS, ROWS)), rows_spec(WIDTH)]
+        finish_kernel, grid=(VIDEOS,), name="finish",
+        in_specs=[pl.BlockSpec((N_DEV, None, None, 32, WIDTH), lambda i: (0, 0, i, 0, 0)), full((ROWS, ROWS)), video]
         + parts + [ln_spec],
-        out_specs=[rows_spec(WIDTH)] * 2 + parts + [ln_spec],
+        out_specs=[video] * 2 + parts + [ln_spec],
         out_shape=[sds((TOKENS, WIDTH), BF16)] * 2 + [sds(g.shape, F32) for g in flat] + [sds((2, 4, WIDTH), F32)],
         compiler_params=pltpu.CompilerParams(dimension_semantics=("arbitrary",), vmem_limit_bytes=VMEM_LIMIT),
         cost_estimate=cost(12, 40),

time: 314 us -> 319 us (1.016)
  Pallas kernels: 313 us -> 318 us
    pallas_call x1, Pallas kernels: 15.9 us -> 19.8 us  [finish_call(): pl.pallas_call(finish_kernel, grid=(VIDEOS,), name='finish', in_specs=[pl...]
where the time goes in v6:
time: 319 us; the launch traced here: 318 us
  Pallas kernels  318 us (100%)
    pallas_call x1, Pallas kernels, forward_call(): pl.pallas_call(forward_kernel, grid=(2 * STEPS,), name='forward', in_spec...  157 us
    pallas_call x1, Pallas kernels, spatial_backward_call(): pl.pallas_call(spatial_backward_kernel, grid=(2 * STEPS,), name='spatial_...  140 us
    pallas_call x1, Pallas kernels, finish_call(): pl.pallas_call(finish_kernel, grid=(VIDEOS,), name='finish', in_specs=[pl...  19.8 us

profile of v6, /device:TPU:0, one launch (start us, length us, event | category | flops | bytes accessed | tf_op | source)
XLA Modules:
  0.0 318.4 jit_solution(5002911222891126396)
XLA Ops:
  0.6 157.5 %forward.1 = (bf16[8,2,16,32,384]{4,3,2,1,0:T(8,128)(2,1)}, f32[4616,384]{1,0:T(8,128)}, bf16[4096,384]{1,0:T(8,128)(2,1)}, bf16[4096,384]{1,0:T(8,128)(2,1)}, b...) custom-call(bf16[4096,384]{1,0:T(8,128)(2,1)} %bitcast.14, bf16[4096,384]{1,0:T(8,128)(2,1)} %bitcast.13, ...), custom_call_target="tpu_custom_call" | custom-call | flops 143999991808 | bytes 62914560 | tf_op jit(solution)/shard_map/forward/pallas_call | solution.py:695
  158.1 140.2 %spatial_bwd.1 = (bf16[4096,384]{1,0:T(8,128)(2,1)}, f32[2,384,1152]{2,1,0:T(8,128)}, f32[2,384,384]{2,1,0:T(8,128)}, f32[2,384,1536]{2,1,0:T(8,128)}, f32[2,1536,384]{2,1,0:T(8,128)}, /*index=5*/f32[2,4,384]{2,1,0:T(4,128)}) custom-call(bf16[8,2,16,32,384]{4,3,2,1,0:T(8,128)(2,1)} %get-tuple-element.26.refs_0_.back_ref, bf16[4096,384]{1,0:T(8,128)(2,1)} %bitcast.15, ...), custom_call_target="tpu_custom_call" | custom-call | flops 143999991808 | bytes 62914560 | tf_op jit(solution)/shard_map/spatial_bwd/pallas_call | solution.py:716
  298.4 19.8 %finish.1 = (bf16[4096,384]{1,0:T(8,128)(2,1)}, bf16[4096,384]{1,0:T(8,128)(2,1)}, f32[768,1152]{1,0:T(8,128)}, f32[768,384]{1,0:T(8,128)}, f32[768,1536]{1,0:T(...) custom-call(bf16[8,2,16,32,384]{4,3,2,1,0:T(8,128)(2,1)} %get-tuple-element.26.refs_0_.back_ref, ...), custom_call_target="tpu_custom_call" | custom-call | flops 10800000000 | bytes 41943040 | tf_op jit(solution)/shard_map/finish/pallas_call | solution.py:737
